TPU v7x, 32 devices: a whole 2x2x4 slice. The times are simulated.
32 devices in a mesh: rows: 8 (over z, x), cols: 4 (over y, core).
Axes of the slice: x: 2, y: 2, z: 4, core: 2. Of those that a mesh axis runs over, the one named last changes fastest.
Arguments:
- tokens: bfloat16 [36864, 1280], P(('rows', 'cols')), may hold values from -6 to 6
- cotangent: bfloat16 [36864, 1280], P(('rows', 'cols')), may hold values from -6 to 6
- clip_lengths: int32 [24], P('rows'), may hold values from 384 to 1536, as said below
- clip_sets: int32 [24], P('rows'), may hold values from 0 to 7
- clip_scales: float32 [24], P('rows'), may hold values from 0.5 to 2
- norm1_gain: float32 [1280], replicated, may hold values from 0.5 to 1.5
- norm1_shift: float32 [1280], replicated, may hold values from -3 to 3
- w_query: bfloat16 [1280, 1280], P('rows', 'cols'), may hold values from -0.15625 to 0.15625
- query_bias: float32 [1280], P('cols'), may hold values from -3 to 3
- w_key: bfloat16 [1280, 1280], P('rows', 'cols'), may hold values from -0.15625 to 0.15625
- w_value: bfloat16 [1280, 1280], P('rows', 'cols'), may hold values from -0.15625 to 0.15625
- value_bias: float32 [1280], P('cols'), may hold values from -3 to 3
- w_out: bfloat16 [1280, 1280], P('cols', 'rows'), may hold values from -1.25 to 1.25
- out_bias: float32 [1280], replicated, may hold values from -3 to 3
- norm2_gain: float32 [1280], replicated, may hold values from 0.5 to 1.5
- norm2_shift: float32 [1280], replicated, may hold values from -3 to 3
- w_fc1: bfloat16 [1280, 5120], P('rows', 'cols'), may hold values from -0.15625 to 0.15625
- fc1_bias: float32 [5120], P('cols'), may hold values from -3 to 3
- w_fc2: bfloat16 [5120, 1280], P('cols', 'rows'), may hold values from -0.078125 to 0.078125
- fc2_bias: float32 [1280], replicated, may hold values from -3 to 3
- query_down: bfloat16 [8, 1280, 16], P(None, 'rows'), may hold values from -0.15625 to 0.15625
- query_up: bfloat16 [8, 16, 1280], P(None, 'rows', 'cols'), may hold values from -0.5 to 0.5
- key_down: bfloat16 [8, 1280, 16], P(None, 'rows'), may hold values from -0.15625 to 0.15625
- key_up: bfloat16 [8, 16, 1280], P(None, 'rows', 'cols'), may hold values from -0.5 to 0.5
- value_down: bfloat16 [8, 1280, 16], P(None, 'rows'), may hold values from -0.15625 to 0.15625
- value_up: bfloat16 [8, 16, 1280], P(None, 'rows', 'cols'), may hold values from -0.5 to 0.5
- out_down: bfloat16 [8, 1280, 16], P(None, 'cols', 'rows'), may hold values from -1.25 to 1.25
- out_up: bfloat16 [8, 16, 1280], P(None, None, 'rows'), may hold values from -0.5 to 0.5
- fc1_down: bfloat16 [8, 1280, 16], P(None, 'rows'), may hold values from -0.15625 to 0.15625
- fc1_up: bfloat16 [8, 16, 5120], P(None, 'rows', 'cols'), may hold values from -0.5 to 0.5
- fc2_down: bfloat16 [8, 5120, 16], P(None, 'cols', 'rows'), may hold values from -0.078125 to 0.078125
- fc2_up: bfloat16 [8, 16, 1280], P(None, None, 'rows'), may hold values from -0.5 to 0.5
Outputs:
- output: bfloat16 [36864, 1280], P(('rows', 'cols'))
- grad_tokens: bfloat16 [36864, 1280], P(('rows', 'cols'))
- grad_query_down: float32 [8, 1280, 16], P(None, 'rows')
- grad_query_up: float32 [8, 16, 1280], P(None, 'rows', 'cols')
- grad_key_down: float32 [8, 1280, 16], P(None, 'rows')
- grad_key_up: float32 [8, 16, 1280], P(None, 'rows', 'cols')
- grad_value_down: float32 [8, 1280, 16], P(None, 'rows')
- grad_value_up: float32 [8, 16, 1280], P(None, 'rows', 'cols')
- grad_out_down: float32 [8, 1280, 16], P(None, 'cols', 'rows')
- grad_out_up: float32 [8, 16, 1280], P(None, None, 'rows')
- grad_fc1_down: float32 [8, 1280, 16], P(None, 'rows')
- grad_fc1_up: float32 [8, 16, 5120], P(None, 'rows', 'cols')
- grad_fc2_down: float32 [8, 5120, 16], P(None, 'cols', 'rows')
- grad_fc2_up: float32 [8, 16, 1280], P(None, None, 'rows')
Inputs may be any that keep to these rules, and one draw needn't show every extreme that they name: `clip_lengths`: every clip has at least 384 real tokens; clip 0 fills all 1536 slots and clip 1 has exactly 384.
All inputs are finite; a program needn't handle non-finite values.
Results may differ from a plain program's by a relative error of at most 0.02.
Values may be sent and summed in bfloat16 or wider, within the bound.
A program may use at most 448 MiB of HBM per device.

v0:
```python
from functools import partial
import math

import jax
import jax.numpy as jnp
from jax import lax
from jax.sharding import PartitionSpec as P

D = 1280
SETS = 8
HEAD_DIM = 80


HIGHEST = lax.Precision.HIGHEST
EPSILON = 1e-05
MASKED = -1000000000.0


def gather_adapter_sets(adapter_set_lookup, selected_adapter):
    return jnp.take(adapter_set_lookup, selected_adapter, axis=0)


def split_pair(values_in):
    upper_part = values_in.astype(jnp.bfloat16)
    lower_part = (values_in - upper_part.astype(jnp.float32)).astype(jnp.bfloat16)
    return (upper_part, lower_part)


def paired_contraction(form, wide_part, narrow_side):
    upper_part, lower_part = split_pair(wide_part)
    first_term = jnp.einsum(form, upper_part, narrow_side, preferred_element_type=jnp.float32)
    return first_term + jnp.einsum(
        form, lower_part, narrow_side, preferred_element_type=jnp.float32
    )


def rank_down(hidden_state, adapter_set_lookup, selected_adapter):
    return jnp.einsum(
        "jdy,jyf->jdf",
        hidden_state,
        gather_adapter_sets(adapter_set_lookup, selected_adapter),
        preferred_element_type=jnp.float32,
    )


def rank_up(low_rank_piece, adapter_set_lookup, selected_adapter, adapter_factor_list):
    return (
        paired_contraction(
            "htw,hws->hts",
            low_rank_piece,
            gather_adapter_sets(adapter_set_lookup, selected_adapter),
        )
        * adapter_factor_list[:, None, None]
    )


def rank_grad(hidden_gradient, adapter_set_lookup, selected_adapter, adapter_factor_list):
    selected_rows = gather_adapter_sets(adapter_set_lookup, selected_adapter)
    return (
        jnp.einsum(
            "yow,yqw->yoq", hidden_gradient, selected_rows, preferred_element_type=jnp.float32
        )
        * adapter_factor_list[:, None, None]
    )


def rank_back(low_rank_gradient, adapter_set_lookup, selected_adapter):
    return paired_contraction(
        "tsj,tvj->tsv", low_rank_gradient, gather_adapter_sets(adapter_set_lookup, selected_adapter)
    )


def up_gradient(low_rank_piece, widened_gradient, adapter_factor_list):
    return paired_contraction(
        "osi,osj->oij", low_rank_piece * adapter_factor_list[:, None, None], widened_gradient
    )


def down_gradient(widened_hidden, low_rank_gradient):
    return paired_contraction("nxs,nxq->nqs", low_rank_gradient, widened_hidden)


def per_set(per_clip, selected_adapter):
    onehot = (selected_adapter[:, None] == jnp.arange(SETS, dtype=jnp.int32)[None, :]).astype(
        jnp.float32
    )
    return jnp.tensordot(onehot, per_clip, axes=((0,), (0,)), precision=HIGHEST)


def dot_trans(left_side, right_side):
    return lax.dot_general(
        left_side,
        right_side,
        (((left_side.ndim - 1,), (1,)), ((), ())),
        preferred_element_type=jnp.float32,
    )


def body(
    tokens,
    cotangent,
    clip_lengths,
    clip_sets,
    clip_scales,
    norm1_gain,
    norm1_shift,
    w_query,
    query_bias,
    w_key,
    w_value,
    value_bias,
    w_out,
    out_bias,
    norm2_gain,
    norm2_shift,
    w_fc1,
    fc1_bias,
    w_fc2,
    fc2_bias,
    query_down,
    query_up,
    key_down,
    key_up,
    value_down,
    value_up,
    out_down,
    out_up,
    fc1_down,
    fc1_up,
    fc2_down,
    fc2_up,
):
    clip_count = clip_lengths.shape[0]
    own_rows = tokens.shape[0]
    token_rows = own_rows * lax.axis_size("cols")
    clip_len = token_rows // clip_count
    column = lax.axis_index("cols")
    col_width = query_bias.shape[0]
    heads_here = col_width // HEAD_DIM
    block_rows = math.gcd(clip_len, 512)
    block_count = clip_len // block_rows
    score_scale = HEAD_DIM ** (-0.5)

    def own_rows_of(values_in):
        return lax.dynamic_slice_in_dim(values_in, column * own_rows, own_rows, 0)

    (
        w_query,
        w_key,
        w_value,
        w_out,
        w_fc1,
        w_fc2,
        query_down,
        key_down,
        value_down,
        fc1_down,
        out_up,
        fc2_up,
        query_up,
        key_up,
        value_up,
        fc1_up,
        out_down,
        fc2_down,
    ) = (
        lax.all_gather(w_query, "rows", axis=0, tiled=True),
        lax.all_gather(w_key, "rows", axis=0, tiled=True),
        lax.all_gather(w_value, "rows", axis=0, tiled=True),
        lax.all_gather(w_out, "rows", axis=1, tiled=True),
        lax.all_gather(w_fc1, "rows", axis=0, tiled=True),
        lax.all_gather(w_fc2, "rows", axis=1, tiled=True),
        lax.all_gather(query_down, "rows", axis=1, tiled=True),
        lax.all_gather(key_down, "rows", axis=1, tiled=True),
        lax.all_gather(value_down, "rows", axis=1, tiled=True),
        lax.all_gather(fc1_down, "rows", axis=1, tiled=True),
        lax.all_gather(out_up, "rows", axis=2, tiled=True),
        lax.all_gather(fc2_up, "rows", axis=2, tiled=True),
        lax.all_gather(query_up, "rows", axis=1, tiled=True),
        lax.all_gather(key_up, "rows", axis=1, tiled=True),
        lax.all_gather(value_up, "rows", axis=1, tiled=True),
        lax.all_gather(fc1_up, "rows", axis=1, tiled=True),
        lax.all_gather(out_down, "rows", axis=2, tiled=True),
        lax.all_gather(fc2_down, "rows", axis=2, tiled=True),
    )
    full_tokens = lax.all_gather(tokens, "cols", axis=0, tiled=True).astype(jnp.float32)
    row_mean = jnp.mean(full_tokens, axis=-1, keepdims=True)
    centred = full_tokens - row_mean
    inverse_first = lax.rsqrt(jnp.mean(centred * centred, axis=-1, keepdims=True) + EPSILON)
    unit_first = centred * inverse_first
    unit_first_own = own_rows_of(unit_first)
    inverse_first_own = own_rows_of(inverse_first)
    normed = (
        (unit_first * norm1_gain + norm1_shift)
        .astype(jnp.bfloat16)
        .reshape(clip_count, clip_len, D)
    )
    query_rank = rank_down(normed, query_down, clip_sets)
    key_rank = rank_down(normed, key_down, clip_sets)
    value_rank = rank_down(normed, value_down, clip_sets)
    queries = (
        jnp.dot(normed, w_query, preferred_element_type=jnp.float32)
        + query_bias
        + rank_up(query_rank, query_up, clip_sets, clip_scales)
    ).astype(jnp.bfloat16)
    keys_all = (
        jnp.dot(normed, w_key, preferred_element_type=jnp.float32)
        + rank_up(key_rank, key_up, clip_sets, clip_scales)
    ).astype(jnp.bfloat16)
    values_all = (
        jnp.dot(normed, w_value, preferred_element_type=jnp.float32)
        + value_bias
        + rank_up(value_rank, value_up, clip_sets, clip_scales)
    ).astype(jnp.bfloat16)

    def split_heads(values_in):
        return values_in.reshape(clip_count, clip_len, heads_here, HEAD_DIM)

    query_heads = split_heads(queries)
    key_heads = split_heads(keys_all)
    value_heads = split_heads(values_all)

    def block_scores(query_block, key_clip, length):
        raw_scores = (
            jnp.einsum("qhd,khd->hqk", query_block, key_clip, preferred_element_type=jnp.float32)
            * score_scale
        )
        key_valid = jnp.arange(clip_len, dtype=jnp.int32) < length
        return jnp.where(key_valid[None, None, :], raw_scores, MASKED)

    def attend_clip(inputs):
        query_clip, key_clip, value_clip, length = inputs

        def one_block(block_index):
            query_block = lax.dynamic_slice_in_dim(
                query_clip, block_index * block_rows, block_rows, 0
            )
            scores = block_scores(query_block, key_clip, length)
            row_top = jnp.max(scores, axis=-1, keepdims=True)
            exp_terms = jnp.exp(scores - row_top)
            row_total = jnp.sum(exp_terms, axis=-1, keepdims=True)
            attn_probs = (exp_terms / row_total).astype(jnp.bfloat16)
            result = jnp.einsum(
                "hqk,khd->qhd", attn_probs, value_clip, preferred_element_type=jnp.float32
            )
            return (result, (row_top + jnp.log(row_total))[..., 0])

        results, logsum = lax.map(one_block, jnp.arange(block_count))
        return (results.reshape(clip_len, col_width), logsum)

    attended, logsums = lax.map(attend_clip, (query_heads, key_heads, value_heads, clip_lengths))
    attended = attended.astype(jnp.bfloat16)
    out_rank = rank_down(attended, out_down, clip_sets)
    branch = jnp.dot(attended, w_out, preferred_element_type=jnp.float32) + rank_up(
        out_rank, out_up, clip_sets, clip_scales
    )
    branch_sum = lax.psum_scatter(
        branch.reshape(token_rows, D), "cols", scatter_dimension=0, tiled=True
    )
    middle = tokens.astype(jnp.float32) + branch_sum + out_bias
    full_middle = lax.all_gather(middle, "cols", axis=0, tiled=True)
    mean_second = jnp.mean(full_middle, axis=-1, keepdims=True)
    centred_second = full_middle - mean_second
    inverse_second = lax.rsqrt(
        jnp.mean(centred_second * centred_second, axis=-1, keepdims=True) + EPSILON
    )
    unit_second = centred_second * inverse_second
    normed_mlp = (unit_second * norm2_gain + norm2_shift).astype(jnp.bfloat16)
    normed_mlp = normed_mlp.reshape(clip_count, clip_len, D)
    fc1_rank = rank_down(normed_mlp, fc1_down, clip_sets)
    pre_act = (
        jnp.dot(normed_mlp, w_fc1, preferred_element_type=jnp.float32)
        + fc1_bias
        + rank_up(fc1_rank, fc1_up, clip_sets, clip_scales)
    )
    gelu_exact = partial(jax.nn.gelu, approximate=False)
    activated = gelu_exact(pre_act).astype(jnp.bfloat16)
    fc2_rank = rank_down(activated, fc2_down, clip_sets)
    branch_mlp = jnp.dot(activated, w_fc2, preferred_element_type=jnp.float32) + rank_up(
        fc2_rank, fc2_up, clip_sets, clip_scales
    )
    output = (
        middle
        + lax.psum_scatter(
            branch_mlp.reshape(token_rows, D), "cols", scatter_dimension=0, tiled=True
        )
        + fc2_bias
    )
    grad_out = lax.all_gather(cotangent, "cols", axis=0, tiled=True).reshape(
        clip_count, clip_len, D
    )
    grad_fc2_rank = rank_grad(grad_out, fc2_up, clip_sets, clip_scales)
    fc2_up_clip = up_gradient(fc2_rank, grad_out, clip_scales)
    fc2_down_clip = down_gradient(activated, grad_fc2_rank)
    grad_activated = dot_trans(grad_out, w_fc2) + rank_back(grad_fc2_rank, fc2_down, clip_sets)
    gelu_value, gelu_back = jax.vjp(gelu_exact, pre_act)
    grad_pre = gelu_back(grad_activated)[0].astype(jnp.bfloat16)
    grad_fc1_rank = rank_grad(grad_pre, fc1_up, clip_sets, clip_scales)
    fc1_up_clip = up_gradient(fc1_rank, grad_pre, clip_scales)
    fc1_down_clip = down_gradient(normed_mlp, grad_fc1_rank)
    grad_normed_mlp = dot_trans(grad_pre, w_fc1) + rank_back(grad_fc1_rank, fc1_down, clip_sets)
    grad_normed_mlp = lax.psum_scatter(
        grad_normed_mlp.reshape(token_rows, D), "cols", scatter_dimension=0, tiled=True
    )
    full_grad = lax.all_gather(grad_normed_mlp, "cols", axis=0, tiled=True)
    scaled = full_grad * norm2_gain
    first_stat = jnp.mean(scaled, axis=-1, keepdims=True)
    second = jnp.mean(scaled * unit_second, axis=-1, keepdims=True)
    grad_middle_full = grad_out.astype(jnp.float32).reshape(token_rows, D) + inverse_second * (
        scaled - first_stat - unit_second * second
    )
    grad_branch = grad_middle_full.astype(jnp.bfloat16)
    grad_middle = own_rows_of(grad_middle_full)
    grad_branch = grad_branch.reshape(clip_count, clip_len, D)
    grad_out_rank = rank_grad(grad_branch, out_up, clip_sets, clip_scales)
    out_up_clip = up_gradient(out_rank, grad_branch, clip_scales)
    out_down_clip = down_gradient(attended, grad_out_rank)
    grad_attended = (
        dot_trans(grad_branch, w_out) + rank_back(grad_out_rank, out_down, clip_sets)
    ).astype(jnp.bfloat16)
    grad_heads = split_heads(grad_attended)

    def attend_back(inputs):
        query_clip, key_clip, value_clip, grad_clip, length, logsum = inputs

        def one_block(running, block_index):
            grad_keys, grad_values = running
            query_block = lax.dynamic_slice_in_dim(
                query_clip, block_index * block_rows, block_rows, 0
            )
            grad_block = lax.dynamic_slice_in_dim(
                grad_clip, block_index * block_rows, block_rows, 0
            )
            scores = block_scores(query_block, key_clip, length)
            attn_probs = jnp.exp(scores - logsum[block_index][..., None])
            grad_probs = jnp.einsum(
                "qhd,khd->hqk", grad_block, value_clip, preferred_element_type=jnp.float32
            )
            row_inner = jnp.sum(attn_probs * grad_probs, axis=-1, keepdims=True)
            grad_scores = (attn_probs * (grad_probs - row_inner)).astype(jnp.bfloat16)
            grad_query = (
                jnp.einsum(
                    "hqk,khd->qhd", grad_scores, key_clip, preferred_element_type=jnp.float32
                )
                * score_scale
            )
            grad_keys = (
                grad_keys
                + jnp.einsum(
                    "hqk,qhd->khd", grad_scores, query_block, preferred_element_type=jnp.float32
                )
                * score_scale
            )
            grad_values = grad_values + jnp.einsum(
                "hqk,qhd->khd",
                attn_probs.astype(jnp.bfloat16),
                grad_block,
                preferred_element_type=jnp.float32,
            )
            return ((grad_keys, grad_values), grad_query)

        zero_heads = jnp.zeros((clip_len, heads_here, HEAD_DIM), jnp.float32)
        (grad_keys, grad_values), grad_queries = lax.scan(
            one_block, (zero_heads, zero_heads), jnp.arange(block_count)
        )
        return (
            grad_queries.reshape(clip_len, col_width),
            grad_keys.reshape(clip_len, col_width),
            grad_values.reshape(clip_len, col_width),
        )

    grad_queries, grad_keys, grad_values = lax.map(
        attend_back, (query_heads, key_heads, value_heads, grad_heads, clip_lengths, logsums)
    )
    grad_queries = grad_queries.astype(jnp.bfloat16)
    grad_keys = grad_keys.astype(jnp.bfloat16)
    grad_values = grad_values.astype(jnp.bfloat16)
    grad_query_rank = rank_grad(grad_queries, query_up, clip_sets, clip_scales)
    grad_key_rank = rank_grad(grad_keys, key_up, clip_sets, clip_scales)
    grad_value_rank = rank_grad(grad_values, value_up, clip_sets, clip_scales)
    query_up_clip = up_gradient(query_rank, grad_queries, clip_scales)
    key_up_clip = up_gradient(key_rank, grad_keys, clip_scales)
    value_up_clip = up_gradient(value_rank, grad_values, clip_scales)
    query_down_clip = down_gradient(normed, grad_query_rank)
    key_down_clip = down_gradient(normed, grad_key_rank)
    value_down_clip = down_gradient(normed, grad_value_rank)
    grad_normed = (
        dot_trans(grad_queries, w_query)
        + dot_trans(grad_keys, w_key)
        + dot_trans(grad_values, w_value)
    )
    grad_normed = (
        grad_normed
        + rank_back(grad_query_rank, query_down, clip_sets)
        + rank_back(grad_key_rank, key_down, clip_sets)
        + rank_back(grad_value_rank, value_down, clip_sets)
    )
    grad_normed = lax.psum_scatter(
        grad_normed.reshape(token_rows, D), "cols", scatter_dimension=0, tiled=True
    )
    scaled_first = grad_normed * norm1_gain
    first_mean = jnp.mean(scaled_first, axis=-1, keepdims=True)
    second_mean = jnp.mean(scaled_first * unit_first_own, axis=-1, keepdims=True)
    grad_tokens = grad_middle + inverse_first_own * (
        scaled_first - first_mean - unit_first_own * second_mean
    )
    summed = (
        lax.psum_scatter(
            per_set(query_down_clip, clip_sets), "rows", scatter_dimension=1, tiled=True
        ),
        lax.psum_scatter(
            per_set(key_down_clip, clip_sets), "rows", scatter_dimension=1, tiled=True
        ),
        lax.psum_scatter(
            per_set(value_down_clip, clip_sets), "rows", scatter_dimension=1, tiled=True
        ),
        lax.psum_scatter(
            per_set(fc1_down_clip, clip_sets), "rows", scatter_dimension=1, tiled=True
        ),
        lax.psum_scatter(per_set(out_up_clip, clip_sets), "rows", scatter_dimension=2, tiled=True),
        lax.psum_scatter(per_set(fc2_up_clip, clip_sets), "rows", scatter_dimension=2, tiled=True),
        lax.psum_scatter(
            per_set(query_up_clip, clip_sets), "rows", scatter_dimension=1, tiled=True
        ),
        lax.psum_scatter(per_set(key_up_clip, clip_sets), "rows", scatter_dimension=1, tiled=True),
        lax.psum_scatter(
            per_set(value_up_clip, clip_sets), "rows", scatter_dimension=1, tiled=True
        ),
        lax.psum_scatter(per_set(fc1_up_clip, clip_sets), "rows", scatter_dimension=1, tiled=True),
        lax.psum_scatter(
            per_set(out_down_clip, clip_sets), "rows", scatter_dimension=2, tiled=True
        ),
        lax.psum_scatter(
            per_set(fc2_down_clip, clip_sets), "rows", scatter_dimension=2, tiled=True
        ),
    )
    feature_side = lax.psum(
        (summed[0], summed[1], summed[2], summed[3], summed[4], summed[5]), "cols"
    )
    return (
        output.astype(jnp.bfloat16),
        grad_tokens.astype(jnp.bfloat16),
        feature_side[0],
        summed[6],
        feature_side[1],
        summed[7],
        feature_side[2],
        summed[8],
        summed[10],
        feature_side[4],
        feature_side[3],
        summed[9],
        summed[11],
        feature_side[5],
    )


def solution(mesh):
    return jax.shard_map(
        body,
        mesh=mesh,
        in_specs=(
            P(("rows", "cols"), None),
            P(("rows", "cols"), None),
            P("rows"),
            P("rows"),
            P("rows"),
            P(),
            P(),
            P("rows", "cols"),
            P("cols"),
            P("rows", "cols"),
            P("rows", "cols"),
            P("cols"),
            P("cols", "rows"),
            P(),
            P(),
            P(),
            P("rows", "cols"),
            P("cols"),
            P("cols", "rows"),
            P(),
            P(None, "rows", None),
            P(None, "rows", "cols"),
            P(None, "rows", None),
            P(None, "rows", "cols"),
            P(None, "rows", None),
            P(None, "rows", "cols"),
            P(None, "cols", "rows"),
            P(None, None, "rows"),
            P(None, "rows", None),
            P(None, "rows", "cols"),
            P(None, "cols", "rows"),
            P(None, None, "rows"),
        ),
        out_specs=(
            P(("rows", "cols"), None),
            P(("rows", "cols"), None),
            P(None, "rows", None),
            P(None, "rows", "cols"),
            P(None, "rows", None),
            P(None, "rows", "cols"),
            P(None, "rows", None),
            P(None, "rows", "cols"),
            P(None, "cols", "rows"),
            P(None, None, "rows"),
            P(None, "rows", None),
            P(None, "rows", "cols"),
            P(None, "cols", "rows"),
            P(None, None, "rows"),
        ),
        check_vma=False,
    )
```

profile of v0, /device:TPU:0, one launch (start us, length us, event | category | flops | bytes accessed | tf_op | source)
XLA Modules:
  0.0 3390.8 jit_solution(3267643330150437728)
XLA Ops:
  146.1 51.4 %all_gather.78 = bf16[8,16,1280]{1,0,2:T(8,128)(2,1)S(1)} all-gather(bf16[8,16,160]{1,0,2:T(8,128)(2,1)} %copy.170), channel_id=1, replica_groups=mesh['rows'=8,'cols'=4] {'rows'}, dimensions={2}, use_global_device_ids=true | all-gather | bytes 368640 | tf_op jit(solution)/shard_map/all_gather | solution.py:177
  201.9 52.5 %all_gather.74 = bf16[8,1280,16]{2,0,1:T(8,128)(2,1)S(1)} all-gather(bf16[8,160,16]{2,0,1:T(8,128)(2,1)S(1)} %copy.164), channel_id=1, replica_groups=mesh['rows'=8,'cols'=4] {'rows'}, dimensions={1}, use_global_device_ids=true | all-gather | bytes 368640 | tf_op jit(solution)/shard_map/all_gather | solution.py:175
  256.6 54.6 %all_gather.71 = bf16[8,1280,16]{2,0,1:T(8,128)(2,1)S(1)} all-gather(bf16[8,160,16]{2,0,1:T(8,128)(2,1)} %copy.160), channel_id=1, replica_groups=mesh['rows'=8,'cols'=4] {'rows'}, dimensions={1}, use_global_device_ids=true | all-gather | bytes 368640 | tf_op jit(solution)/shard_map/all_gather | solution.py:174
  592.4 246.2 %while.54 = (s32[]{:T(128)}, bf16[3,1536,320]{1,2,0:T(8,128)(2,1)}, f32[3,3,4,512]{3,2,1,0:T(4,128)}, bf16[3,1536,4,80]{1,3,2,0:T(8,128)(2,1)}, bf16[3,1536,4,80...) while((s32[]{:T(128)}, bf16[3,1536,320]{1,2,0:T(8,128)(2,1)}, ...), condition=%wide.region_7.10_spmd, body=%wide.region_2.9_spmd.sunk | while | flops 1044381184 | bytes 51633116 | solution.py:251
  597.3 72.9 %while.57 = (s32[]{:T(128)}, bf16[3,512,4,80]{1,0,3,2:T(4,128)(2,1)}, f32[3,4,512]{2,1,0:T(4,128)S(1)}, s32[]{:T(128)}, s32[3]{0:T(128)S(1)}, /*index=5*/bf16[15...) while((s32[]{:T(128)}, ...), condition=%wide.region_6.8_spmd, body=%wide.region_3.7_spmd.sunk | while | flops 1044381184 | bytes 41753288 | solution.py:248
  679.2 72.9 %while.57 = (s32[]{:T(128)}, bf16[3,512,4,80]{1,0,3,2:T(4,128)(2,1)}, f32[3,4,512]{2,1,0:T(4,128)S(1)}, s32[]{:T(128)}, s32[3]{0:T(128)S(1)}, /*index=5*/bf16[15...) while((s32[]{:T(128)}, ...), condition=%wide.region_6.8_spmd, body=%wide.region_3.7_spmd.sunk | while | flops 1044381184 | bytes 41753288 | solution.py:248
  761.2 72.9 %while.57 = (s32[]{:T(128)}, bf16[3,512,4,80]{1,0,3,2:T(4,128)(2,1)}, f32[3,4,512]{2,1,0:T(4,128)S(1)}, s32[]{:T(128)}, s32[3]{0:T(128)S(1)}, /*index=5*/bf16[15...) while((s32[]{:T(128)}, ...), condition=%wide.region_6.8_spmd, body=%wide.region_3.7_spmd.sunk | while | flops 1044381184 | bytes 41753288 | solution.py:248
  889.4 167.2 %reduce-scatter.29.cloned.1.call-done = f32[1152,1280]{1,0:T(8,128)} async-done(((f32[4608,1280]{1,0:T(8,128)}), f32[1152,1280]{1,0:T(8,128)}) %reduce-scatter.29.cloned.1.call-update) | async-done | bytes 5898256 | tf_op jit(solution)/shard_map/reduce_scatter | solution.py:257
  1130.8 49.0 %all_gather.85 = bf16[8,16,1280]{1,0,2:T(8,128)(2,1)S(1)} all-gather(bf16[8,16,160]{1,0,2:T(8,128)(2,1)} %copy.178), channel_id=1, replica_groups=mesh['rows'=8,'cols'=4] {'rows'}, dimensions={2}, use_global_device_ids=true | all-gather | bytes 368640 | tf_op jit(solution)/shard_map/all_gather | solution.py:178
  1183.5 45.3 %all_gather.81 = bf16[8,1280,16]{2,0,1:T(8,128)(2,1)S(1)} all-gather(bf16[8,160,16]{2,0,1:T(8,128)(2,1)S(1)} %copy.172), channel_id=1, replica_groups=mesh['rows'=8,'cols'=4] {'rows'}, dimensions={1}, use_global_device_ids=true | all-gather | bytes 368640 | tf_op jit(solution)/shard_map/all_gather | solution.py:176
  1381.0 54.6 %multiply_convert_fusion.1 = (bf16[3,1536,1280]{2,1,0:T(8,128)(2,1)}, f32[3,1536,1280]{2,1,0:T(8,128)}) fusion(f32[3,1536,1280]{2,1,0:T(8,128)} %get-tuple-element.418, u8[1536,1280]{1,0:T(8,128)(4,1)S(1)} %get-tuple-element.417), kind=kLoop, calls=%fused_computation.77 | loop fusion | flops 401080320 | bytes 60948480 | tf_op jit(solution)/shard_map/convert_element_type | solution.py:277
  1534.0 170.4 %reduce-scatter.33.cloned.1.call-done = f32[1152,1280]{1,0:T(8,128)} async-done(((f32[4608,1280]{1,0:T(8,128)}), f32[1152,1280]{1,0:T(8,128)}) %reduce-scatter.33.cloned.1.call-update) | async-done | bytes 5898256 | tf_op jit(solution)/shard_map/reduce_scatter | solution.py:302
  1778.9 73.1 %all-gather.17.cloned.1.call-done = f32[4608,1280]{1,0:T(8,128)} async-done(((f32[1152,1280]{1,0:T(8,128)}), f32[4608,1280]{1,0:T(8,128)}) %all-gather.17.cloned.1.call-update) | async-done | bytes 23592976 | tf_op jit(solution)/shard_map/all_gather | solution.py:305
  1923.2 391.7 %while.56 = (s32[]{:T(128)}, bf16[3,1536,320]{1,2,0:T(8,128)(2,1)}, bf16[3,1536,320]{1,2,0:T(8,128)(2,1)}, bf16[3,1536,320]{1,2,0:T(8,128)(2,1)}, bf16[3,1536,4,...) while((s32[]{:T(128)}, bf16[3,1536,320]{1,2,0:T(8,128)(2,1)}, ...), condition=%wide.region_19.24_spmd, body=%wide.region_15.23_spmd.sunk | while | flops 2547678720 | bytes 172715760 | solution.py:372
  1930.9 115.2 %while.58 = (s32[]{:T(128)}, f32[1536,4,80]{0,2,1:T(8,128)}, f32[1536,4,80]{0,2,1:T(8,128)S(1)}, bf16[3,512,4,80]{1,0,3,2:T(4,128)(2,1)}, s32[3]{0:T(128)S(1)}, ...) while((s32[]{:T(128)}, f32[1536,4,80]{0,2,1:T(8,128)}, ...), condition=%wide.region_18.22_spmd.clone, body=%wide.region_16.21_spmd.clone.sunk | while | flops 2547678720 | bytes 153005456 | solution.py:363
  2061.3 115.2 %while.58 = (s32[]{:T(128)}, f32[1536,4,80]{0,2,1:T(8,128)}, f32[1536,4,80]{0,2,1:T(8,128)S(1)}, bf16[3,512,4,80]{1,0,3,2:T(4,128)(2,1)}, s32[3]{0:T(128)S(1)}, ...) while((s32[]{:T(128)}, f32[1536,4,80]{0,2,1:T(8,128)}, ...), condition=%wide.region_18.22_spmd.clone, body=%wide.region_16.21_spmd.clone.sunk | while | flops 2547678720 | bytes 153005456 | solution.py:363
  2191.7 115.2 %while.58 = (s32[]{:T(128)}, f32[1536,4,80]{0,2,1:T(8,128)}, f32[1536,4,80]{0,2,1:T(8,128)S(1)}, bf16[3,512,4,80]{1,0,3,2:T(4,128)(2,1)}, s32[3]{0:T(128)S(1)}, ...) while((s32[]{:T(128)}, f32[1536,4,80]{0,2,1:T(8,128)}, ...), condition=%wide.region_18.22_spmd.clone, body=%wide.region_16.21_spmd.clone.sunk | while | flops 2547678720 | bytes 153005456 | solution.py:363
  2622.1 66.9 %add_add_fusion = f32[3,1536,1280]{2,1,0:T(8,128)} fusion(f32[3,1536,1280]{2,1,0:T(8,128)} %fusion.125, f32[3,1536,1280]{2,1,0:T(8,128)} %fusion.129, f32[3,1536,1280]{2,1,0:T(8,128)} %fusion.131, f32[3,1536,1280]{2,1,0:T(8,128)} %fusion.134, f32[3,1536,1280]{2,1,0:T(8,128)} %fusion.136, f32[3,1536,1280]{2,1,0:T(8,128)} %fusion.48, ...), kind=kOutput, calls=%fused_computation.71 | convolution fusion | flops 236285952 | bytes 212754432 | tf_op jit(solution)/shard_map/tsj,tvj->tsv/dot_general | solution.py:32
  2732.9 171.5 %reduce-scatter.31.cloned.1.call-done = f32[1152,1280]{1,0:T(8,128)} async-done(((f32[4608,1280]{1,0:T(8,128)}), f32[1152,1280]{1,0:T(8,128)}) %reduce-scatter.31.cloned.1.call-update) | async-done | bytes 5898256 | tf_op jit(solution)/shard_map/reduce_scatter | solution.py:284
  2911.2 58.3 %reduce-scatter.43.cloned.1.call-done = f32[8,320,2]{1,0,2:T(8,128)} async-done(((f32[8,320,16]{1,0,2:T(8,128)}), f32[8,320,2]{1,0,2:T(8,128)}) %reduce-scatter.43.cloned.1.call-update) | async-done | bytes 20496 | tf_op jit(solution)/shard_map/reduce_scatter | solution.py:430
  2970.9 63.0 %reduce-scatter.39.cloned.1.call-done = f32[8,2,320]{2,0,1:T(8,128)} async-done(((f32[8,16,320]{2,0,1:T(8,128)}), f32[8,2,320]{2,0,1:T(8,128)}) %reduce-scatter.39.cloned.1.call-update) | async-done | bytes 20496 | tf_op jit(solution)/shard_map/reduce_scatter | solution.py:425
  3035.2 63.4 %reduce-scatter.37.cloned.1.call-done = f32[8,2,320]{2,0,1:T(8,128)} async-done(((f32[8,16,320]{2,0,1:T(8,128)}), f32[8,2,320]{2,0,1:T(8,128)}) %reduce-scatter.37.cloned.1.call-update) | async-done | bytes 20496 | tf_op jit(solution)/shard_map/reduce_scatter | solution.py:422
  3099.9 62.9 %reduce-scatter.41.cloned.1.call-done = f32[8,2,320]{2,0,1:T(8,128)} async-done(((f32[8,16,320]{2,0,1:T(8,128)}), f32[8,2,320]{2,0,1:T(8,128)}) %reduce-scatter.41.cloned.1.call-update) | async-done | bytes 20496 | tf_op jit(solution)/shard_map/reduce_scatter | solution.py:426
  3210.7 160.9 %reduce-scatter.35.cloned.1.call-done = f32[1152,1280]{1,0:T(8,128)} async-done(((f32[4608,1280]{1,0:T(8,128)}), f32[1152,1280]{1,0:T(8,128)}) %reduce-scatter.35.cloned.1.call-update) | async-done | bytes 5898256 | tf_op jit(solution)/shard_map/reduce_scatter | solution.py:398
  (760 shorter events, 1979.2 us)
Async XLA Ops:
  7.2 490.4 %all-gather.7.cloned.1.call-start = ((), (), s32[]{:S(2)}) async-start(), calls=%async_computation.16 | async-start | bytes 14745600 | tf_op jit(solution)/shard_map/all_gather | solution.py:186
  7.9 1048.8 %reduce-scatter.29.cloned.1.call-start = ((), (), s32[]{:S(2)}) async-start(), calls=%async_computation.17 | async-start | bytes 29491200 | tf_op jit(solution)/shard_map/reduce_scatter | solution.py:257
  888.6 342.4 %all-gather.15.cloned.1.call-start = ((), (), s32[]{:S(2)}) async-start(), calls=%async_computation.22 | async-start | bytes 14745600 | tf_op jit(solution)/shard_map/all_gather | solution.py:289
  889.4 394.1 %all-gather.9.cloned.1.call-start = ((), (), s32[]{:S(2)}) async-start(), calls=%async_computation.18 | async-start | bytes 29491200 | tf_op jit(solution)/shard_map/all_gather | solution.py:261
  1062.5 284.4 %all-gather.11.cloned.1.call-start = ((), (), s32[]{:S(2)}) async-start(), calls=%async_computation.19 | async-start | bytes 3686400 | tf_op jit(solution)/shard_map/all_gather | solution.py:171
  1063.1 372.4 %all-gather.13.cloned.1.call-start = ((), (), s32[]{:S(2)}) async-start(), calls=%async_computation.20 | async-start | bytes 3686400 | tf_op jit(solution)/shard_map/all_gather | solution.py:172
  1063.7 640.7 %reduce-scatter.33.cloned.1.call-start = ((), (), s32[]{:S(2)}) async-start(), calls=%async_computation.23 | async-start | bytes 29491200 | tf_op jit(solution)/shard_map/reduce_scatter | solution.py:302
  1534.0 318.1 %all-gather.17.cloned.1.call-start = ((), (), s32[]{:S(2)}) async-start(), calls=%async_computation.24 | async-start | bytes 29491200 | tf_op jit(solution)/shard_map/all_gather | solution.py:305
  1704.4 787.6 %reduce-scatter.59.cloned.1.call-start = ((), (), s32[]{:S(2)}) async-start(), calls=%async_computation.37 | async-start | bytes 737280
  1750.2 747.2 %reduce-scatter.57.cloned.1.call-start = ((), (), s32[]{:S(2)}) async-start(), calls=%async_computation.36 | async-start | bytes 737280
  1778.9 831.6 %reduce-scatter.53.cloned.1.call-start = ((), (), s32[]{:S(2)}) async-start(), calls=%async_computation.34 | async-start | bytes 737280
  2343.3 270.1 %reduce-scatter.49.cloned.1.call-start = ((), (), s32[]{:S(2)}) async-start(), calls=%async_computation.32 | async-start | bytes 737280
  2373.5 242.7 %reduce-scatter.51.cloned.1.call-start = ((), (), s32[]{:S(2)}) async-start(), calls=%async_computation.33 | async-start | bytes 737280
  2400.7 218.4 %reduce-scatter.55.cloned.1.call-start = ((), (), s32[]{:S(2)}) async-start(), calls=%async_computation.35 | async-start | bytes 737280
  2427.6 262.1 %reduce-scatter.47.cloned.1.call-start = ((), (), s32[]{:S(2)}) async-start(), calls=%async_computation.31 | async-start | bytes 737280 | tf_op jit(solution)/shard_map/reduce_scatter | solution.py:433
  2443.7 287.7 %reduce-scatter.45.cloned.1.call-start = ((), (), s32[]{:S(2)}) async-start(), calls=%async_computation.30 | async-start | bytes 737280 | tf_op jit(solution)/shard_map/reduce_scatter | solution.py:429
  2461.2 443.2 %reduce-scatter.31.cloned.1.call-start = ((), (), s32[]{:S(2)}) async-start(), calls=%async_computation.21 | async-start | bytes 29491200 | tf_op jit(solution)/shard_map/reduce_scatter | solution.py:284
  2492.0 477.6 %reduce-scatter.43.cloned.1.call-start = ((), (), s32[]{:S(2)}) async-start(), calls=%async_computation.29 | async-start | bytes 221184 | tf_op jit(solution)/shard_map/reduce_scatter | solution.py:430
  2590.8 443.0 %reduce-scatter.39.cloned.1.call-start = ((), (), s32[]{:S(2)}) async-start(), calls=%async_computation.27 | async-start | bytes 221184 | tf_op jit(solution)/shard_map/reduce_scatter | solution.py:425
  2594.8 503.7 %reduce-scatter.37.cloned.1.call-start = ((), (), s32[]{:S(2)}) async-start(), calls=%async_computation.26 | async-start | bytes 221184 | tf_op jit(solution)/shard_map/reduce_scatter | solution.py:422
  2597.7 565.1 %reduce-scatter.41.cloned.1.call-start = ((), (), s32[]{:S(2)}) async-start(), calls=%async_computation.28 | async-start | bytes 221184 | tf_op jit(solution)/shard_map/reduce_scatter | solution.py:426
  2600.7 600.4 %all-reduce.3.cloned.1.call-start = ((), (), s32[]{:S(2)}) async-start(), calls=%async_computation.38 | async-start | bytes 1572864 | tf_op jit(solution)/shard_map/psum | solution.py:437
  2622.0 749.6 %reduce-scatter.35.cloned.1.call-start = ((), (), s32[]{:S(2)}) async-start(), calls=%async_computation.25 | async-start | bytes 29491200 | tf_op jit(solution)/shard_map/reduce_scatter | solution.py:398
  2689.0 682.7 %copy-start.72 = (f32[1280]{0:T(1024)S(1)}, f32[1280]{0:T(1024)}, u32[]{:S(2)}) copy-start(f32[1280]{0:T(1024)} %param.53) | copy-start | bytes 15364
  (132 other events, 6242.3 us)
Sparse Core Ops, SparseCore 0:
  9.5 80.3 all-gather.6
  888.7 167.9 reduce-scatter.28
  1058.2 77.6 all-gather.14
  1137.3 146.0 all-gather.8
  1285.5 61.4 all-gather.10
  1349.0 60.1 all-gather.12
  1534.1 170.2 reduce-scatter.32
  1705.9 146.0 all-gather.16
  1855.3 62.7 reduce-scatter.58
  1921.3 61.7 reduce-scatter.56
  2343.4 62.9 reduce-scatter.52
  2409.6 61.7 reduce-scatter.48
  2474.7 61.7 reduce-scatter.50
  2539.6 61.7 reduce-scatter.54
  2604.6 61.7 reduce-scatter.46
  2669.5 61.7 reduce-scatter.44
  2733.8 170.5 reduce-scatter.30
  2907.5 61.9 reduce-scatter.42
  2972.8 61.0 reduce-scatter.38
  3037.5 60.9 reduce-scatter.36
  3101.8 60.9 reduce-scatter.40
  3166.7 34.2 all-reduce.2
  3203.7 167.8 reduce-scatter.34
where the time goes:
time: 3420 us; the launch traced here: 3390 us
  waiting for transfers between devices  1100 us (32%)
  matrix products  851 us (25%)
  blocking collectives  624 us (18%)
  local copies, waits for them, and re-layouts  518 us (15%)
  other arithmetic  249 us (7%)
    dynamic_update_slice x36, local copies, waits for them, and re-layouts, attend_clip(): results, logsum = lax.map(one_block, jnp.arange(block_count))  242 us
    dot_general x24, matrix products, paired_contraction(): jnp.einsum(form, lower_part, narrow_side, preferred_element_type=jnp.floa...  214 us
    reduce_scatter x1, waiting for transfers between devices, body(): lax.psum_scatter(branch_mlp.reshape(token_rows, D), 'cols', scatter_dimen...  172 us
    reduce_scatter x1, waiting for transfers between devices, body(): lax.psum_scatter(grad_normed_mlp.reshape(token_rows, D), 'cols', scatter_...  170 us
    reduce_scatter x1, waiting for transfers between devices, body(): lax.psum_scatter(branch.reshape(token_rows, D), 'cols', scatter_dimension...  167 us
    reduce_scatter x1, waiting for transfers between devices, body(): lax.psum_scatter(grad_normed.reshape(token_rows, D), 'cols', scatter_dime...  161 us
    unnamed x242, local copies, waits for them, and re-layouts  145 us
    dot_general x24, matrix products, paired_contraction(): jnp.einsum(form, upper_part, narrow_side, preferred_element_type=jnp.floa...  144 us
  transfers between devices with their start and end apart: 23, of which 13 were waited for; matrix products, arithmetic and copies ran while one was open for 32% of the time, Pallas kernels for 0%

commit v1 on v0

v1 whole, which is shorter than its diff:
```python
import functools
import math

import jax
import jax.numpy as jnp
from jax import lax
from jax.experimental import pallas as pl
from jax.experimental.pallas import tpu as pltpu
from jax.sharding import PartitionSpec as P

D = 1280
SETS = 8
RANK = 16
HEAD_DIM = 80
EPSILON = 1e-05
LOG2E = 1.4426950408889634
LOW = -1e30
F32 = jnp.float32
BF = jnp.bfloat16
BOTH = ("rows", "cols")


def dot(a, b):
    return lax.dot_general(a, b, (((1,), (0,)), ((), ())), preferred_element_type=F32)


def dot_t(a, b):
    return lax.dot_general(a, b, (((1,), (1,)), ((), ())), preferred_element_type=F32)


def token_sum(a, b):
    return dot(a.T.astype(BF), b)


def norm_parts(x):
    mean = jnp.mean(x, axis=-1, keepdims=True)
    centred = x - mean
    inverse = lax.rsqrt(jnp.mean(centred * centred, axis=-1, keepdims=True) + EPSILON)
    return centred * inverse, inverse


def params(n, limit=60 << 20):
    return pltpu.CompilerParams(
        dimension_semantics=("arbitrary",) * n, vmem_limit_bytes=limit
    )


def cost(flops, nbytes, trans=0):
    return pl.CostEstimate(flops=int(flops), bytes_accessed=int(nbytes), transcendentals=int(trans))


def attend_kernel(hh, length, qb, kb, lens, x_ref, o_ref, lse_ref, k_scr, vt_scr, acc, m_scr, l_scr):
    p = pl.program_id(0)
    qi = pl.program_id(1)
    w = hh * HEAD_DIM
    c = HEAD_DIM**-0.5 * LOG2E

    @pl.when(qi == 0)
    def _():
        vt_scr[...] = x_ref[0, :, 2 * w : 3 * w].T
        for h in range(hh):
            k_scr[h] = x_ref[0, :, w + h * HEAD_DIM : w + (h + 1) * HEAD_DIM]

    size = lens[p]
    block = x_ref[0, pl.ds(pl.multiple_of(qi * qb, qb), qb), 0:w]
    qs = [block[:, h * HEAD_DIM : (h + 1) * HEAD_DIM] for h in range(hh)]
    m_scr[...] = jnp.full_like(m_scr, LOW)
    l_scr[...] = jnp.zeros_like(l_scr)
    acc[...] = jnp.zeros_like(acc)

    def chunk(i, masked):
        r0 = pl.multiple_of(i * kb, kb)
        for h in range(hh):
            s = dot_t(k_scr[h, pl.ds(r0, kb), :], qs[h])
            if masked:
                keys = lax.broadcasted_iota(jnp.int32, (kb, qb), 0) + i * kb
                s = jnp.where(keys < size, s, LOW)
            old = m_scr[h : h + 1]
            top = jnp.maximum(old, jnp.max(s, axis=0, keepdims=True))
            probs = jnp.exp2((s - top) * c)
            shrink = jnp.exp2((old - top) * c)
            l_scr[h : h + 1] = l_scr[h : h + 1] * shrink + jnp.sum(probs, axis=0, keepdims=True)
            m_scr[h : h + 1] = top
            acc[h] = acc[h] * shrink + dot(
                vt_scr[h * HEAD_DIM : (h + 1) * HEAD_DIM, pl.ds(r0, kb)], probs.astype(BF)
            )

    full = size // kb

    def step(i, carry):
        chunk(i, False)
        return carry

    lax.fori_loop(0, full, step, 0)

    @pl.when(full * kb < size)
    def _():
        chunk(full, True)

    outs = [acc[h] * (1.0 / l_scr[h : h + 1]) for h in range(hh)]
    o_ref[0] = jnp.concatenate(outs, axis=0).T.astype(BF)
    lse_ref[0] = m_scr[0:hh] * c + jnp.log2(l_scr[0:hh])


def attend(x, lens, hh):
    problems, length, w3 = x.shape
    w = hh * HEAD_DIM
    qb = math.gcd(length, 512)
    kb = math.gcd(length, 768)
    return pl.pallas_call(
        functools.partial(attend_kernel, hh, length, qb, kb),
        out_shape=(
            jax.ShapeDtypeStruct((problems, length, w), BF),
            jax.ShapeDtypeStruct((problems, hh, length), F32),
        ),
        grid_spec=pltpu.PrefetchScalarGridSpec(
            num_scalar_prefetch=1,
            grid=(problems, length // qb),
            in_specs=[pl.BlockSpec((1, length, w3), lambda p, q, l: (p, 0, 0))],
            out_specs=[
                pl.BlockSpec((1, qb, w), lambda p, q, l: (p, q, 0)),
                pl.BlockSpec((1, hh, qb), lambda p, q, l: (p, 0, q)),
            ],
            scratch_shapes=[
                pltpu.VMEM((hh, length, HEAD_DIM), BF),
                pltpu.VMEM((w, length), BF),
                pltpu.VMEM((hh, HEAD_DIM, qb), F32),
                pltpu.VMEM((max(8, hh), qb), F32),
                pltpu.VMEM((max(8, hh), qb), F32),
            ],
        ),
        compiler_params=params(2),
        cost_estimate=cost(
            problems * hh * 4 * length * length * 256, x.size * 3, problems * hh * length * length
        ),
        name="attend",
    )(lens, x)


def attend_back_kernel(
    hh, length, qb, kb, lens, x_ref, o_ref, do_ref, lse_ref, dx_ref, k_scr, v_scr, kt_scr, dk, dv, dqt
):
    p = pl.program_id(0)
    qi = pl.program_id(1)
    w = hh * HEAD_DIM
    scale = HEAD_DIM**-0.5
    c = scale * LOG2E

    @pl.when(qi == 0)
    def _():
        kt_scr[...] = x_ref[0, :, w : 2 * w].T
        for h in range(hh):
            k_scr[h] = x_ref[0, :, w + h * HEAD_DIM : w + (h + 1) * HEAD_DIM]
            v_scr[h] = x_ref[0, :, 2 * w + h * HEAD_DIM : 2 * w + (h + 1) * HEAD_DIM]
        dk[...] = jnp.zeros_like(dk)
        dv[...] = jnp.zeros_like(dv)

    size = lens[p]
    rows = pl.ds(pl.multiple_of(qi * qb, qb), qb)
    block = x_ref[0, rows, 0:w]
    qs = [block[:, h * HEAD_DIM : (h + 1) * HEAD_DIM] for h in range(hh)]
    do = do_ref[0]
    dos = [do[:, h * HEAD_DIM : (h + 1) * HEAD_DIM] for h in range(hh)]
    prod = (do.astype(F32) * o_ref[0].astype(F32)).T
    inner = [
        jnp.sum(prod[h * HEAD_DIM : (h + 1) * HEAD_DIM], axis=0, keepdims=True) for h in range(hh)
    ]
    dqt[...] = jnp.zeros_like(dqt)

    def chunk(i, masked):
        keys_at = pl.ds(pl.multiple_of(i * kb, kb), kb)
        for h in range(hh):
            s = dot_t(k_scr[h, keys_at, :], qs[h])
            probs = jnp.exp2(s * c - lse_ref[0, h : h + 1])
            if masked:
                keys = lax.broadcasted_iota(jnp.int32, (kb, qb), 0) + i * kb
                probs = jnp.where(keys < size, probs, 0.0)
            dp = dot_t(v_scr[h, keys_at, :], dos[h])
            ds = (probs * (dp - inner[h])).astype(BF)
            dv[h, keys_at, :] += dot(probs.astype(BF), dos[h])
            dk[h, keys_at, :] += dot(ds, qs[h])
            dqt[h] += dot(kt_scr[h * HEAD_DIM : (h + 1) * HEAD_DIM, keys_at], ds)

    full = size // kb

    def step(i, carry):
        chunk(i, False)
        return carry

    lax.fori_loop(0, full, step, 0)

    @pl.when(full * kb < size)
    def _():
        chunk(full, True)

    dq = jnp.concatenate([dqt[h] for h in range(hh)], axis=0).T * scale
    dx_ref[0, rows, 0:w] = dq.astype(BF)

    @pl.when(qi == pl.num_programs(1) - 1)
    def _():
        for h in range(hh):
            dx_ref[0, :, w + h * HEAD_DIM : w + (h + 1) * HEAD_DIM] = (dk[h] * scale).astype(BF)
            dx_ref[0, :, 2 * w + h * HEAD_DIM : 2 * w + (h + 1) * HEAD_DIM] = dv[h].astype(BF)


def attend_back(x, o, do, lse, lens, hh):
    problems, length, w3 = x.shape
    w = hh * HEAD_DIM
    qb = math.gcd(length, 512)
    kb = math.gcd(length, 512)
    return pl.pallas_call(
        functools.partial(attend_back_kernel, hh, length, qb, kb),
        out_shape=jax.ShapeDtypeStruct((problems, length, w3), BF),
        grid_spec=pltpu.PrefetchScalarGridSpec(
            num_scalar_prefetch=1,
            grid=(problems, length // qb),
            in_specs=[
                pl.BlockSpec((1, length, w3), lambda p, q, l: (p, 0, 0)),
                pl.BlockSpec((1, qb, w), lambda p, q, l: (p, q, 0)),
                pl.BlockSpec((1, qb, w), lambda p, q, l: (p, q, 0)),
                pl.BlockSpec((1, hh, qb), lambda p, q, l: (p, 0, q)),
            ],
            out_specs=pl.BlockSpec((1, length, w3), lambda p, q, l: (p, 0, 0)),
            scratch_shapes=[
                pltpu.VMEM((hh, length, HEAD_DIM), BF),
                pltpu.VMEM((hh, length, HEAD_DIM), BF),
                pltpu.VMEM((w, length), BF),
                pltpu.VMEM((hh, length, HEAD_DIM), F32),
                pltpu.VMEM((hh, length, HEAD_DIM), F32),
                pltpu.VMEM((hh, HEAD_DIM, qb), F32),
            ],
        ),
        compiler_params=params(2),
        cost_estimate=cost(
            problems * hh * 10 * length * length * 256, x.size * 6, problems * hh * length * length
        ),
        name="attend_back",
    )(lens, x, o, do, lse)


def spread(up3, width):
    piece = lax.broadcasted_iota(jnp.int32, up3.shape, 0) // RANK
    return jnp.concatenate([jnp.where(piece == j, up3, jnp.zeros_like(up3)) for j in range(3)], axis=1)


def project_kernel(
    tm, width, sets, scales, x_ref, gain, shift, w_ref, bias, down, up, normed_ref, ranks_ref, y_ref, n_scr, r_scr
):
    c = pl.program_id(0)
    m = pl.program_id(1)
    rows = pl.ds(pl.multiple_of(m * tm, tm), tm)

    @pl.when(c == 0)
    def _():
        unit, _ = norm_parts(x_ref[...].astype(F32))
        normed = (unit * gain[...] + shift[...]).astype(BF)
        n_scr[rows, :] = normed
        normed_ref[...] = normed
        rank = (dot_t(normed, down[0]) * scales[m]).astype(BF)
        r_scr[rows, :] = rank
        ranks_ref[...] = rank

    y = dot(n_scr[rows, :], w_ref[:, 0].reshape(D, 3 * width))
    y += dot(r_scr[rows, :], spread(up[0, 0], width))
    y_ref[0] = (y + bias[0]).astype(BF)


def project(tokens, gain, shift, gathered, bias, down, up, sets, scales, tm):
    own = tokens.shape[0]
    rr, nc, _, w3 = gathered.shape
    width = w3 // 3
    first = lambda c, m, s, a: (jnp.where(c == 0, m, own // tm - 1), 0)
    return pl.pallas_call(
        functools.partial(project_kernel, tm, width),
        out_shape=(
            jax.ShapeDtypeStruct((own, D), BF),
            jax.ShapeDtypeStruct((own, 3 * RANK), BF),
            jax.ShapeDtypeStruct((nc, own, w3), BF),
        ),
        grid_spec=pltpu.PrefetchScalarGridSpec(
            num_scalar_prefetch=2,
            grid=(nc, own // tm),
            in_specs=[
                pl.BlockSpec((tm, D), first),
                pl.BlockSpec((1, D), lambda c, m, s, a: (0, 0)),
                pl.BlockSpec((1, D), lambda c, m, s, a: (0, 0)),
                pl.BlockSpec((rr, 1, D // rr, w3), lambda c, m, s, a: (0, c, 0, 0)),
                pl.BlockSpec((1, 1, w3), lambda c, m, s, a: (c, 0, 0)),
                pl.BlockSpec((1, 3 * RANK, D), lambda c, m, s, a: (s[m], 0, 0)),
                pl.BlockSpec((1, 1, 3 * RANK, width), lambda c, m, s, a: (s[m], c, 0, 0)),
            ],
            out_specs=[
                pl.BlockSpec((tm, D), first),
                pl.BlockSpec((tm, 3 * RANK), first),
                pl.BlockSpec((1, tm, w3), lambda c, m, s, a: (c, m, 0)),
            ],
            scratch_shapes=[pltpu.VMEM((own, D), BF), pltpu.VMEM((own, 3 * RANK), BF)],
        ),
        compiler_params=params(2),
        cost_estimate=cost(2 * own * D * nc * w3 * 1.3, D * nc * w3 * 2 + own * (2 * D + nc * w3) * 2),
        name="project",
    )(sets, scales, tokens, gain, shift, gathered, bias, down, up)


def project_back_kernel(
    tm,
    width,
    sets,
    scales,
    dy_ref,
    w_ref,
    up,
    down,
    x_ref,
    normed_ref,
    ranks_ref,
    gm_ref,
    gain,
    gt_ref,
    gup_ref,
    gdown_ref,
    acc,
    racc,
):
    c = pl.program_id(0)
    m = pl.program_id(1)
    last = c == pl.num_programs(0) - 1
    rows = pl.ds(pl.multiple_of(m * tm, tm), tm)
    which = sets[m]
    dy = dy_ref[0]
    part = dot_t(dy, w_ref[:, 0].reshape(D, 3 * width))
    rpart = dot_t(dy, spread(up[0, 0], width))

    @pl.when(c == 0)
    def _():
        acc[rows, :] = part
        racc[rows, :] = rpart

    @pl.when(c > 0)
    def _():
        acc[rows, :] += part
        racc[rows, :] += rpart

    @pl.when(m == 0)
    def _():
        gup_ref[...] = jnp.zeros_like(gup_ref)

    @pl.when((m == 0) & (c == 0))
    def _():
        gdown_ref[...] = jnp.zeros_like(gdown_ref)

    wide = token_sum(ranks_ref[...].astype(F32), dy)
    gup_ref[which, 0] += jnp.concatenate(
        [wide[j * RANK : (j + 1) * RANK, j * width : (j + 1) * width] for j in range(3)], axis=0
    )

    @pl.when(last)
    def _():
        grank = racc[rows, :] * scales[m]
        grad = acc[rows, :] + dot(grank.astype(BF), down[0])
        gdown_ref[which] += token_sum(grank, normed_ref[...])
        unit, inverse = norm_parts(x_ref[...].astype(F32))
        e = grad * gain[...]
        mean = jnp.mean(e, axis=-1, keepdims=True)
        second = jnp.mean(e * unit, axis=-1, keepdims=True)
        gt_ref[...] = (gm_ref[...] + (e - mean - unit * second) * inverse).astype(BF)


def project_back(dy, gathered, up, down, tokens, normed, ranks, grad_middle, gain, sets, scales, tm):
    own = tokens.shape[0]
    rr, nc, _, w3 = gathered.shape
    width = w3 // 3
    final = lambda c, m, s, a: (jnp.where(c == nc - 1, m, 0), 0)
    return pl.pallas_call(
        functools.partial(project_back_kernel, tm, width),
        out_shape=(
            jax.ShapeDtypeStruct((own, D), BF),
            jax.ShapeDtypeStruct((SETS, nc, 3 * RANK, width), F32),
            jax.ShapeDtypeStruct((SETS, 3 * RANK, D), F32),
        ),
        grid_spec=pltpu.PrefetchScalarGridSpec(
            num_scalar_prefetch=2,
            grid=(nc, own // tm),
            in_specs=[
                pl.BlockSpec((1, tm, w3), lambda c, m, s, a: (c, m, 0)),
                pl.BlockSpec((rr, 1, D // rr, w3), lambda c, m, s, a: (0, c, 0, 0)),
                pl.BlockSpec((1, 1, 3 * RANK, width), lambda c, m, s, a: (s[m], c, 0, 0)),
                pl.BlockSpec((1, 3 * RANK, D), lambda c, m, s, a: (s[m], 0, 0)),
                pl.BlockSpec((tm, D), final),
                pl.BlockSpec((tm, D), final),
                pl.BlockSpec((tm, 3 * RANK), lambda c, m, s, a: (m, 0)),
                pl.BlockSpec((tm, D), final),
                pl.BlockSpec((1, D), lambda c, m, s, a: (0, 0)),
            ],
            out_specs=[
                pl.BlockSpec((tm, D), final),
                pl.BlockSpec((SETS, 1, 3 * RANK, width), lambda c, m, s, a: (0, c, 0, 0)),
                pl.BlockSpec((SETS, 3 * RANK, D), lambda c, m, s, a: (0, 0, 0)),
            ],
            scratch_shapes=[pltpu.VMEM((own, D), F32), pltpu.VMEM((own, 3 * RANK), F32)],
        ),
        compiler_params=params(2),
        cost_estimate=cost(2 * own * D * nc * w3 * 1.5, D * nc * w3 * 2 + own * (4 * D + nc * w3) * 2),
        name="project_back",
    )(sets, scales, dy, gathered, up, down, tokens, normed, ranks, grad_middle, gain)


def out_kernel(
    nc,
    sets,
    scales,
    att_ref,
    x_ref,
    w_ref,
    bias,
    odown,
    oup,
    gain,
    shift,
    fdown,
    att_out,
    middle_ref,
    normed_ref,
    ro_ref,
    r1_ref,
):
    m = pl.program_id(0)
    a = scales[m]
    att = jnp.concatenate([att_ref[i] for i in range(nc)], axis=1)
    att_out[...] = att
    ro = (dot_t(att, odown[0]) * a).astype(BF)
    ro_ref[...] = ro
    middle = x_ref[...].astype(F32) + dot_t(att, w_ref[...]) + dot(ro, oup[0]) + bias[...]
    middle_ref[...] = middle
    unit, _ = norm_parts(middle)
    normed = (unit * gain[...] + shift[...]).astype(BF)
    normed_ref[...] = normed
    r1_ref[...] = (dot_t(normed, fdown[0]) * a).astype(BF)


def out_project(att, tokens, wo_t, bias, odown, oup, gain, shift, fdown, sets, scales, tm):
    nc, own, width = att.shape
    row = lambda m, s, a: (m, 0)
    flat = lambda m, s, a: (0, 0)
    table = lambda m, s, a: (s[m], 0, 0)
    return pl.pallas_call(
        functools.partial(out_kernel, nc),
        out_shape=(
            jax.ShapeDtypeStruct((own, D), BF),
            jax.ShapeDtypeStruct((own, D), F32),
            jax.ShapeDtypeStruct((own, D), BF),
            jax.ShapeDtypeStruct((own, RANK), BF),
            jax.ShapeDtypeStruct((own, RANK), BF),
        ),
        grid_spec=pltpu.PrefetchScalarGridSpec(
            num_scalar_prefetch=2,
            grid=(own // tm,),
            in_specs=[
                pl.BlockSpec((nc, tm, width), lambda m, s, a: (0, m, 0)),
                pl.BlockSpec((tm, D), row),
                pl.BlockSpec((D, D), flat),
                pl.BlockSpec((1, D), flat),
                pl.BlockSpec((1, RANK, D), table),
                pl.BlockSpec((1, RANK, D), table),
                pl.BlockSpec((1, D), flat),
                pl.BlockSpec((1, D), flat),
                pl.BlockSpec((1, RANK, D), table),
            ],
            out_specs=[
                pl.BlockSpec((tm, D), row),
                pl.BlockSpec((tm, D), row),
                pl.BlockSpec((tm, D), row),
                pl.BlockSpec((tm, RANK), row),
                pl.BlockSpec((tm, RANK), row),
            ],
        ),
        compiler_params=params(1),
        cost_estimate=cost(2 * own * D * D * 1.5, D * D * 2 + own * D * 12),
        name="out_project",
    )(sets, scales, att, tokens, wo_t, bias, odown, oup, gain, shift, fdown)


def out_back_kernel(nc, width, sets, scales, gb_ref, w_ref, oup, odown, att_ref, ro_ref, ga_ref, gup_ref, gdown_ref):
    m = pl.program_id(0)
    which = sets[m]

    @pl.when(m == 0)
    def _():
        gup_ref[...] = jnp.zeros_like(gup_ref)
        gdown_ref[...] = jnp.zeros_like(gdown_ref)

    gb = gb_ref[...]
    gro = dot_t(gb, oup[0]) * scales[m]
    ga = (dot(gb, w_ref[...]) + dot(gro.astype(BF), odown[0])).astype(BF)
    for i in range(nc):
        ga_ref[i] = ga[:, i * width : (i + 1) * width]
    gup_ref[which] += token_sum(ro_ref[...].astype(F32), gb)
    gdown_ref[which] += token_sum(gro, att_ref[...])


def out_back(gb, wo_t, oup, odown, att, ro, sets, scales, tm, nc):
    own = gb.shape[0]
    width = D // nc
    row = lambda m, s, a: (m, 0)
    table = lambda m, s, a: (s[m], 0, 0)
    whole = lambda m, s, a: (0, 0, 0)
    return pl.pallas_call(
        functools.partial(out_back_kernel, nc, width),
        out_shape=(
            jax.ShapeDtypeStruct((nc, own, width), BF),
            jax.ShapeDtypeStruct((SETS, RANK, D), F32),
            jax.ShapeDtypeStruct((SETS, RANK, D), F32),
        ),
        grid_spec=pltpu.PrefetchScalarGridSpec(
            num_scalar_prefetch=2,
            grid=(own // tm,),
            in_specs=[
                pl.BlockSpec((tm, D), row),
                pl.BlockSpec((D, D), lambda m, s, a: (0, 0)),
                pl.BlockSpec((1, RANK, D), table),
                pl.BlockSpec((1, RANK, D), table),
                pl.BlockSpec((tm, D), row),
                pl.BlockSpec((tm, RANK), row),
            ],
            out_specs=[
                pl.BlockSpec((nc, tm, width), lambda m, s, a: (0, m, 0)),
                pl.BlockSpec((SETS, RANK, D), whole),
                pl.BlockSpec((SETS, RANK, D), whole),
            ],
        ),
        compiler_params=params(1),
        cost_estimate=cost(2 * own * D * D * 1.5, D * D * 2 + own * D * 6),
        name="out_back",
    )(sets, scales, gb, wo_t, oup, odown, att, ro)


def mlp_kernel(
    tm,
    sets,
    scales,
    n_ref,
    g_ref,
    mid_ref,
    w1_ref,
    w2_ref,
    b1,
    f1up,
    f2down,
    f2up,
    f1down,
    r1_ref,
    bias2,
    gain,
    out_ref,
    gm_ref,
    gb_ref,
    gf1up,
    gf2down,
    gf2up,
    gf1down,
    acc,
    gacc,
    r2acc,
    gr1acc,
    gr2,
):
    c = pl.program_id(0)
    m = pl.program_id(1)
    rows = pl.ds(pl.multiple_of(m * tm, tm), tm)
    which = sets[m]
    a = scales[m]
    g = g_ref[...]
    normed = n_ref[...]
    hidden = w1_ref.shape[-1]

    @pl.when(c == 0)
    def _():
        gr2[rows, :] = dot_t(g, f2up[0]) * a
        acc[rows, :] = jnp.zeros((tm, D), F32)
        gacc[rows, :] = jnp.zeros((tm, D), F32)
        r2acc[rows, :] = jnp.zeros((tm, RANK), F32)
        gr1acc[rows, :] = jnp.zeros((tm, RANK), F32)

    @pl.when(m == 0)
    def _():
        gf1up[...] = jnp.zeros_like(gf1up)
        gf2down[...] = jnp.zeros_like(gf2down)

    @pl.when((m == 0) & (c == 0))
    def _():
        gf2up[...] = jnp.zeros_like(gf2up)
        gf1down[...] = jnp.zeros_like(gf1down)

    w1 = w1_ref[:, 0].reshape(D, hidden)
    w2 = w2_ref[:, 0].reshape(D, hidden)
    r1 = r1_ref[...]
    grank2 = gr2[rows, :]
    pre = dot(normed, w1) + dot(r1, f1up[0, 0]) + b1[0]
    phi_up = 0.5 + 0.5 * lax.erf(pre * (0.5**0.5))
    density = jnp.exp(pre * pre * -0.5) * ((2.0 * math.pi) ** -0.5)
    act = (pre * phi_up).astype(BF)
    slope = phi_up + pre * density
    gact = dot(g, w2) + dot(grank2.astype(BF), f2down[0, 0])
    gpre = (gact * slope).astype(BF)
    acc[rows, :] += dot_t(act, w2)
    r2acc[rows, :] += dot_t(act, f2down[0, 0])
    gacc[rows, :] += dot_t(gpre, w1)
    gr1acc[rows, :] += dot_t(gpre, f1up[0, 0])
    gf2down[which, 0] += token_sum(grank2, act)
    gf1up[which, 0] += token_sum(r1.astype(F32), gpre)

    @pl.when(c == pl.num_programs(0) - 1)
    def _():
        r2 = r2acc[rows, :] * a
        middle = mid_ref[...]
        out_ref[...] = (middle + acc[rows, :] + dot(r2.astype(BF), f2up[0]) + bias2[...]).astype(BF)
        gf2up[which] += token_sum(r2, g)
        gr1 = gr1acc[rows, :] * a
        e = (gacc[rows, :] + dot(gr1.astype(BF), f1down[0])) * gain[...]
        gf1down[which] += token_sum(gr1, normed)
        unit, inverse = norm_parts(middle)
        mean = jnp.mean(e, axis=-1, keepdims=True)
        second = jnp.mean(e * unit, axis=-1, keepdims=True)
        gm = g.astype(F32) + (e - mean - unit * second) * inverse
        gm_ref[...] = gm
        gb_ref[...] = gm.astype(BF)


def mlp(normed, g, middle, gathered, b1, f1up, f2down, f2up, f1down, r1, bias2, gain, sets, scales, tm):
    own = g.shape[0]
    rr, nc, _, hidden = gathered.shape
    row = lambda c, m, s, a: (m, 0)
    final = lambda c, m, s, a: (jnp.where(c == nc - 1, m, 0), 0)
    flat = lambda c, m, s, a: (0, 0)
    table = lambda c, m, s, a: (s[m], 0, 0)
    ctable = lambda c, m, s, a: (s[m], c, 0, 0)
    whole = lambda c, m, s, a: (0, 0, 0)
    cwhole = lambda c, m, s, a: (0, c, 0, 0)
    wblock = (rr, 1, D // rr, hidden)
    return pl.pallas_call(
        functools.partial(mlp_kernel, tm),
        out_shape=(
            jax.ShapeDtypeStruct((own, D), BF),
            jax.ShapeDtypeStruct((own, D), F32),
            jax.ShapeDtypeStruct((own, D), BF),
            jax.ShapeDtypeStruct((SETS, nc, RANK, hidden), F32),
            jax.ShapeDtypeStruct((SETS, nc, RANK, hidden), F32),
            jax.ShapeDtypeStruct((SETS, RANK, D), F32),
            jax.ShapeDtypeStruct((SETS, RANK, D), F32),
        ),
        grid_spec=pltpu.PrefetchScalarGridSpec(
            num_scalar_prefetch=2,
            grid=(nc, own // tm),
            in_specs=[
                pl.BlockSpec((tm, D), row),
                pl.BlockSpec((tm, D), row),
                pl.BlockSpec((tm, D), final),
                pl.BlockSpec(wblock, lambda c, m, s, a: (0, c, 0, 0)),
                pl.BlockSpec(wblock, lambda c, m, s, a: (0, c, 1, 0)),
                pl.BlockSpec((1, 1, hidden), lambda c, m, s, a: (c, 0, 0)),
                pl.BlockSpec((1, 1, RANK, hidden), ctable),
                pl.BlockSpec((1, 1, RANK, hidden), ctable),
                pl.BlockSpec((1, RANK, D), table),
                pl.BlockSpec((1, RANK, D), table),
                pl.BlockSpec((tm, RANK), row),
                pl.BlockSpec((1, D), flat),
                pl.BlockSpec((1, D), flat),
            ],
            out_specs=[
                pl.BlockSpec((tm, D), final),
                pl.BlockSpec((tm, D), final),
                pl.BlockSpec((tm, D), final),
                pl.BlockSpec((SETS, 1, RANK, hidden), cwhole),
                pl.BlockSpec((SETS, 1, RANK, hidden), cwhole),
                pl.BlockSpec((SETS, RANK, D), whole),
                pl.BlockSpec((SETS, RANK, D), whole),
            ],
            scratch_shapes=[
                pltpu.VMEM((own, D), F32),
                pltpu.VMEM((own, D), F32),
                pltpu.VMEM((own, RANK), F32),
                pltpu.VMEM((own, RANK), F32),
                pltpu.VMEM((own, RANK), F32),
            ],
        ),
        compiler_params=params(2, 67043328),
        cost_estimate=cost(8 * own * D * nc * hidden * 1.2, D * nc * hidden * 4 + own * D * 30, own * nc * hidden * 2),
        name="mlp",
    )(sets, scales, normed, g, middle, gathered, gathered, b1, f1up, f2down, f2up, f1down, r1, bias2, gain)


def pick(flag, first, second):
    return jnp.where(flag, first, second)


class Exchange:
    def __init__(self, nc, own, clips, clip_len):
        self.nc, self.own, self.clips, self.clip_len = nc, own, clips, clip_len
        self.local = nc == 4 and clips == 3 and 2 * own * 2 == clips * clip_len
        col = lax.axis_index("cols")
        self.y, self.k = col // 2, col % 2
        self.holder = self.y != self.k

    def lens(self, lengths):
        if not self.local:
            return (lengths,)
        mine = pick(self.y == 0, lengths[0], lengths[2])
        return (jnp.stack([mine, mine]), lengths[1:2])

    def to_heads(self, v):
        if not self.local:
            moved = lax.all_to_all(v, "cols", 0, 0, tiled=True)
            return (moved.reshape(self.clips, self.clip_len, v.shape[-1]),)
        y, k, own, half = self.y, self.k, self.own, self.clip_len // 2
        f = v.shape[-1]
        start = pick(k == 1, own - half, 0)
        one = lax.dynamic_slice(v, (2 * k + 1 - y, start, 0), (1, half, f))
        two = lax.dynamic_slice(v, (2 * (1 - k) + 1 - y, start, 0), (1, half, f))
        got_one = lax.ppermute(one, "cols", [(1, 3), (2, 0)])
        got_two = lax.ppermute(two, "cols", [(1, 2), (2, 1)])
        away = lax.dynamic_slice(v, (2 * (1 - k), 0, 0), (2, own, f))
        mine = lax.dynamic_slice(v, (2 * k, 0, 0), (2, own, f))
        got = lax.ppermute(away, "cols", [(i, i ^ 1) for i in range(4)])
        chip = jnp.concatenate([pick(k == 0, mine, got), pick(k == 0, got, mine)], axis=1)
        clip = lax.dynamic_slice(chip, (0, y * half, 0), (2, self.clip_len, f))
        near = lax.dynamic_slice(chip, (y, (1 - y) * self.clip_len, 0), (1, half, f))
        far = pick(self.holder, got_two, got_one)
        shared = jnp.concatenate([pick(y == 0, near, far), pick(y == 0, far, near)], axis=1)
        return (clip, shared)

    def from_heads(self, parts):
        if not self.local:
            (v,) = parts
            return lax.all_to_all(v.reshape(self.nc, self.own, v.shape[-1]), "cols", 0, 0, tiled=True)
        clip, shared = parts
        y, k, own, half = self.y, self.k, self.own, self.clip_len // 2
        f = clip.shape[-1]
        far = lax.dynamic_slice(shared, (0, (1 - y) * half, 0), (1, half, f))
        near = lax.dynamic_slice(shared, (0, y * half, 0), (1, half, f))
        got_one = lax.ppermute(far, "cols", [(3, 1), (0, 2)])
        got_two = lax.ppermute(far, "cols", [(2, 1), (1, 2)])
        both = jnp.concatenate([near, near], axis=0)
        chip = jnp.concatenate(
            [
                pick(y == 0, clip[:, :half], both),
                clip[:, half:] * 0 + pick(y == 0, clip[:, half:], clip[:, :half]),
                pick(y == 0, both, clip[:, half:]),
            ],
            axis=1,
        )
        mine = lax.dynamic_slice(chip, (0, k * own, 0), (2, own, f))
        away = lax.dynamic_slice(chip, (0, (1 - k) * own, 0), (2, own, f))
        got = lax.ppermute(away, "cols", [(i, i ^ 1) for i in range(4)])
        low, high = pick(k == 0, mine, got), pick(k == 0, got, mine)
        out = jnp.concatenate([low, high], axis=0)
        row = lax.broadcasted_iota(jnp.int32, (own, 1), 0)
        inside = self.holder & pick(k == 1, row >= own - half, row < half)
        pad = ((0, 0), (own - half, 0), (0, 0))
        end = ((0, 0), (0, own - half), (0, 0))
        place = lambda v: pick(k == 1, jnp.pad(v, pad), jnp.pad(v, end))[0]
        one, two = place(got_one), place(got_two)
        pieces = []
        for c in range(4):
            from_one = inside & (2 * k + 1 - y == c)
            from_two = inside & (2 * (1 - k) + 1 - y == c)
            pieces.append(pick(from_one, one, pick(from_two, two, out[c])))
        return jnp.stack(pieces)


def pack(pieces, lanes):
    flat = jnp.concatenate([v.astype(BF).reshape(-1, lanes) for v in pieces], axis=0)
    extra = -flat.shape[0] % 16
    return jnp.pad(flat, ((0, extra), (0, 0)))


def scatter_sum(pieces, lanes):
    whole = jnp.concatenate([v.astype(BF) for v in pieces], axis=1).reshape(-1, lanes)
    return lax.psum_scatter(whole, BOTH, scatter_dimension=0, tiled=True).astype(F32).reshape(-1)


def halves(v):
    high = v.astype(BF)
    return high, (v - high.astype(F32)).astype(BF)


def body(
    tokens,
    cotangent,
    clip_lengths,
    clip_sets,
    clip_scales,
    norm1_gain,
    norm1_shift,
    w_query,
    query_bias,
    w_key,
    w_value,
    value_bias,
    w_out,
    out_bias,
    norm2_gain,
    norm2_shift,
    w_fc1,
    fc1_bias,
    w_fc2,
    fc2_bias,
    query_down,
    query_up,
    key_down,
    key_up,
    value_down,
    value_up,
    out_down,
    out_up,
    fc1_down,
    fc1_up,
    fc2_down,
    fc2_up,
):
    nr = lax.axis_size("rows")
    nc = lax.axis_size("cols")
    col = lax.axis_index("cols")
    clips = clip_lengths.shape[0]
    own = tokens.shape[0]
    clip_len = own * nc // clips
    tm = math.gcd(own, clip_len)
    width = query_bias.shape[0]
    hidden = fc1_bias.shape[0]
    hh = width // HEAD_DIM
    dr = w_query.shape[0]
    rk = RANK // nr
    part = SETS * RANK // nc
    exchange = Exchange(nc, own, clips, clip_len)

    block_clip = (col * own + jnp.arange(own // tm, dtype=jnp.int32) * tm) // clip_len
    sets = jnp.take(clip_sets, block_clip)
    scales = jnp.take(clip_scales, block_clip)

    def shared_rows(v):
        return lax.dynamic_slice(v.reshape(SETS * RANK, dr), (col * part, 0), (part, dr))

    def flip(v):
        return jnp.swapaxes(v, 1, 2)

    qh, ql = halves(query_bias)
    vh, vl = halves(value_bias)
    none = jnp.zeros_like(qh)
    pieces = [
        jnp.concatenate([w_query, w_key, w_value], axis=1),
        jnp.stack([shared_rows(flip(v)) for v in (query_down, key_down, value_down)]),
        jnp.stack([query_up, key_up, value_up]),
        jnp.stack([qh, none, vh, ql, none, vl]),
    ]
    g1 = lax.all_gather(pack(pieces, 3 * width), BOTH, axis=0).reshape(nr, nc, -1, 3 * width)
    at = dr
    rows = 3 * part * dr // (3 * width)
    down_qkv = (
        g1[:, :, at : at + rows]
        .reshape(nr, nc, 3, part, dr)
        .transpose(2, 1, 3, 0, 4)
        .reshape(3, SETS, RANK, D)
        .transpose(1, 0, 2, 3)
        .reshape(SETS, 3 * RANK, D)
    )
    at += rows
    rows = SETS * rk
    up_qkv = (
        g1[:, :, at : at + rows]
        .reshape(nr, nc, 3, SETS, rk, width)
        .transpose(3, 1, 2, 0, 4, 5)
        .reshape(SETS, nc, 3 * RANK, width)
    )
    at += rows
    bias_qkv = jnp.sum(g1[0, :, at : at + 2].astype(F32), axis=1, keepdims=True)

    pieces = [
        w_fc1,
        w_fc2.T,
        w_out.T,
        jnp.stack([shared_rows(flip(fc1_down)), shared_rows(out_up), shared_rows(fc2_up)]),
        fc1_up,
        flip(fc2_down),
        flip(out_down),
        jnp.stack(halves(fc1_bias)),
    ]
    packed, _ = lax.optimization_barrier((pack(pieces, hidden), g1))
    g2 = lax.all_gather(packed, BOTH, axis=0).reshape(nr, nc, -1, hidden)
    at = 2 * dr

    def take(rows):
        nonlocal at
        got = g2[:, :, at : at + rows]
        at += rows
        return got

    wo_t = take(dr * width // hidden).reshape(nr, nc, dr, width).transpose(0, 2, 1, 3).reshape(D, D)
    tables = (
        take(3 * part * dr // hidden)
        .reshape(nr, nc, 3, part, dr)
        .transpose(2, 1, 3, 0, 4)
        .reshape(3, SETS, RANK, D)
    )
    f1down, oup, f2up = tables[0], tables[1], tables[2]
    by_hidden = lambda v: v.reshape(nr, nc, SETS, rk, hidden).transpose(2, 1, 0, 3, 4).reshape(SETS, nc, RANK, hidden)
    f1up = by_hidden(take(SETS * rk))
    f2down = by_hidden(take(SETS * rk))
    odown = (
        take(SETS * rk * width // hidden)
        .reshape(nr, nc, SETS, rk, width)
        .transpose(2, 0, 3, 1, 4)
        .reshape(SETS, RANK, D)
    )
    b1 = jnp.sum(take(2)[0].astype(F32), axis=1, keepdims=True)

    gain1, shift1 = norm1_gain[None], norm1_shift[None]
    gain2, shift2 = norm2_gain[None], norm2_shift[None]

    normed, ranks, y = project(tokens, gain1, shift1, g1, bias_qkv, down_qkv, up_qkv, sets, scales, tm)
    heads = exchange.to_heads(y)
    lens = exchange.lens(clip_lengths)
    results = [attend(v, n, hh) for v, n in zip(heads, lens)]
    att = exchange.from_heads([r[0] for r in results])
    att, middle, normed_mlp, ro, r1 = out_project(
        att, tokens, wo_t, out_bias[None], odown, oup, gain2, shift2, f1down, sets, scales, tm
    )
    output, grad_middle, grad_branch, gf1up, gf2down, gf2up, gf1down = mlp(
        normed_mlp, cotangent, middle, g2, b1, f1up, f2down, f2up, f1down, r1, fc2_bias[None], gain2, sets, scales, tm
    )
    ga, goup, godown = out_back(grad_branch, wo_t, oup, odown, att, ro, sets, scales, tm, nc)

    def split_model(v):
        k = v.shape[0]
        return v.reshape(k, nc, part, nr, dr).transpose(3, 1, 0, 2, 4).reshape(nr * nc, -1)

    def join_model(v, k):
        every = lax.all_gather(v.reshape(k, part, dr), "cols", axis=1, tiled=True)
        return every.reshape(k, SETS, RANK, dr)

    by_rank = lambda v: v.reshape(SETS, nc, nr, rk, hidden).transpose(2, 1, 0, 3, 4).reshape(nr * nc, -1)
    late = [
        split_model(jnp.stack([gf1down, goup, gf2up])),
        by_rank(gf1up),
        by_rank(gf2down),
        godown.reshape(SETS, nr, rk, nc, width).transpose(1, 3, 0, 2, 4).reshape(nr * nc, -1),
    ]
    summed = scatter_sum(late, hidden)
    sizes = [3 * part * dr, SETS * rk * hidden, SETS * rk * hidden, SETS * rk * width]
    edges = [sum(sizes[:i]) for i in range(5)]
    cut = [summed[edges[i] : edges[i + 1]] for i in range(4)]
    model = join_model(cut[0], 3)
    grad_fc1_down, grad_out_up, grad_fc2_up = flip(model[0]), model[1], model[2]
    grad_fc1_up = cut[1].reshape(SETS, rk, hidden)
    grad_fc2_down = flip(cut[2].reshape(SETS, rk, hidden))
    grad_out_down = flip(cut[3].reshape(SETS, rk, width))

    grads = exchange.to_heads(ga)
    backs = [
        attend_back(v, r[0], d, r[1], n, hh) for v, r, d, n in zip(heads, results, grads, lens)
    ]
    dy = exchange.from_heads(backs)
    grad_tokens, gup, gdown = project_back(
        dy, g1, up_qkv, down_qkv, tokens, normed, ranks, grad_middle, gain1, sets, scales, tm
    )
    last = [
        split_model(gdown.reshape(SETS, 3, RANK, D).swapaxes(0, 1)),
        gup.reshape(SETS, nc, 3, nr, rk, width).transpose(3, 1, 2, 0, 4, 5).reshape(nr * nc, -1),
    ]
    summed = scatter_sum(last, 3 * width)
    model = join_model(summed[: 3 * part * dr], 3)
    ups = summed[3 * part * dr :].reshape(3, SETS, rk, width)
    return (
        output,
        grad_tokens,
        flip(model[0]),
        ups[0],
        flip(model[1]),
        ups[1],
        flip(model[2]),
        ups[2],
        grad_out_down,
        grad_out_up,
        grad_fc1_down,
        grad_fc1_up,
        grad_fc2_down,
        grad_fc2_up,
    )


def solution(mesh):
    both = P(("rows", "cols"), None)
    grid = P("rows", "cols")
    turned = P("cols", "rows")
    down = P(None, "rows", None)
    up = P(None, "rows", "cols")
    far_down = P(None, "cols", "rows")
    far_up = P(None, None, "rows")
    return jax.shard_map(
        body,
        mesh=mesh,
        in_specs=(
            both,
            both,
            P("rows"),
            P("rows"),
            P("rows"),
            P(),
            P(),
            grid,
            P("cols"),
            grid,
            grid,
            P("cols"),
            turned,
            P(),
            P(),
            P(),
            grid,
            P("cols"),
            turned,
            P(),
            down,
            up,
            down,
            up,
            down,
            up,
            far_down,
            far_up,
            down,
            up,
            far_down,
            far_up,
        ),
        out_specs=(
            both,
            both,
            down,
            up,
            down,
            up,
            down,
            up,
            far_down,
            far_up,
            down,
            up,
            far_down,
            far_up,
        ),
        check_vma=False,
    )
```

time: 3420 us -> 1020 us (0.30)
  matrix products: 851 us -> 0 us
  waiting for transfers between devices: 1100 us -> 299 us
  blocking collectives: 624 us -> 12.9 us
  Pallas kernels: 0 us -> 332 us
  local copies, waits for them, and re-layouts: 518 us -> 232 us
  other arithmetic: 249 us -> 89.1 us
    dot_general x147 -> x0, matrix products: 851 us -> none  [the longest x24 214 us: paired_contraction(): jnp.einsum(form, lower_part, narrow_side, preferred_element_type=jnp.floa...]
    reduce_scatter x10 -> x2, waiting for transfers between devices: 958 us -> 172 us  [scatter_sum(): lax.psum_scatter(whole, BOTH, scatter_dimension=0, tiled=True).astype(F32)]
    all_gather x16 -> x2, blocking collectives: 624 us -> 12.9 us  [join_model(): every = lax.all_gather(v.reshape(k, part, dr), 'cols', axis=1, tiled=True)]
    pallas_call x0 -> x9, Pallas kernels: none -> 332 us  [the longest x1 97.4 us: mlp(): pl.pallas_call(functools.partial(mlp_kernel, tm), out_shape=(jax.ShapeDty...]
    dynamic_update_slice x51 -> x0, local copies, waits for them, and re-layouts: 261 us -> none  [the longest x36 242 us: attend_clip(): results, logsum = lax.map(one_block, jnp.arange(block_count))]
    unnamed x242 -> x80, local copies, waits for them, and re-layouts: 145 us -> 3.78 us
    convert_element_type x14 -> x8, other arithmetic: 132 us -> 8.2 us  [the longest x5 5.89 us: scatter_sum(): v.astype(BF)]
    reduce_sum x15 -> x2, other arithmetic: 80.9 us -> 1.83 us  [the longest x1 0.95 us: body(): b1 = jnp.sum(take(2)[0].astype(F32), axis=1, keepdims=True)]
  transfers between devices with their start and end apart: 23 -> 16, of which waited for: 13 -> 5; matrix products, arithmetic and copies ran while one was open for 32% -> 21% of each run, Pallas kernels for 0% -> 19%
where the time goes in v1:
time: 1020 us; the launch traced here: 1000 us
  Pallas kernels  332 us (33%)
  waiting for transfers between devices  299 us (29%)
  local copies, waits for them, and re-layouts  232 us (23%)
  other arithmetic  89.1 us (9%)
  starting transfers between devices  23 us (2%)
  between operations  16.7 us (2%)
  blocking collectives  12.9 us (1%)
    reduce_scatter x2, waiting for transfers between devices, scatter_sum(): lax.psum_scatter(whole, BOTH, scatter_dimension=0, tiled=True).astype(F32)  172 us
    pallas_call x1, Pallas kernels, mlp(): pl.pallas_call(functools.partial(mlp_kernel, tm), out_shape=(jax.ShapeDty...  97.4 us
    all_gather x1, waiting for transfers between devices, body(): lax.all_gather(pack(pieces, 3 * width), BOTH, axis=0)  96.8 us
    pallas_call x2, Pallas kernels, attend_back(): pl.pallas_call(functools.partial(attend_back_kernel, hh, length, qb, kb),...  86.2 us
    pallas_call x2, Pallas kernels, attend(): pl.pallas_call(functools.partial(attend_kernel, hh, length, qb, kb), out_...  59.5 us
    select_n x12, other arithmetic, pick(): return jnp.where(flag, first, second)  40.7 us
    pallas_call x1, Pallas kernels, project_back(): pl.pallas_call(functools.partial(project_back_kernel, tm, width), out_sha...  35.5 us
    ppermute x2, waiting for transfers between devices, to_heads(): got_one = lax.ppermute(one, 'cols', [(1, 3), (2, 0)])  29 us
  transfers between devices with their start and end apart: 16, of which 5 were waited for; matrix products, arithmetic and copies ran while one was open for 21% of the time, Pallas kernels for 19%

profile of v1, /device:TPU:0, one launch (start us, length us, event | category | flops | bytes accessed | tf_op | source)
XLA Modules:
  0.0 1004.4 jit_solution(14002780515467902630)
XLA Ops:
  19.5 96.8 %all-gather.5.cloned.1.call-done = bf16[6656,960]{1,0:T(8,128)(2,1)} async-done(((bf16[208,960]{1,0:T(8,128)(2,1)}), bf16[6656,960]{1,0:T(8,128)(2,1)}) %all-gather.5.cloned.1.call-update) | async-done | bytes 12779536 | tf_op jit(solution)/shard_map/all_gather | solution.py:854
  132.6 25.6 %project.1 = (bf16[1152,1280]{1,0:T(8,128)(2,1)}, bf16[1152,48]{1,0:T(8,128)(2,1)}, bf16[4,1152,960]{2,1,0:T(8,128)(2,1)}) custom-call(s32[3]{0:T(128)} %broadcast_select_fusion.19.sets, f32[3]{0:T(128)} %broadcast_select_fusion.18.scales, bf16[1152,1280]{1,0:T(8,128)(2,1)} %x_ref.5, f32[1,1280]{1,0:T(1,128)} %broadcast_in_dim.115.gain, ...), custom_call_target="tpu_custom_call" | custom-call | flops 14722007040 | bytes 24576000 | tf_op jit(solution)/shard_map/project/pallas_call | solution.py:273
  163.8 6.7 copy.92
  182.7 29.0 %collective-permute-done.2 = bf16[1,768,960]{1,2,0:T(8,128)(2,1)S(1)} collective-permute-done((bf16[1,768,960]{1,2,0:T(8,128)(2,1)}, bf16[1,768,960]{1,2,0:T(8,128)(2,1)S(1)}, u32[]{:S(2)}, u32[]{:S(2)}) %collective-permute-start.2) | collective-permute-done | bytes 1474592 | tf_op jit(solution)/shard_map/ppermute | solution.py:719
  213.3 7.2 copy.93
  232.6 15.5 %attend.2 = (bf16[1,1536,320]{2,1,0:T(8,128)(2,1)}, f32[1,4,1536]{2,1,0:T(4,128)}) custom-call(s32[1]{0:T(128)} %get-tuple-element.127.lens, bf16[1,1536,960]{2,1,0:T(8,128)(2,1)} %pad_maximum_fusion.5.x_ref), custom_call_target="tpu_custom_call" | custom-call | flops 9663676416 | bytes 4423680 | tf_op jit(solution)/shard_map/attend/pallas_call | solution.py:110
  250.4 9.1 fusion.x_ref
  259.5 44.0 %attend.3 = (bf16[2,1536,320]{2,1,0:T(8,128)(2,1)}, f32[2,4,1536]{2,1,0:T(4,128)}) custom-call(s32[2]{0:T(128)} %pad_add_fusion.lens, bf16[2,1536,960]{2,1,0:T(8,128)(2,1)} %fusion.x_ref), custom_call_target="tpu_custom_call" | custom-call | flops 19327352832 | bytes 8847360 | tf_op jit(solution)/shard_map/attend/pallas_call | solution.py:110
  410.2 6.1 copy.151
  416.2 7.6 reshape.433.w_ref
  423.8 13.8 %out_project.1 = (bf16[1152,1280]{1,0:T(8,128)(2,1)}, f32[1152,1280]{1,0:T(8,128)}, bf16[1152,1280]{1,0:T(8,128)(2,1)}, bf16[1152,16]{1,0:T(8,128)(2,1)}, bf16[1152,16]{1,0:T(8,128)(2,1)}) custom-call(s32[3]{0:T(128)} %broadcast_select_fusion.19.sets, f32[3]{0:T(128)} %broadcast_select_fusion.18.scales, bf16[4,1152,320]{2,1,0:T(8,128)(2,1)} %pad_maximum_fusion.4.att_ref, ...), custom_call_target="tpu_custom_call" | custom-call | flops 5662310400 | bytes 20971520 | tf_op jit(solution)/shard_map/out_project/pallas_call | solution.py:446
  437.7 97.4 %mlp.1 = (bf16[1152,1280]{1,0:T(8,128)(2,1)}, f32[1152,1280]{1,0:T(8,128)}, bf16[1152,1280]{1,0:T(8,128)(2,1)}, f32[8,4,16,1280]{3,2,1,0:T(8,128)}, f32[8,4,16,1...) custom-call(s32[3]{0:T(128)} %broadcast_select_fusion.19.sets, f32[3]{0:T(128)} %broadcast_select_fusion.18.scales, ...), custom_call_target="tpu_custom_call" | custom-call | flops 72477573120 | bytes 70451200 | tf_op jit(solution)/shard_map/mlp/pallas_call | solution.py:640
  535.1 13.9 %out_back.1 = (bf16[4,1152,320]{2,1,0:T(8,128)(2,1)}, f32[8,16,1280]{2,1,0:T(8,128)}, f32[8,16,1280]{2,1,0:T(8,128)}) custom-call(s32[3]{0:T(128)} %broadcast_select_fusion.19.sets, f32[3]{0:T(128)} %broadcast_select_fusion.18.scales, bf16[1152,1280]{1,0:T(8,128)(2,1)} %get-tuple-element.48.gb_ref, bf16[1280,1280]{1,0:T(8,128)(2,1)} %reshape.433.w_ref, ...), custom_call_target="tpu_custom_call" | custom-call | flops 5662310400 | bytes 12124160 | tf_op jit(solution)/shard_map/out_back/pallas_call | solution.py:507
  591.4 19.7 %attend_back.2 = bf16[1,1536,960]{2,1,0:T(8,128)(2,1)} custom-call(s32[1]{0:T(128)} %get-tuple-element.127.lens, bf16[1,1536,960]{2,1,0:T(8,128)(2,1)} %pad_maximum_fusion.5.x_ref, bf16[1,1536,320]{2,1,0:T(8,128)(2,1)} %get-tuple-element.41.o_ref, bf16[1,1536,320]{2,1,0:T(8,128)(2,1)} %pad_maximum_fusion.9.do_ref, f32[1,4,1536]{2,1,0:T(4,128)} %get-tuple-element.52.lse_ref), custom_call_target="tpu_custom_call" | custom-call | flops 24159191040 | bytes 8847360 | tf_op jit(solution)/shard_map/attend_back/pallas_call | solution.py:211
  616.8 8.0 collective-permute-start.9
  624.8 66.5 %attend_back.3 = bf16[2,1536,960]{2,1,0:T(8,128)(2,1)} custom-call(s32[2]{0:T(128)} %pad_add_fusion.lens, bf16[2,1536,960]{2,1,0:T(8,128)(2,1)} %fusion.x_ref, bf16[2,1536,320]{2,1,0:T(8,128)(2,1)} %get-tuple-element.42.o_ref, bf16[2,1536,320]{2,1,0:T(8,128)(2,1)} %fusion.1.do_ref, f32[2,4,1536]{2,1,0:T(4,128)} %get-tuple-element.53.lse_ref), custom_call_target="tpu_custom_call" | custom-call | flops 48318382080 | bytes 17694720 | tf_op jit(solution)/shard_map/attend_back/pallas_call | solution.py:211
  703.7 6.8 copy.128
  724.4 6.6 copy.129
  731.0 6.5 broadcast_select_fusion.1
  751.5 35.5 %project_back.1 = (bf16[1152,1280]{1,0:T(8,128)(2,1)}, f32[8,4,48,320]{3,2,1,0:T(8,128)}, f32[8,48,1280]{2,1,0:T(8,128)}) custom-call(s32[3]{0:T(128)} %broadcast_select_fusion.19.sets, f32[3]{0:T(128)} %broadcast_select_fusion.18.scales, bf16[4,1152,960]{2,1,0:T(8,128)(2,1)} %pad_maximum_fusion.1.dy_ref, bf16[8,4,208,960]{3,2,1,0:T(8,128)(2,1)} %bitcast.160, ...), custom_call_target="tpu_custom_call" | custom-call | flops 16986931200 | bytes 30474240 | tf_op jit(solution)/shard_map/project_back/pallas_call | solution.py:374
  804.8 44.6 %reduce-scatter.5.cloned.1.call-done = bf16[48,1280]{1,0:T(8,128)(2,1)} async-done(((bf16[1536,1280]{1,0:T(8,128)(2,1)}), bf16[48,1280]{1,0:T(8,128)(2,1)}) %reduce-scatter.5.cloned.1.call-update) | async-done | bytes 122896 | tf_op jit(solution)/shard_map/reduce_scatter | solution.py:778
  854.1 6.7 all_gather.23
  861.5 127.4 %reduce-scatter.3.cloned.1.call-done = bf16[32,960]{1,0:T(8,128)(2,1)} async-done(((bf16[1024,960]{1,0:T(8,128)(2,1)}), bf16[32,960]{1,0:T(8,128)(2,1)}) %reduce-scatter.3.cloned.1.call-update) | async-done | bytes 61456 | tf_op jit(solution)/shard_map/reduce_scatter | solution.py:778
  990.5 6.1 all_gather.22
  (284 shorter events, 280.6 us)
Async XLA Ops:
  7.2 109.0 %all-gather.5.cloned.1.call-start = ((), (), s32[]{:S(2)}) async-start(), calls=%async_computation.4 | async-start | bytes 14057472 | tf_op jit(solution)/shard_map/all_gather | solution.py:854
  13.4 330.4 %all-gather.7.cloned.1.call-start = ((), (), s32[]{:S(2)}) async-start(), calls=%async_computation.5 | async-start | bytes 35143680 | tf_op jit(solution)/shard_map/all_gather | solution.py:887
  17.7 98.7 %copy-start = (f32[3]{0:T(128)S(1)}, f32[3]{0:T(128)}, u32[]{:S(2)}) copy-start(f32[3]{0:T(128)} %param.36) | copy-start | bytes 40
  18.4 98.6 %copy-start.1 = (s32[3]{0:T(128)S(1)}, s32[3]{0:T(128)}, u32[]{:S(2)}) copy-start(s32[3]{0:T(128)} %param.35) | copy-start | bytes 40
  18.4 99.3 %copy-start.35 = (f32[1280]{0:T(1024)S(1)}, f32[1280]{0:T(1024)}, u32[]{:S(2)}) copy-start(f32[1280]{0:T(1024)} %param.37) | copy-start | bytes 15364
  18.4 99.9 %copy-start.36 = (f32[1280]{0:T(1024)S(1)}, f32[1280]{0:T(1024)}, u32[]{:S(2)}) copy-start(f32[1280]{0:T(1024)} %param.38) | copy-start | bytes 15364
  116.3 733.2 %reduce-scatter.5.cloned.1.call-start = ((), (), s32[]{:S(2)}) async-start(), calls=%async_computation.3 | async-start | bytes 4055040 | tf_op jit(solution)/shard_map/reduce_scatter | solution.py:778
  170.5 42.8 %collective-permute-start = (bf16[2,1152,960]{1,2,0:T(8,128)(2,1)}, bf16[2,1152,960]{1,2,0:T(8,128)(2,1)}, u32[]{:S(2)}, u32[]{:S(2)}) collective-permute-start(bf16[2,1152,960]{1,2,0:T(8,128)(2,1)} %copy.92), channel_id=1, source_target_pairs={{0,1},{1,0},{2,3},{3,2},{4,5},{5,4},{6,7},{7,6},{8,9},{9,8},{10,11... | collective-permute-start | bytes 13271048 | tf_op jit(solution)/shard_map/ppermute | solution.py:723
  174.6 6.5 collective-permute-start.1
  176.9 34.7 %collective-permute-start.2 = (bf16[1,768,960]{1,2,0:T(8,128)(2,1)}, bf16[1,768,960]{1,2,0:T(8,128)(2,1)S(1)}, u32[]{:S(2)}, u32[]{:S(2)}) collective-permute-start(bf16[1,768,960]{1,2,0:T(8,128)(2,1)} %copy.96), channel_id=1, source_target_pairs={{1,3},{2,0},{5,7},{6,4},{9,11},{10,8},{13,15},{14,12},{17,19},{18,... | collective-permute-start | bytes 4423688 | tf_op jit(solution)/shard_map/ppermute | solution.py:719
  311.4 19.6 %collective-permute-start.5 = (bf16[2,1152,320]{1,2,0:T(8,128)(2,1)}, bf16[2,1152,320]{1,2,0:T(8,128)(2,1)}, u32[]{:S(2)}, u32[]{:S(2)}) collective-permute-start(bf16[2,1152,320]{1,2,0:T(8,128)(2,1)} %copy.105), channel_id=1, source_target_pairs={{0,1},{1,0},{2,3},{3,2},{4,5},{5,4},{6,7},{7,6},{8,9},{9,8},{10,11... | collective-permute-start | bytes 4423688 | tf_op jit(solution)/shard_map/ppermute | solution.py:753
  313.7 11.6 %collective-permute-start.4 = (bf16[1,768,320]{1,2,0:T(8,128)(2,1)}, bf16[1,768,320]{1,2,0:T(8,128)(2,1)}, u32[]{:S(2)}, u32[]{:S(2)}) collective-permute-start(bf16[1,768,320]{1,2,0:T(8,128)(2,1)} %copy.99), channel_id=1, source_target_pairs={{2,1},{1,2},{6,5},{5,6},{10,9},{9,10},{14,13},{13,14},{18,17},{17,... | collective-permute-start | bytes 1474568 | tf_op jit(solution)/shard_map/ppermute | solution.py:741
  315.2 13.8 %collective-permute-start.3 = (bf16[1,768,320]{1,2,0:T(8,128)(2,1)}, bf16[1,768,320]{1,2,0:T(8,128)(2,1)}, u32[]{:S(2)}, u32[]{:S(2)}) collective-permute-start(bf16[1,768,320]{1,2,0:T(8,128)(2,1)} %copy.99), channel_id=1, source_target_pairs={{3,1},{0,2},{7,5},{4,6},{11,9},{8,10},{15,13},{12,14},{19,17},{16,... | collective-permute-start | bytes 1474568 | tf_op jit(solution)/shard_map/ppermute | solution.py:740
  324.1 15.1 %copy-start.19 = (pred[1152]{0:T(1024)(128)(4,1)}, pred[1152]{0:T(1024)(128)(4,1)S(1)}, u32[]{:S(2)}) copy-start(pred[1152]{0:T(1024)(128)(4,1)S(1)} %get-tuple-element.135) | copy-start | bytes 3460
  324.1 15.2 %copy-start.21 = (pred[1152]{0:T(1024)(128)(4,1)}, pred[1152]{0:T(1024)(128)(4,1)S(1)}, u32[]{:S(2)}) copy-start(pred[1152]{0:T(1024)(128)(4,1)S(1)} %get-tuple-element.136) | copy-start | bytes 3460
  324.1 15.1 %copy-start.23 = (pred[1152]{0:T(1024)(128)(4,1)}, pred[1152]{0:T(1024)(128)(4,1)S(1)}, u32[]{:S(2)}) copy-start(pred[1152]{0:T(1024)(128)(4,1)S(1)} %get-tuple-element.137) | copy-start | bytes 3460
  324.1 15.1 %copy-start.25 = (pred[1152]{0:T(1024)(128)(4,1)}, pred[1152]{0:T(1024)(128)(4,1)S(1)}, u32[]{:S(2)}) copy-start(pred[1152]{0:T(1024)(128)(4,1)S(1)} %get-tuple-element.138) | copy-start | bytes 3460
  552.9 27.8 %collective-permute-start.6 = (bf16[2,1152,320]{1,2,0:T(8,128)(2,1)}, bf16[2,1152,320]{1,2,0:T(8,128)(2,1)}, u32[]{:S(2)}, u32[]{:S(2)}) collective-permute-start(bf16[2,1152,320]{1,2,0:T(8,128)(2,1)} %copy.115), channel_id=1, source_target_pairs={{0,1},{1,0},{2,3},{3,2},{4,5},{5,4},{6,7},{7,6},{8,9},{9,8},{10,11... | collective-permute-start | bytes 4423688 | tf_op jit(solution)/shard_map/ppermute | solution.py:723
  556.2 21.9 %collective-permute-start.7 = (bf16[1,768,320]{1,2,0:T(8,128)(2,1)}, bf16[1,768,320]{1,2,0:T(8,128)(2,1)}, u32[]{:S(2)}, u32[]{:S(2)}) collective-permute-start(bf16[1,768,320]{1,2,0:T(8,128)(2,1)} %copy.118), channel_id=1, source_target_pairs={{1,2},{2,1},{5,6},{6,5},{9,10},{10,9},{13,14},{14,13},{17,18},{18,... | collective-permute-start | bytes 1474568 | tf_op jit(solution)/shard_map/ppermute | solution.py:720
  558.6 20.7 %collective-permute-start.8 = (bf16[1,768,320]{1,2,0:T(8,128)(2,1)}, bf16[1,768,320]{1,2,0:T(8,128)(2,1)}, u32[]{:S(2)}, u32[]{:S(2)}) collective-permute-start(bf16[1,768,320]{1,2,0:T(8,128)(2,1)} %copy.119), channel_id=1, source_target_pairs={{1,3},{2,0},{5,7},{6,4},{9,11},{10,8},{13,15},{14,12},{17,19},{18,... | collective-permute-start | bytes 1474568 | tf_op jit(solution)/shard_map/ppermute | solution.py:719
  615.0 104.1 %collective-permute-start.10 = (bf16[1,768,960]{1,2,0:T(8,128)(2,1)}, bf16[1,768,960]{1,2,0:T(8,128)(2,1)}, u32[]{:S(2)}, u32[]{:S(2)}) collective-permute-start(bf16[1,768,960]{1,2,0:T(8,128)(2,1)} %copy.122), channel_id=1, source_target_pairs={{2,1},{1,2},{6,5},{5,6},{10,9},{9,10},{14,13},{13,14},{18,17},{17,... | collective-permute-start | bytes 4423688 | tf_op jit(solution)/shard_map/ppermute | solution.py:741
  616.8 105.0 %collective-permute-start.9 = (bf16[1,768,960]{1,2,0:T(8,128)(2,1)}, bf16[1,768,960]{1,2,0:T(8,128)(2,1)}, u32[]{:S(2)}, u32[]{:S(2)}) collective-permute-start(bf16[1,768,960]{1,2,0:T(8,128)(2,1)} %copy.122), channel_id=1, source_target_pairs={{3,1},{0,2},{7,5},{4,6},{11,9},{8,10},{15,13},{12,14},{19,17},{16,... | collective-permute-start | bytes 4423688 | tf_op jit(solution)/shard_map/ppermute | solution.py:740
  710.6 13.9 %collective-permute-start.11 = (bf16[2,1152,960]{1,2,0:T(8,128)(2,1)}, bf16[2,1152,960]{1,2,0:T(8,128)(2,1)}, u32[]{:S(2)}, u32[]{:S(2)}) collective-permute-start(bf16[2,1152,960]{1,2,0:T(8,128)(2,1)} %copy.128), channel_id=1, source_target_pairs={{0,1},{1,0},{2,3},{3,2},{4,5},{5,4},{6,7},{7,6},{8,9},{9,8},{10,11... | collective-permute-start | bytes 13271048 | tf_op jit(solution)/shard_map/ppermute | solution.py:753
  719.0 269.9 %reduce-scatter.3.cloned.1.call-start = ((), (), s32[]{:S(2)}) async-start(), calls=%async_computation.2 | async-start | bytes 2162688 | tf_op jit(solution)/shard_map/reduce_scatter | solution.py:778
  (32 other events, 183.9 us)
Sparse Core Ops, SparseCore 0:
  13.5 102.6 all-gather.4
  119.1 196.8 all-gather.6
  719.1 130.2 reduce-scatter.4
  851.5 137.3 reduce-scatter.2

commit v2 on v1

v2 whole, which is shorter than its diff:
```python
import functools
import math

import jax
import jax.numpy as jnp
from jax import lax
from jax.experimental import pallas as pl
from jax.experimental.pallas import tpu as pltpu
from jax.sharding import PartitionSpec as P


D = 1280
SETS = 8
RANK = 16
HEAD_DIM = 80
EPSILON = 1e-05
LOG2E = 1.4426950408889634
LOW = -1e30
F32 = jnp.float32
BF = jnp.bfloat16
BOTH = ("rows", "cols")


def dot(a, b):
    return lax.dot_general(a, b, (((1,), (0,)), ((), ())), preferred_element_type=F32)


def dot_t(a, b):
    return lax.dot_general(a, b, (((1,), (1,)), ((), ())), preferred_element_type=F32)


def token_sum(a, b):
    return dot(a.T.astype(BF), b)


def norm_parts(x):
    mean = jnp.mean(x, axis=-1, keepdims=True)
    centred = x - mean
    inverse = lax.rsqrt(jnp.mean(centred * centred, axis=-1, keepdims=True) + EPSILON)
    return centred * inverse, inverse


def params(n, limit=60 << 20):
    return pltpu.CompilerParams(
        dimension_semantics=("arbitrary",) * n, vmem_limit_bytes=limit
    )


def cost(flops, nbytes, trans=0):
    return pl.CostEstimate(flops=int(flops), bytes_accessed=int(nbytes), transcendentals=int(trans))


def set_mask(shape, which, group, per):
    column = lax.broadcasted_iota(jnp.int32, shape, len(shape) - 1)
    return (column % group) // per == which


def choose(code, refs, dst, at):
    for j, ref in enumerate(refs):

        @pl.when(code == j)
        def _(ref=ref):
            dst[at] = ref[0, :, 0 : dst.shape[-1]]


def gather_clip(refs, plan, dst, bs):
    blocks = plan.shape[0] // 2
    for b in range(blocks):
        rows = slice(b * bs, (b + 1) * bs)
        for j, ref in enumerate(refs):

            @pl.when(plan[b] == j)
            def _(ref=ref, b=b, rows=rows):
                off = pl.multiple_of(plan[blocks + b] * bs, bs)
                dst[0, rows, :] = ref[0, pl.ds(off, bs), 0 : dst.shape[2]]


def attend_kernel(hh, length, qb, kb, ns, lens, plan, index, *refs):
    sources, (o_ref, lse_ref, x_ref, k_scr, vt_scr, acc, m_scr, l_scr) = refs[:ns], refs[ns:]
    p = pl.program_id(0)
    qi = pl.program_id(1)
    w = hh * HEAD_DIM
    c = HEAD_DIM**-0.5 * LOG2E

    @pl.when(qi == 0)
    def _():
        gather_clip(sources, plan, x_ref, 2 * length // plan.shape[0])
        vt_scr[...] = x_ref[0, :, 2 * w : 3 * w].T
        for h in range(hh):
            k_scr[h] = x_ref[0, :, w + h * HEAD_DIM : w + (h + 1) * HEAD_DIM]

    size = lens[p]
    block = x_ref[0, pl.ds(pl.multiple_of(qi * qb, qb), qb), 0:w]
    qs = [block[:, h * HEAD_DIM : (h + 1) * HEAD_DIM] for h in range(hh)]
    m_scr[...] = jnp.full_like(m_scr, LOW)
    l_scr[...] = jnp.zeros_like(l_scr)
    acc[...] = jnp.zeros_like(acc)

    def chunk(i, masked):
        r0 = pl.multiple_of(i * kb, kb)
        for h in range(hh):
            s = dot_t(k_scr[h, pl.ds(r0, kb), :], qs[h])
            if masked:
                keys = lax.broadcasted_iota(jnp.int32, (kb, qb), 0) + i * kb
                s = jnp.where(keys < size, s, LOW)
            old = m_scr[h : h + 1]
            top = jnp.maximum(old, jnp.max(s, axis=0, keepdims=True))
            probs = jnp.exp2((s - top) * c)
            shrink = jnp.exp2((old - top) * c)
            l_scr[h : h + 1] = l_scr[h : h + 1] * shrink + jnp.sum(probs, axis=0, keepdims=True)
            m_scr[h : h + 1] = top
            acc[h] = acc[h] * shrink + dot(
                vt_scr[h * HEAD_DIM : (h + 1) * HEAD_DIM, pl.ds(r0, kb)], probs.astype(BF)
            )

    full = size // kb

    def step(i, carry):
        chunk(i, False)
        return carry

    lax.fori_loop(0, full, step, 0)

    @pl.when(full * kb < size)
    def _():
        chunk(full, True)

    outs = [acc[h] * (1.0 / l_scr[h : h + 1]) for h in range(hh)]
    o_ref[0, :, 0:w] = jnp.concatenate(outs, axis=0).T.astype(BF)
    lse_ref[0] = m_scr[0:hh] * c + jnp.log2(l_scr[0:hh])


def lanes_of(n):
    return -(-n // 128) * 128


def source_specs(sources, problems):
    def spec(j, v):
        return pl.BlockSpec(
            (1,) + v.shape[1:], lambda p, q, l, plan, index: (index[j * problems + p], 0, 0)
        )

    return [spec(j, v) for j, v in enumerate(sources)]


def attend(sources, plan, index, lens, length, hh):
    problems = lens.shape[0]
    w3 = 3 * hh * HEAD_DIM
    w = hh * HEAD_DIM
    qb = math.gcd(length, 512)
    kb = math.gcd(length, 768)
    return pl.pallas_call(
        functools.partial(attend_kernel, hh, length, qb, kb, len(sources)),
        out_shape=(
            jax.ShapeDtypeStruct((problems, length, lanes_of(w)), BF),
            jax.ShapeDtypeStruct((problems, hh, length), F32),
            jax.ShapeDtypeStruct((problems, length, w3), BF),
        ),
        grid_spec=pltpu.PrefetchScalarGridSpec(
            num_scalar_prefetch=3,
            grid=(problems, length // qb),
            in_specs=source_specs(sources, problems),
            out_specs=[
                pl.BlockSpec((1, qb, lanes_of(w)), lambda p, q, *_: (p, q, 0)),
                pl.BlockSpec((1, hh, qb), lambda p, q, *_: (p, 0, q)),
                pl.BlockSpec((1, length, w3), lambda p, q, *_: (p, 0, 0)),
            ],
            scratch_shapes=[
                pltpu.VMEM((hh, length, HEAD_DIM), BF),
                pltpu.VMEM((w, length), BF),
                pltpu.VMEM((hh, HEAD_DIM, qb), F32),
                pltpu.VMEM((max(8, hh), qb), F32),
                pltpu.VMEM((max(8, hh), qb), F32),
            ],
        ),
        compiler_params=params(2),
        cost_estimate=cost(
            problems * hh * 4 * length * length * 256,
            problems * length * w3 * 6,
            problems * hh * length * length,
        ),
        name="attend",
    )(lens, plan, index, *sources)


def attend_back_kernel(hh, length, qb, kb, ns, lens, plan, index, *refs):
    sources = refs[:ns]
    x_ref, o_ref, lse_ref, dx_ref, do_scr, k_scr, v_scr, kt_scr, dk, dv, dqt = refs[ns:]
    p = pl.program_id(0)
    qi = pl.program_id(1)
    w = hh * HEAD_DIM
    scale = HEAD_DIM**-0.5
    c = scale * LOG2E

    @pl.when(qi == 0)
    def _():
        gather_clip(sources, plan, do_scr, 2 * length // plan.shape[0])
        kt_scr[...] = x_ref[0, :, w : 2 * w].T
        for h in range(hh):
            k_scr[h] = x_ref[0, :, w + h * HEAD_DIM : w + (h + 1) * HEAD_DIM]
            v_scr[h] = x_ref[0, :, 2 * w + h * HEAD_DIM : 2 * w + (h + 1) * HEAD_DIM]
        dk[...] = jnp.zeros_like(dk)
        dv[...] = jnp.zeros_like(dv)

    size = lens[p]
    rows = pl.ds(pl.multiple_of(qi * qb, qb), qb)
    block = x_ref[0, rows, 0:w]
    qs = [block[:, h * HEAD_DIM : (h + 1) * HEAD_DIM] for h in range(hh)]
    do = do_scr[0, rows, :]
    dos = [do[:, h * HEAD_DIM : (h + 1) * HEAD_DIM] for h in range(hh)]
    prod = (do.astype(F32) * o_ref[0, :, 0:w].astype(F32)).T
    inner = [
        jnp.sum(prod[h * HEAD_DIM : (h + 1) * HEAD_DIM], axis=0, keepdims=True) for h in range(hh)
    ]
    dqt[...] = jnp.zeros_like(dqt)

    def chunk(i, masked):
        keys_at = pl.ds(pl.multiple_of(i * kb, kb), kb)
        for h in range(hh):
            s = dot_t(k_scr[h, keys_at, :], qs[h])
            probs = jnp.exp2(s * c - lse_ref[0, h : h + 1])
            if masked:
                keys = lax.broadcasted_iota(jnp.int32, (kb, qb), 0) + i * kb
                probs = jnp.where(keys < size, probs, 0.0)
            dp = dot_t(v_scr[h, keys_at, :], dos[h])
            ds = (probs * (dp - inner[h])).astype(BF)
            dv[h, keys_at, :] += dot(probs.astype(BF), dos[h])
            dk[h, keys_at, :] += dot(ds, qs[h])
            dqt[h] += dot(kt_scr[h * HEAD_DIM : (h + 1) * HEAD_DIM, keys_at], ds)

    full = size // kb

    def step(i, carry):
        chunk(i, False)
        return carry

    lax.fori_loop(0, full, step, 0)

    @pl.when(full * kb < size)
    def _():
        chunk(full, True)

    dq = jnp.concatenate([dqt[h] for h in range(hh)], axis=0).T * scale
    dx_ref[0, rows, 0:w] = dq.astype(BF)

    @pl.when(qi == pl.num_programs(1) - 1)
    def _():
        for h in range(hh):
            dx_ref[0, :, w + h * HEAD_DIM : w + (h + 1) * HEAD_DIM] = (dk[h] * scale).astype(BF)
            dx_ref[0, :, 2 * w + h * HEAD_DIM : 2 * w + (h + 1) * HEAD_DIM] = dv[h].astype(BF)


def attend_back(sources, plan, index, x, o, lse, lens, hh):
    problems, length, w3 = x.shape
    w = hh * HEAD_DIM
    qb = math.gcd(length, 512)
    kb = math.gcd(length, 512)
    return pl.pallas_call(
        functools.partial(attend_back_kernel, hh, length, qb, kb, len(sources)),
        out_shape=jax.ShapeDtypeStruct((problems, length, lanes_of(w3)), BF),
        grid_spec=pltpu.PrefetchScalarGridSpec(
            num_scalar_prefetch=3,
            grid=(problems, length // qb),
            in_specs=source_specs(sources, problems)
            + [
                pl.BlockSpec((1, length, w3), lambda p, q, *_: (p, 0, 0)),
                pl.BlockSpec((1, qb, lanes_of(w)), lambda p, q, *_: (p, q, 0)),
                pl.BlockSpec((1, hh, qb), lambda p, q, *_: (p, 0, q)),
            ],
            out_specs=pl.BlockSpec((1, length, lanes_of(w3)), lambda p, q, *_: (p, 0, 0)),
            scratch_shapes=[
                pltpu.VMEM((1, length, w), BF),
                pltpu.VMEM((hh, length, HEAD_DIM), BF),
                pltpu.VMEM((hh, length, HEAD_DIM), BF),
                pltpu.VMEM((w, length), BF),
                pltpu.VMEM((hh, length, HEAD_DIM), F32),
                pltpu.VMEM((hh, length, HEAD_DIM), F32),
                pltpu.VMEM((hh, HEAD_DIM, qb), F32),
            ],
        ),
        compiler_params=params(2),
        cost_estimate=cost(
            problems * hh * 10 * length * length * 256, x.size * 6, problems * hh * length * length
        ),
        name="attend_back",
    )(lens, plan, index, *sources, x, o, lse)


def project_kernel(
    tm, width, group, per, sets, scales, order, x_ref, gain, shift, w_ref, bias, down, up, *outs
):
    normed_ref, ranks_ref, away_ref, mine_ref, n_scr, r_scr = outs
    c = pl.program_id(0)
    m = pl.program_id(1)
    rows = pl.ds(pl.multiple_of(m * tm, tm), tm)
    wide = group * w_ref.shape[0]

    @pl.when(c == 0)
    def _():
        unit, _ = norm_parts(x_ref[...].astype(F32))
        normed = (unit * gain[...] + shift[...]).astype(BF)
        n_scr[rows, :] = normed
        normed_ref[...] = normed
        rank = dot(normed, down[...]) * scales[m]
        keep = set_mask(rank.shape, sets[m], group, per)
        rank = jnp.where(keep, rank, 0.0).astype(BF)
        r_scr[rows, :] = rank
        ranks_ref[...] = rank

    y = dot(n_scr[rows, :], w_ref[:, 0].reshape(D, 3 * width)) + bias[0]
    table = up[:, 0].reshape(wide, 3 * width)
    rank = r_scr[rows, :]
    extra = [
        dot(rank[:, j * wide : (j + 1) * wide], table[:, j * width : (j + 1) * width]) for j in range(3)
    ]
    y = (y + jnp.concatenate(extra, axis=1)).astype(BF)
    half = pl.num_programs(0) // 2

    @pl.when(c < half)
    def _():
        away_ref[0, :, 0 : 3 * width] = y

    @pl.when(c >= half)
    def _():
        mine_ref[0, :, 0 : 3 * width] = y


def project(tokens, gain, shift, gathered, bias, tables, sets, scales, order, tm, per):
    own = tokens.shape[0]
    rr, nc, _, w3 = gathered.shape
    width = w3 // 3
    group = SETS * per
    wide = group * rr
    nm = own // tm
    half = nc // 2
    first = lambda c, m, *_: (jnp.where(c == 0, m, nm - 1), 0)
    flat = lambda c, m, *_: (0, 0)
    return pl.pallas_call(
        functools.partial(project_kernel, tm, width, group, per),
        out_shape=(
            jax.ShapeDtypeStruct((own, D), BF),
            jax.ShapeDtypeStruct((own, 3 * wide), BF),
            jax.ShapeDtypeStruct((half, own, lanes_of(w3)), BF),
            jax.ShapeDtypeStruct((half, own, lanes_of(w3)), BF),
        ),
        grid_spec=pltpu.PrefetchScalarGridSpec(
            num_scalar_prefetch=3,
            grid=(nc, nm),
            in_specs=[
                pl.BlockSpec((tm, D), first),
                pl.BlockSpec((1, D), flat),
                pl.BlockSpec((1, D), flat),
                pl.BlockSpec((rr, 1, D // rr, w3), lambda c, m, s, a, o: (0, o[c], 0, 0)),
                pl.BlockSpec((1, 1, w3), lambda c, m, s, a, o: (o[c], 0, 0)),
                pl.BlockSpec((D, 3 * wide), flat),
                pl.BlockSpec(
                    (rr, 1, group, w3), lambda c, m, s, a, o: (0, o[c], D // rr // group, 0)
                ),
            ],
            out_specs=[
                pl.BlockSpec((tm, D), first),
                pl.BlockSpec((tm, 3 * wide), first),
                pl.BlockSpec(
                    (1, tm, lanes_of(w3)),
                    lambda c, m, *_: (jnp.minimum(c, half - 1), jnp.where(c < half, m, nm - 1), 0),
                ),
                pl.BlockSpec(
                    (1, tm, lanes_of(w3)),
                    lambda c, m, *_: (jnp.maximum(c - half, 0), jnp.where(c < half, 0, m), 0),
                ),
            ],
            scratch_shapes=[pltpu.VMEM((own, D), BF), pltpu.VMEM((own, 3 * wide), BF)],
        ),
        compiler_params=params(2),
        cost_estimate=cost(2 * own * D * nc * w3 * 1.3, D * nc * w3 * 2 + own * (2 * D + nc * w3) * 2),
        name="project",
    )(sets, scales, order, tokens, gain, shift, gathered, bias, tables, gathered)


def piece_specs(sources, tm, at):
    def spec(j, v):
        def where_from(*ids):
            code = ids[-1]
            i = at(*ids[:-1])
            hit = code[3 * i] == j
            return (jnp.where(hit, code[3 * i + 1], 0), jnp.where(hit, code[3 * i + 2], 0), 0)

        return pl.BlockSpec((1, tm, v.shape[-1]), where_from)

    return [spec(j, v) for j, v in enumerate(sources)]


def lane_tiles(v, group):
    n = v.shape[1]
    pad = -n % 128
    if pad:
        v = jnp.concatenate([v, jnp.zeros((v.shape[0], pad), v.dtype)], axis=1)
    return [
        v[:, t * 128 : (t + 1) * 128].reshape(-1, group, 128) for t in range((n + pad) // 128)
    ]


def put_tiles(ref, first, v, group):
    for t, tile in enumerate(lane_tiles(v, group)):
        at = (first + t) * group
        ref[:, 0, at : at + group, :] = tile.astype(BF)


def adapt_back_kernel(tm, width, group, per, ns, nm, sets, scales, code, *refs):
    sources = refs[:ns]
    up, normed_ref, ranks_ref, dy_ref, grank_ref, gup_ref, gdown_ref, racc, gup, gdown = refs[ns:]
    c = pl.program_id(0)
    m = pl.program_id(1)
    last = c == pl.num_programs(0) - 1
    rows = pl.ds(pl.multiple_of(m * tm, tm), tm)
    wide = group * up.shape[0]
    choose(code[3 * (c * nm + m)], sources, dy_ref, 0)
    dy = dy_ref[0]
    table = up[:, 0].reshape(wide, 3 * width)
    pieces = [dy[:, j * width : (j + 1) * width] for j in range(3)]
    rpart = jnp.concatenate(
        [dot_t(pieces[j], table[:, j * width : (j + 1) * width]) for j in range(3)], axis=1
    )

    @pl.when(c == 0)
    def _():
        racc[rows, :] = rpart

    @pl.when(c > 0)
    def _():
        racc[rows, :] += rpart

    turned = ranks_ref[...].T
    for j in range(3):
        part = dot(turned[j * wide : (j + 1) * wide], pieces[j])

        @pl.when(m == 0)
        def _(j=j, part=part):
            gup[j] = part

        @pl.when(m > 0)
        def _(j=j, part=part):
            gup[j] += part

    @pl.when(m == nm - 1)
    def _():
        tiles = -(-width // 128)
        for j in range(3):
            put_tiles(gup_ref, j * tiles, gup[j], group)

    @pl.when(last)
    def _():
        grank = racc[rows, :] * scales[m]
        grank = jnp.where(set_mask(grank.shape, sets[m], group, per), grank, 0.0)
        grank_ref[...] = grank.astype(BF)
        part = token_sum(grank, normed_ref[...])

        @pl.when(m == 0)
        def _():
            gdown[...] = part

        @pl.when(m > 0)
        def _():
            gdown[...] += part

        @pl.when(m == nm - 1)
        def _():
            for j in range(3):
                gdown_ref[j] = gdown[j * wide : (j + 1) * wide, :].T.astype(BF)


def adapt_back(sources, code, gathered, normed, ranks, sets, scales, tm, per):
    own = normed.shape[0]
    rr, nc, _, w3 = gathered.shape
    width = w3 // 3
    group = SETS * per
    wide = group * rr
    nm = own // tm
    tiles = 3 * -(-width // 128)
    final = lambda c, m, *_: (jnp.where(c == nc - 1, m, 0), 0)
    return pl.pallas_call(
        functools.partial(adapt_back_kernel, tm, width, group, per, len(sources), nm),
        out_shape=(
            jax.ShapeDtypeStruct((nc, own, w3), BF),
            jax.ShapeDtypeStruct((own, 3 * wide), BF),
            jax.ShapeDtypeStruct((rr, nc, tiles * group, 128), BF),
            jax.ShapeDtypeStruct((3, D, wide), BF),
        ),
        grid_spec=pltpu.PrefetchScalarGridSpec(
            num_scalar_prefetch=3,
            grid=(nc, nm),
            in_specs=piece_specs(sources, tm, lambda c, m, s, a: c * nm + m)
            + [
                pl.BlockSpec((rr, 1, group, w3), lambda c, m, *_: (0, c, D // rr // group, 0)),
                pl.BlockSpec((tm, D), final),
                pl.BlockSpec((tm, 3 * wide), lambda c, m, *_: (m, 0)),
            ],
            out_specs=[
                pl.BlockSpec((1, tm, w3), lambda c, m, *_: (c, m, 0)),
                pl.BlockSpec((tm, 3 * wide), final),
                pl.BlockSpec((rr, 1, tiles * group, 128), lambda c, m, *_: (0, c, 0, 0)),
                pl.BlockSpec((3, D, wide), lambda c, m, *_: (0, 0, 0)),
            ],
            scratch_shapes=[
                pltpu.VMEM((own, 3 * wide), F32),
                pltpu.VMEM((3, wide, width), F32),
                pltpu.VMEM((3 * wide, D), F32),
            ],
        ),
        compiler_params=params(2),
        cost_estimate=cost(own * D * nc * w3 * 0.6, own * nc * w3 * 4),
        name="adapt_back",
    )(sets, scales, code, *sources, gathered, normed, ranks)


def project_back_kernel(tm, width, dy_ref, w_ref, grank_ref, down, x_ref, gm_ref, gain, gt_ref, acc):
    c = pl.program_id(0)
    m = pl.program_id(1)
    rows = pl.ds(pl.multiple_of(m * tm, tm), tm)
    part = dot_t(dy_ref[0], w_ref[:, 0].reshape(D, 3 * width))

    @pl.when(c == 0)
    def _():
        acc[rows, :] = part + dot_t(grank_ref[...], down[...])

    @pl.when(c > 0)
    def _():
        acc[rows, :] += part

    @pl.when(c == pl.num_programs(0) - 1)
    def _():
        unit, inverse = norm_parts(x_ref[...].astype(F32))
        e = acc[rows, :] * gain[...]
        mean = jnp.mean(e, axis=-1, keepdims=True)
        second = jnp.mean(e * unit, axis=-1, keepdims=True)
        gt_ref[...] = (gm_ref[...] + (e - mean - unit * second) * inverse).astype(BF)


def project_back(dy, gathered, grank, tables, tokens, grad_middle, gain, tm):
    own = tokens.shape[0]
    rr, nc, _, w3 = gathered.shape
    width = w3 // 3
    wide3 = grank.shape[1]
    nm = own // tm
    final = lambda c, m: (jnp.where(c == nc - 1, m, 0), 0)
    return pl.pallas_call(
        functools.partial(project_back_kernel, tm, width),
        out_shape=jax.ShapeDtypeStruct((own, D), BF),
        grid=(nc, nm),
        in_specs=[
            pl.BlockSpec((1, tm, w3), lambda c, m: (c, m, 0)),
            pl.BlockSpec((rr, 1, D // rr, w3), lambda c, m: (0, c, 0, 0)),
            pl.BlockSpec((tm, wide3), lambda c, m: (jnp.where(c == 0, m, nm - 1), 0)),
            pl.BlockSpec((D, wide3), lambda c, m: (0, 0)),
            pl.BlockSpec((tm, D), final),
            pl.BlockSpec((tm, D), final),
            pl.BlockSpec((1, D), lambda c, m: (0, 0)),
        ],
        out_specs=pl.BlockSpec((tm, D), final),
        scratch_shapes=[pltpu.VMEM((own, D), F32)],
        compiler_params=params(2),
        cost_estimate=cost(2 * own * D * nc * w3 * 1.1, D * nc * w3 * 2 + own * (4 * D + nc * w3) * 2),
        name="project_back",
    )(dy, gathered, grank, tables, tokens, grad_middle, gain)


def out_kernel(nc, nm, group, per, ns, sets, scales, code, *refs):
    sources = refs[:ns]
    x_ref, w_ref, bias, odown, oup, gain, shift, fdown = refs[ns : ns + 8]
    att_out, middle_ref, normed_ref, ro_ref, r1_ref, a_scr = refs[ns + 8 :]
    m = pl.program_id(0)
    c = pl.program_id(1)
    choose(code[3 * (c * nm + m)], sources, a_scr, c)

    @pl.when(c == nc - 1)
    def _():
        att = jnp.concatenate([a_scr[i] for i in range(nc)], axis=1)
        att_out[...] = att
        ro = dot_t(att, odown[...]) * scales[m]
        keep = set_mask(ro.shape, sets[m], group, per)
        ro = jnp.where(keep, ro, 0.0).astype(BF)
        ro_ref[...] = ro
        middle = x_ref[...].astype(F32) + dot_t(att, w_ref[...]) + dot_t(ro, oup[...]) + bias[...]
        middle_ref[...] = middle
        unit, _ = norm_parts(middle)
        normed = (unit * gain[...] + shift[...]).astype(BF)
        normed_ref[...] = normed
        r1_ref[...] = jnp.where(keep, dot(normed, fdown[...]) * scales[m], 0.0).astype(BF)


def out_project(sources, code, tokens, wo_t, bias, odown, tables, gain, shift, sets, scales, tm, nc, per, rr):
    own = tokens.shape[0]
    width = D // nc
    group = SETS * per
    wide = group * rr
    nm = own // tm
    row = lambda m, c, *_: (m, 0)
    flat = lambda m, c, *_: (0, 0)
    return pl.pallas_call(
        functools.partial(out_kernel, nc, nm, group, per, len(sources)),
        out_shape=(
            jax.ShapeDtypeStruct((own, D), BF),
            jax.ShapeDtypeStruct((own, D), F32),
            jax.ShapeDtypeStruct((own, D), BF),
            jax.ShapeDtypeStruct((own, wide), BF),
            jax.ShapeDtypeStruct((own, wide), BF),
        ),
        grid_spec=pltpu.PrefetchScalarGridSpec(
            num_scalar_prefetch=3,
            grid=(nm, nc),
            in_specs=piece_specs(sources, tm, lambda m, c, s, a: c * nm + m)
            + [
                pl.BlockSpec((tm, D), row),
                pl.BlockSpec((D, D), flat),
                pl.BlockSpec((1, D), flat),
                pl.BlockSpec((wide, D), flat),
                pl.BlockSpec((D, wide), lambda m, c, *_: (0, 4)),
                pl.BlockSpec((1, D), flat),
                pl.BlockSpec((1, D), flat),
                pl.BlockSpec((D, wide), lambda m, c, *_: (0, 3)),
            ],
            out_specs=[
                pl.BlockSpec((tm, D), row),
                pl.BlockSpec((tm, D), row),
                pl.BlockSpec((tm, D), row),
                pl.BlockSpec((tm, wide), row),
                pl.BlockSpec((tm, wide), row),
            ],
            scratch_shapes=[pltpu.VMEM((nc, tm, width), BF)],
        ),
        compiler_params=params(2),
        cost_estimate=cost(2 * own * D * D * 1.5, D * D * 2 + own * D * 12),
        name="out_project",
    )(sets, scales, code, *sources, tokens, wo_t, bias, odown, tables, gain, shift, tables)


def out_back_kernel(nc, width, group, per, sets, scales, side, gb_ref, w_ref, oup, odown, att_ref, ro_ref, *outs):
    away_ref, mine_ref, gup_ref, gdown_ref, gup, gdown = outs
    m = pl.program_id(0)

    @pl.when(m == 0)
    def _():
        gup[...] = jnp.zeros_like(gup)
        gdown[...] = jnp.zeros_like(gdown)

    gb = gb_ref[...]
    gro = dot(gb, oup[...]) * scales[m]
    gro = jnp.where(set_mask(gro.shape, sets[m], group, per), gro, 0.0)
    ga = (dot(gb, w_ref[...]) + dot(gro.astype(BF), odown[...])).astype(BF)
    half = nc // 2
    for i in range(nc):
        piece = ga[:, i * width : (i + 1) * width]

        @pl.when(side[0] == i // half)
        def _(i=i, piece=piece):
            mine_ref[i % half, :, 0:width] = piece

        @pl.when(side[0] != i // half)
        def _(i=i, piece=piece):
            away_ref[i % half, :, 0:width] = piece

    gup[...] += dot(ro_ref[...].T, gb)
    gdown[...] += token_sum(gro, att_ref[...])

    @pl.when(m == pl.num_programs(0) - 1)
    def _():
        gup_ref[...] = gup[...].T.astype(BF)
        whole = gdown[...]
        for i in range(nc):
            for t, tile in enumerate(lane_tiles(whole[:, i * width : (i + 1) * width], group)):
                gdown_ref[:, i, t * group : (t + 1) * group, :] = tile.astype(BF)


def out_back(gb, wo_t, tables, odown, att, ro, sets, scales, side, tm, nc, per, rr):
    own = gb.shape[0]
    width = D // nc
    group = SETS * per
    wide = group * rr
    half = nc // 2
    tiles = -(-width // 128)
    row = lambda m, *_: (m, 0)
    flat = lambda m, *_: (0, 0)
    return pl.pallas_call(
        functools.partial(out_back_kernel, nc, width, group, per),
        out_shape=(
            jax.ShapeDtypeStruct((half, own, lanes_of(width)), BF),
            jax.ShapeDtypeStruct((half, own, lanes_of(width)), BF),
            jax.ShapeDtypeStruct((D, wide), BF),
            jax.ShapeDtypeStruct((rr, nc, tiles * group, 128), BF),
        ),
        grid_spec=pltpu.PrefetchScalarGridSpec(
            num_scalar_prefetch=3,
            grid=(own // tm,),
            in_specs=[
                pl.BlockSpec((tm, D), row),
                pl.BlockSpec((D, D), flat),
                pl.BlockSpec((D, wide), lambda m, *_: (0, 4)),
                pl.BlockSpec((wide, D), flat),
                pl.BlockSpec((tm, D), row),
                pl.BlockSpec((tm, wide), row),
            ],
            out_specs=[
                pl.BlockSpec((half, tm, lanes_of(width)), lambda m, *_: (0, m, 0)),
                pl.BlockSpec((half, tm, lanes_of(width)), lambda m, *_: (0, m, 0)),
                pl.BlockSpec((D, wide), flat),
                pl.BlockSpec((rr, nc, tiles * group, 128), lambda m, *_: (0, 0, 0, 0)),
            ],
            scratch_shapes=[pltpu.VMEM((wide, D), F32), pltpu.VMEM((wide, D), F32)],
        ),
        compiler_params=params(1),
        cost_estimate=cost(2 * own * D * D * 1.5, D * D * 2 + own * D * 6),
        name="out_back",
    )(sets, scales, side, gb, wo_t, tables, odown, att, ro)


def mlp_kernel(tm, nm, group, per, sets, scales, *refs):
    n_ref, g_ref, mid_ref, w1_ref, w2_ref, b1, up1_ref, down2_ref, up2, down1, r1_ref, bias2, gain = refs[:13]
    out_ref, gm_ref, gb_ref, gup1_ref, gdown2_ref, gup2_ref, gdown1_ref = refs[13:20]
    acc, gacc, r2acc, gr1acc, gr2, gup1, gdown2, gup2, gdown1 = refs[20:]
    c = pl.program_id(0)
    m = pl.program_id(1)
    rows = pl.ds(pl.multiple_of(m * tm, tm), tm)
    a = scales[m]
    g = g_ref[...]
    normed = n_ref[...]
    hidden = w1_ref.shape[-1]
    wide = r1_ref.shape[1]
    keep = set_mask((tm, wide), sets[m], group, per)

    @pl.when(c == 0)
    def _():
        gr2[rows, :] = jnp.where(keep, dot(g, up2[...]) * a, 0.0).astype(BF)
        acc[rows, :] = jnp.zeros((tm, D), F32)
        gacc[rows, :] = jnp.zeros((tm, D), F32)
        r2acc[rows, :] = jnp.zeros((tm, wide), F32)
        gr1acc[rows, :] = jnp.zeros((tm, wide), F32)

    @pl.when(m == 0)
    def _():
        gup1[...] = jnp.zeros_like(gup1)
        gdown2[...] = jnp.zeros_like(gdown2)

    @pl.when((m == 0) & (c == 0))
    def _():
        gup2[...] = jnp.zeros_like(gup2)
        gdown1[...] = jnp.zeros_like(gdown1)

    w1 = w1_ref[:, 0].reshape(D, hidden)
    w2 = w2_ref[:, 0].reshape(D, hidden)
    up1 = up1_ref[:, 0].reshape(wide, hidden)
    down2 = down2_ref[:, 0].reshape(wide, hidden)
    r1 = r1_ref[...]
    grank2 = gr2[rows, :]
    pre = dot(normed, w1) + dot(r1, up1) + b1[0]
    upper = 0.5 + 0.5 * lax.erf(pre * (0.5**0.5))
    density = jnp.exp(pre * pre * -0.5) * ((2.0 * math.pi) ** -0.5)
    act = (pre * upper).astype(BF)
    slope = upper + pre * density
    gact = dot(g, w2) + dot(grank2, down2)
    gpre = (gact * slope).astype(BF)
    acc[rows, :] += dot_t(act, w2)
    r2acc[rows, :] += dot_t(act, down2)
    gacc[rows, :] += dot_t(gpre, w1)
    gr1acc[rows, :] += dot_t(gpre, up1)
    gdown2[...] += dot(grank2.T, act)
    gup1[...] += dot(r1.T, gpre)

    @pl.when(m == nm - 1)
    def _():
        put_tiles(gup1_ref, 0, gup1[...], group)
        put_tiles(gdown2_ref, 0, gdown2[...], group)

    @pl.when(c == pl.num_programs(0) - 1)
    def _():
        r2 = jnp.where(keep, r2acc[rows, :] * a, 0.0).astype(BF)
        middle = mid_ref[...]
        out_ref[...] = (middle + acc[rows, :] + dot_t(r2, up2[...]) + bias2[...]).astype(BF)
        gup2[...] += dot(r2.T, g)
        gr1 = jnp.where(keep, gr1acc[rows, :] * a, 0.0).astype(BF)
        e = (gacc[rows, :] + dot_t(gr1, down1[...])) * gain[...]
        gdown1[...] += dot(gr1.T, normed)
        unit, inverse = norm_parts(middle)
        mean = jnp.mean(e, axis=-1, keepdims=True)
        second = jnp.mean(e * unit, axis=-1, keepdims=True)
        gm = g.astype(F32) + (e - mean - unit * second) * inverse
        gm_ref[...] = gm
        gb_ref[...] = gm.astype(BF)

        @pl.when(m == nm - 1)
        def _():
            gup2_ref[...] = gup2[...].T.astype(BF)
            gdown1_ref[...] = gdown1[...].T.astype(BF)


def mlp(normed, g, middle, gathered, b1, tables, r1, bias2, gain, sets, scales, tm, per, at):
    own = g.shape[0]
    rr, nc, _, hidden = gathered.shape
    group = SETS * per
    wide = group * rr
    nm = own // tm
    tiles = -(-hidden // 128)
    row = lambda c, m, *_: (m, 0)
    final = lambda c, m, *_: (jnp.where(c == nc - 1, m, 0), 0)
    flat = lambda c, m, *_: (0, 0)
    wblock = (rr, 1, D // rr, hidden)
    return pl.pallas_call(
        functools.partial(mlp_kernel, tm, nm, group, per),
        out_shape=(
            jax.ShapeDtypeStruct((own, D), BF),
            jax.ShapeDtypeStruct((own, D), F32),
            jax.ShapeDtypeStruct((own, D), BF),
            jax.ShapeDtypeStruct((rr, nc, tiles * group, 128), BF),
            jax.ShapeDtypeStruct((rr, nc, tiles * group, 128), BF),
            jax.ShapeDtypeStruct((D, wide), BF),
            jax.ShapeDtypeStruct((D, wide), BF),
        ),
        grid_spec=pltpu.PrefetchScalarGridSpec(
            num_scalar_prefetch=2,
            grid=(nc, nm),
            in_specs=[
                pl.BlockSpec((tm, D), row),
                pl.BlockSpec((tm, D), row),
                pl.BlockSpec((tm, D), final, pipeline_mode=pl.Buffered(1)),
                pl.BlockSpec(wblock, lambda c, m, *_: (0, c, 0, 0)),
                pl.BlockSpec(wblock, lambda c, m, *_: (0, c, 1, 0)),
                pl.BlockSpec((1, 1, hidden), lambda c, m, *_: (c, 0, 0)),
                pl.BlockSpec((rr, 1, group, hidden), lambda c, m, *_: (0, c, at // group, 0)),
                pl.BlockSpec((rr, 1, group, hidden), lambda c, m, *_: (0, c, at // group + 1, 0)),
                pl.BlockSpec((D, wide), lambda c, m, *_: (0, 5), pipeline_mode=pl.Buffered(1)),
                pl.BlockSpec((D, wide), lambda c, m, *_: (0, 3), pipeline_mode=pl.Buffered(1)),
                pl.BlockSpec((tm, wide), row),
                pl.BlockSpec((1, D), flat),
                pl.BlockSpec((1, D), flat),
            ],
            out_specs=[
                pl.BlockSpec((tm, D), final),
                pl.BlockSpec((tm, D), final),
                pl.BlockSpec((tm, D), final),
                pl.BlockSpec((rr, 1, tiles * group, 128), lambda c, m, *_: (0, c, 0, 0)),
                pl.BlockSpec((rr, 1, tiles * group, 128), lambda c, m, *_: (0, c, 0, 0)),
                pl.BlockSpec((D, wide), flat),
                pl.BlockSpec((D, wide), flat),
            ],
            scratch_shapes=[
                pltpu.VMEM((own, D), F32),
                pltpu.VMEM((own, D), F32),
                pltpu.VMEM((own, wide), F32),
                pltpu.VMEM((own, wide), F32),
                pltpu.VMEM((own, wide), BF),
                pltpu.VMEM((wide, hidden), F32),
                pltpu.VMEM((wide, hidden), F32),
                pltpu.VMEM((wide, D), F32),
                pltpu.VMEM((wide, D), F32),
            ],
        ),
        compiler_params=params(2, 67043328),
        cost_estimate=cost(8 * own * D * nc * hidden * 1.2, D * nc * hidden * 4 + own * D * 30, own * nc * hidden * 2),
        name="mlp",
    )(
        sets, scales, normed, g, middle, gathered, gathered, b1, gathered, gathered, tables, tables, r1, bias2, gain
    )


def assemble_kernel(width, parts, w_ref, o_ref, w_out, o_out):
    _, nc = w_ref.shape[:2]
    columns, downs = [], []
    for c in range(nc):
        block = w_ref[:, c]
        rows = [block[:, :, j * width : (j + 1) * width] for j in range(parts)]
        columns.append(jnp.concatenate(rows, axis=1).reshape(D, width))
        downs.append(o_ref[:, c, :, 0:width].reshape(-1, width))
    w_out[...] = jnp.concatenate(columns, axis=1)
    o_out[...] = jnp.concatenate(downs, axis=1)


def assemble(gathered, at_w, rows_w, at_o, group, width):
    nr, nc, _, hidden = gathered.shape
    parts = hidden // width
    if rows_w % 8 == 0 and at_w % rows_w == 0:
        return pl.pallas_call(
            functools.partial(assemble_kernel, width, parts),
            out_shape=(
                jax.ShapeDtypeStruct((D, D), BF),
                jax.ShapeDtypeStruct((nr * group, D), BF),
            ),
            grid=(1,),
            in_specs=[
                pl.BlockSpec((nr, nc, rows_w, hidden), lambda i: (0, 0, at_w // rows_w, 0)),
                pl.BlockSpec((nr, nc, group, hidden), lambda i: (0, 0, at_o // group, 0)),
            ],
            out_specs=[
                pl.BlockSpec((D, D), lambda i: (0, 0)),
                pl.BlockSpec((nr * group, D), lambda i: (0, 0)),
            ],
            compiler_params=params(1),
            name="assemble",
        )(gathered, gathered)
    w = gathered[:, :, at_w : at_w + rows_w].reshape(nr, nc, rows_w, parts, width)
    o = gathered[:, :, at_o : at_o + group, :width]
    return (
        w.transpose(0, 3, 2, 1, 4).reshape(D, D),
        o.transpose(0, 2, 1, 3).reshape(nr * group, D),
    )


def pick(flag, first, second):
    return jnp.where(flag, first, second)


def table_of(values):
    return jnp.stack([jnp.asarray(v, jnp.int32) for v in values])


class Exchange:
    def __init__(self, nc, own, clips, clip_len, tm):
        self.nc, self.own, self.clips, self.clip_len, self.tm = nc, own, clips, clip_len, tm
        self.local = nc == 4 and clips == 3 and own == 3 * tm and clip_len == 4 * tm
        col = lax.axis_index("cols")
        self.nm = nm = own // tm
        if not self.local:
            self.order = jnp.arange(nc, dtype=jnp.int32)
            self.side = jnp.ones((1,), jnp.int32)
            self.plans = [jnp.zeros((2,), jnp.int32)]
            self.indices = [jnp.arange(clips, dtype=jnp.int32)]
            entry = jnp.arange(nc * nm, dtype=jnp.int32)
            self.code = jnp.stack([entry * 0, entry // nm, entry % nm], axis=1).reshape(-1)
            return
        y, k = col // 2, col % 2
        self.y, self.k = y, k
        self.holder = y != k
        self.order = (jnp.arange(4, dtype=jnp.int32) + 2 * (1 - k)) % 4
        self.side = k[None]
        b = jnp.arange(4, dtype=jnp.int32)
        g = b + 2 * y
        clip_plan = jnp.concatenate([pick(g // 3 == k, 0, 1), g % 3])
        g = pick(y == 0, 4 + b, b - 2)
        near = b // 2 == y
        source = pick(near, pick(g // 3 == k, 0, 1), pick(self.holder, 3, 2))
        shared_plan = jnp.concatenate([source, pick(near, g % 3, b % 2)])
        self.plans = [clip_plan.astype(jnp.int32), shared_plan.astype(jnp.int32)]
        self.indices = [jnp.array([0, 1, 0, 1], jnp.int32), table_of([y, y, 0, 0])]
        entry = jnp.arange(12, dtype=jnp.int32)
        c, m = entry // 3, entry % 3
        g = 3 * k + m
        inside = (g >= 2 * y) & (g < 2 * y + 4)
        same, idx = c // 2 == k, c % 2
        source = pick(
            inside,
            pick(same, 0, 2),
            pick(idx == y, pick(same, 1, 3), pick(same, 4, 5)),
        )
        block = pick(
            inside,
            g - 2 * y,
            pick(y == 0, g - 4, pick(idx == y, g + 2, g)),
        )
        self.code = (
            jnp.stack([source, pick(inside, idx, 0), block], axis=1).astype(jnp.int32).reshape(-1)
        )

    def lens(self, lengths):
        if not self.local:
            return (lengths,)
        mine = pick(self.y == 0, lengths[0], lengths[2])
        return (jnp.stack([mine, mine]), lengths[1:2])

    def to_heads(self, away, mine):
        f = mine.shape[-1]
        if not self.local:
            moved = lax.all_to_all(jnp.concatenate([away, mine]), "cols", 0, 0, tiled=True)
            return [[moved.reshape(self.clips, self.clip_len, f)]]
        y, k, half = self.y, self.k, self.clip_len // 2
        start = pick(k == 1, self.own - half, 0)
        got = lax.ppermute(away, "cols", [(i, i ^ 1) for i in range(4)])
        one = lax.dynamic_slice(mine, (1 - y, start, 0), (1, half, f))
        two = lax.dynamic_slice(away, (1 - y, start, 0), (1, half, f))
        got_one = lax.ppermute(one, "cols", [(1, 3), (2, 0)])
        got_two = lax.ppermute(two, "cols", [(1, 2), (2, 1)])
        return [[mine, got], [mine, got, got_one, got_two]]

    def from_heads(self, parts):
        if not self.local:
            (v,) = parts
            v = v.reshape(self.nc, self.own, v.shape[-1])
            return [lax.all_to_all(v, "cols", 0, 0, tiled=True)]
        clip, shared = parts
        half = self.clip_len // 2
        far = lax.dynamic_slice(shared, (0, (1 - self.y) * half, 0), (1, half, clip.shape[-1]))
        swap = [(i, i ^ 1) for i in range(4)]
        got_one = lax.ppermute(far, "cols", [(3, 1), (0, 2)])
        got_two = lax.ppermute(far, "cols", [(2, 1), (1, 2)])
        got_shared = lax.ppermute(shared, "cols", swap)
        return [clip, shared, lax.ppermute(clip, "cols", swap), got_shared, got_one, got_two]


def up_to(n, k):
    return -(-n // k) * k


def rows_padded(v, rows, lanes):
    return jnp.pad(v.astype(BF), ((0, rows - v.shape[0]), (0, lanes - v.shape[1])))


def halves(v):
    high = v.astype(BF)
    return high, (v - high.astype(F32)).astype(BF)


def scatter_sum(pieces):
    whole = jnp.concatenate(pieces, axis=2)
    n = whole.shape[2]
    whole = jnp.pad(whole, ((0, 0), (0, 0), (0, up_to(n, 8) - n), (0, 0)))
    return whole.reshape(-1, 128)


def join(v, nc):
    col = lax.axis_index("cols")
    zeros = (0,) * v.ndim
    held = lax.dynamic_update_slice(jnp.zeros((nc,) + v.shape, v.dtype), v[None], (col,) + zeros)
    step = 1
    while step < nc:
        base = col // step * step
        sent = lax.dynamic_slice(held, (base,) + zeros, (step,) + v.shape)
        got = lax.ppermute(sent, "cols", [(i, i ^ step) for i in range(nc)])
        held = lax.dynamic_update_slice(held, got, (base ^ step,) + zeros)
        step *= 2
    return held


def body(
    tokens,
    cotangent,
    clip_lengths,
    clip_sets,
    clip_scales,
    norm1_gain,
    norm1_shift,
    w_query,
    query_bias,
    w_key,
    w_value,
    value_bias,
    w_out,
    out_bias,
    norm2_gain,
    norm2_shift,
    w_fc1,
    fc1_bias,
    w_fc2,
    fc2_bias,
    query_down,
    query_up,
    key_down,
    key_up,
    value_down,
    value_up,
    out_down,
    out_up,
    fc1_down,
    fc1_up,
    fc2_down,
    fc2_up,
):
    nr = lax.axis_size("rows")
    nc = lax.axis_size("cols")
    col = lax.axis_index("cols")
    clips = clip_lengths.shape[0]
    own = tokens.shape[0]
    clip_len = own * nc // clips
    tm = math.gcd(own, clip_len)
    width = query_bias.shape[0]
    hidden = fc1_bias.shape[0]
    hh = width // HEAD_DIM
    dr = w_query.shape[0]
    per = RANK // nr
    group = SETS * per
    wide = group * nr
    dc = dr // nc
    exchange = Exchange(nc, own, clips, clip_len, tm)

    block_clip = (col * own + jnp.arange(own // tm, dtype=jnp.int32) * tm) // clip_len
    sets = jnp.take(clip_sets, block_clip)
    scales = jnp.take(clip_scales, block_clip)

    downs = jnp.stack([query_down, key_down, value_down, fc1_down])
    downs = lax.dynamic_slice(downs, (0, 0, col * dc, 0), (4, SETS, dc, RANK))
    downs = downs.reshape(4, SETS, dc, nr, per).transpose(2, 0, 3, 1, 4).reshape(dc, 4 * wide)
    ups = jnp.stack([out_up, fc2_up])
    ups = lax.dynamic_slice(ups, (0, 0, 0, col * dc), (2, SETS, RANK, dc))
    ups = ups.reshape(2, SETS, nr, per, dc).transpose(4, 0, 2, 1, 3).reshape(dc, 2 * wide)
    tables = jnp.concatenate([downs, ups], axis=1)

    lanes = 3 * width
    qh, ql = halves(query_bias)
    vh, vl = halves(value_bias)
    none = jnp.zeros_like(qh)
    natural = lanes >= 6 * wide
    small = rows_padded(tables, dc, lanes) if natural else tables.reshape(-1, lanes)
    small_rows = small.shape[0]
    at_bias = dr + group
    at_table = up_to(at_bias + 2, 16)
    packed = jnp.concatenate(
        [
            jnp.concatenate([w_query, w_key, w_value], axis=1),
            jnp.concatenate([v.reshape(group, width) for v in (query_up, key_up, value_up)], axis=1),
            rows_padded(jnp.stack([jnp.concatenate([qh, none, vh]), jnp.concatenate([ql, none, vl])]), at_table - at_bias, lanes),
            rows_padded(small, up_to(small_rows, 16), lanes),
        ],
        axis=0,
    )
    g1 = lax.all_gather(packed, BOTH, axis=0).reshape(nr, nc, -1, lanes)
    tables = g1[:, :, at_table : at_table + small_rows]
    if natural:
        tables = tables[..., : 6 * wide]
    tables = tables.reshape(D, 6 * wide)
    bias_qkv = jnp.sum(g1[0, :, at_bias : at_bias + 2].astype(F32), axis=1, keepdims=True)

    parts = hidden // width
    rows_w = dr // parts
    at_w = 2 * dr
    at_f = up_to(at_w + rows_w, 16)
    at_o = at_f + 2 * group
    at_b = at_o + group
    wo = w_out.T.reshape(parts, rows_w, width).transpose(1, 0, 2).reshape(rows_w, hidden)
    turn = lambda v: jnp.swapaxes(v, 1, 2).reshape(group, -1)
    packed = jnp.concatenate(
        [
            w_fc1,
            w_fc2.T,
            rows_padded(wo, at_f - at_w, hidden),
            fc1_up.reshape(group, hidden),
            turn(fc2_down),
            rows_padded(turn(out_down), group, hidden),
            rows_padded(jnp.stack(halves(fc1_bias)), 16, hidden),
        ],
        axis=0,
    )
    packed, g1 = lax.optimization_barrier((packed, g1))
    g2 = lax.all_gather(packed, BOTH, axis=0).reshape(nr, nc, -1, hidden)
    wo_t, odown = assemble(g2, at_w, rows_w, at_o, group, width)
    b1 = jnp.sum(g2[0, :, at_b : at_b + 2].astype(F32), axis=1, keepdims=True)

    gain1, shift1 = norm1_gain[None], norm1_shift[None]
    gain2, shift2 = norm2_gain[None], norm2_shift[None]

    normed, ranks, away, mine = project(
        tokens, gain1, shift1, g1, bias_qkv, tables, sets, scales, exchange.order, tm, per
    )
    lens = exchange.lens(clip_lengths)
    results = []
    for sources, plan, index, n in zip(
        exchange.to_heads(away, mine), exchange.plans, exchange.indices, lens
    ):
        if results:
            n, _ = lax.optimization_barrier((n, results[-1][1]))
        results.append(attend(sources, plan, index, n, clip_len, hh))
    pieces = exchange.from_heads([r[0] for r in results])
    att, middle, normed_mlp, ro, r1 = out_project(
        pieces, exchange.code, tokens, wo_t, out_bias[None], odown, tables, gain2, shift2, sets, scales, tm, nc, per, nr
    )
    output, grad_middle, grad_branch, gup1, gdown2, gup2, gdown1 = mlp(
        normed_mlp, cotangent, middle, g2, b1, tables, r1, fc2_bias[None], gain2, sets, scales, tm, per, at_f
    )
    away, mine, goup, godown = out_back(
        grad_branch, wo_t, tables, odown, att, ro, sets, scales, exchange.side, tm, nc, per, nr
    )

    by_model = lambda v: v.reshape(nr, nc, dc, wide)
    late = scatter_sum([gup1, gdown2, godown, by_model(gdown1), by_model(goup), by_model(gup2)])
    late, away, mine = lax.optimization_barrier((late, away, mine))
    summed = lax.psum_scatter(late, BOTH, scatter_dimension=0, tiled=True).astype(F32)

    def untile(v, n):
        t = v.shape[0] // group
        return v.reshape(t, group, 128).transpose(1, 0, 2).reshape(group, t * 128)[:, :n].reshape(SETS, per, n)

    def model_tables(v):
        k = v.shape[0] // dc
        every = join(v, nc).reshape(nc, k, dc, wide).swapaxes(0, 1)
        return every.reshape(k, dr, nr, SETS, per)

    as_down = lambda v: v.transpose(2, 0, 1, 3).reshape(SETS, dr, RANK)
    as_up = lambda v: v.transpose(2, 1, 3, 0).reshape(SETS, RANK, dr)
    flip = lambda v: jnp.swapaxes(v, 1, 2)
    a = gup1.shape[2]
    b = godown.shape[2]
    grad_fc1_up = untile(summed[:a], hidden)
    grad_fc2_down = flip(untile(summed[a : 2 * a], hidden))
    grad_out_down = flip(untile(summed[2 * a : 2 * a + b], width))
    model = model_tables(summed[2 * a + b : 2 * a + b + 3 * dc])
    grad_fc1_down, grad_out_up, grad_fc2_up = as_down(model[0]), as_up(model[1]), as_up(model[2])

    calls = list(
        zip(exchange.to_heads(away, mine), exchange.plans, exchange.indices, results, lens)
    )
    backs = []
    for sources, plan, index, (o, lse, x), n in reversed(calls):
        if backs:
            n, _ = lax.optimization_barrier((n, backs[-1]))
        backs.append(attend_back(sources, plan, index, x, o, lse, n, hh))
    pieces = exchange.from_heads(backs[::-1])
    dy, grank, gup, gdown = adapt_back(
        pieces, exchange.code, g1, normed, ranks, sets, scales, tm, per
    )
    last = scatter_sum([gup] + [by_model(gdown[j]) for j in range(3)])
    last, dy = lax.optimization_barrier((last, dy))
    summed = lax.psum_scatter(last, BOTH, scatter_dimension=0, tiled=True).astype(F32)
    grad_tokens = project_back(dy, g1, grank, tables, tokens, grad_middle, gain1, tm)
    a = gup.shape[2] // 3
    up = [untile(summed[j * a : (j + 1) * a], width) for j in range(3)]
    model = model_tables(summed[3 * a : 3 * a + 3 * dc])
    down = [as_down(model[j]) for j in range(3)]
    return (
        output,
        grad_tokens,
        down[0],
        up[0],
        down[1],
        up[1],
        down[2],
        up[2],
        grad_out_down,
        grad_out_up,
        grad_fc1_down,
        grad_fc1_up,
        grad_fc2_down,
        grad_fc2_up,
    )


def solution(mesh):
    both = P(("rows", "cols"), None)
    grid = P("rows", "cols")
    turned = P("cols", "rows")
    down = P(None, "rows", None)
    up = P(None, "rows", "cols")
    far_down = P(None, "cols", "rows")
    far_up = P(None, None, "rows")
    return jax.shard_map(
        body,
        mesh=mesh,
        in_specs=(
            both,
            both,
            P("rows"),
            P("rows"),
            P("rows"),
            P(),
            P(),
            grid,
            P("cols"),
            grid,
            grid,
            P("cols"),
            turned,
            P(),
            P(),
            P(),
            grid,
            P("cols"),
            turned,
            P(),
            down,
            up,
            down,
            up,
            down,
            up,
            far_down,
            far_up,
            down,
            up,
            far_down,
            far_up,
        ),
        out_specs=(
            both,
            both,
            down,
            up,
            down,
            up,
            down,
            up,
            far_down,
            far_up,
            down,
            up,
            far_down,
            far_up,
        ),
        check_vma=False,
    )
```

time: 1020 us -> 826 us (0.81)
  local copies, waits for them, and re-layouts: 232 us -> 49.8 us
  other arithmetic: 89.1 us -> 11.3 us
  Pallas kernels: 332 us -> 393 us
  waiting for transfers between devices: 299 us -> 316 us
  blocking collectives: 12.9 us -> 0 us
  starting transfers between devices: 23 us -> 34 us
    reduce_scatter x2 -> x0, waiting for transfers between devices: 172 us -> none  [scatter_sum(): lax.psum_scatter(whole, BOTH, scatter_dimension=0, tiled=True).astype(F32)]
    all_gather x1, waiting for transfers between devices: 0.01 us -> 87.2 us  [body(): g2 = lax.all_gather(packed, BOTH, axis=0).reshape(nr, nc, -1, hidden)]
    reshape x36 -> x19, local copies, waits for them, and re-layouts: 74.8 us -> 5.72 us  [the longest x8 2.52 us: untile(): v.reshape(t, group, 128).transpose(1, 0, 2).reshape(group, t * 128)[:, :n]]
    pallas_call x8 -> x10, Pallas kernels: 297 us -> 364 us  [the longest x1 105 us: mlp(): pl.pallas_call(functools.partial(mlp_kernel, tm, nm, group, per), out_sha...]
    unnamed x4 -> x6, waiting for transfers between devices: 0.07 us -> 63.8 us
    dynamic_slice x18 -> x10, local copies, waits for them, and re-layouts: 48 us -> 5.67 us  [the longest x2 2.66 us: to_heads(): one = lax.dynamic_slice(mine, (1 - y, start, 0), (1, half, f))]
    ppermute x2, waiting for transfers between devices: 1.49 us -> 42 us  [from_heads(): got_one = lax.ppermute(far, 'cols', [(3, 1), (0, 2)])]
    select_n x12 -> x5, other arithmetic: 40.7 us -> 0.67 us  [pick(): return jnp.where(flag, first, second)]
  transfers between devices with their start and end apart: 16 -> 22, of which waited for: 5 -> 6; matrix products, arithmetic and copies ran while one was open for 21% -> 4% of each run, Pallas kernels for 19% -> 30%
where the time goes in v2:
time: 826 us; the launch traced here: 820 us
  Pallas kernels  393 us (48%)
  waiting for transfers between devices  316 us (38%)
  local copies, waits for them, and re-layouts  49.8 us (6%)
  starting transfers between devices  34 us (4%)
  between operations  16.5 us (2%)
  other arithmetic  11.3 us (1%)
    all_gather x1, waiting for transfers between devices, body(): g1 = lax.all_gather(packed, BOTH, axis=0).reshape(nr, nc, -1, lanes)  112 us
    pallas_call x1, Pallas kernels, mlp(): pl.pallas_call(functools.partial(mlp_kernel, tm, nm, group, per), out_sha...  105 us
    pallas_call x2, Pallas kernels, attend_back(): pl.pallas_call(functools.partial(attend_back_kernel, hh, length, qb, kb,...  88.4 us
    all_gather x1, waiting for transfers between devices, body(): g2 = lax.all_gather(packed, BOTH, axis=0).reshape(nr, nc, -1, hidden)  87.2 us
    pallas_call x2, Pallas kernels, attend(): pl.pallas_call(functools.partial(attend_kernel, hh, length, qb, kb, len(s...  67 us
    unnamed x6, waiting for transfers between devices  63.8 us
    ppermute x2, waiting for transfers between devices, from_heads(): got_one = lax.ppermute(far, 'cols', [(3, 1), (0, 2)])  42 us
    pallas_call x1, Pallas kernels, project(): pl.pallas_call(functools.partial(project_kernel, tm, width, group, per),...  29.6 us
  transfers between devices with their start and end apart: 22, of which 6 were waited for; matrix products, arithmetic and copies ran while one was open for 4% of the time, Pallas kernels for 30%

profile of v2, /device:TPU:0, one launch (start us, length us, event | category | flops | bytes accessed | tf_op | source)
XLA Modules:
  0.0 820.4 jit_solution(17102802017653520657)
XLA Ops:
  15.6 111.8 %all-gather.5.cloned.1.call-done = bf16[7680,960]{1,0:T(8,128)(2,1)} async-done(((bf16[240,960]{1,0:T(8,128)(2,1)}), bf16[7680,960]{1,0:T(8,128)(2,1)}) %all-gather.5.cloned.1.call-update) | async-done | bytes 14745616 | tf_op jit(solution)/shard_map/all_gather | solution.py:1111
  131.6 3.0 slice.121
  136.1 29.6 %project.1 = (bf16[1152,1280]{1,0:T(8,128)(2,1)}, bf16[1152,384]{1,0:T(8,128)(2,1)}, bf16[2,1152,1024]{2,1,0:T(8,128)(2,1)}, bf16[2,1152,1024]{2,1,0:T(8,128)(2,1)}) custom-call(s32[3]{0:T(128)} %broadcast_select_fusion.4.sets, f32[3]{0:T(128)} %broadcast_select_fusion.3.scales, s32[4]{0:T(128)} %and_select_fusion.4.order, bf16[1152,1280]{1,0:T(8,128)(2,1)} %x_ref.3, ...), custom_call_target="tpu_custom_call" | custom-call | flops 14722007040 | bytes 24576000 | tf_op jit(solution)/shard_map/project/pallas_call | solution.py:338
  175.6 46.1 %attend.2 = (bf16[2,1536,384]{2,1,0:T(8,128)(2,1)}, f32[2,4,1536]{2,1,0:T(4,128)}, bf16[2,1536,960]{2,1,0:T(8,128)(2,1)}) custom-call(s32[2]{0:T(128)} %pad_add_fusion.1.lens, s32[8]{0:T(128)} %pad_add_fusion.2.plan, s32[4]{0:T(128)} %constant.181.clone.index, bf16[2,1152,1024]{2,1,0:T(8,128)(2,1)} %get-tuple-element.56.refs_0_, ...), custom_call_target="tpu_custom_call" | custom-call | flops 19327352832 | bytes 17694720 | tf_op jit(solution)/shard_map/attend/pallas_call | solution.py:152
  221.7 4.0 collective-permute-start.3
  226.8 20.9 %attend.3 = (bf16[1,1536,384]{2,1,0:T(8,128)(2,1)}, f32[1,4,1536]{2,1,0:T(4,128)}, bf16[1,1536,960]{2,1,0:T(8,128)(2,1)}) custom-call(s32[1]{0:T(128)} %get-tuple-element.60.lens, s32[8]{0:T(128)} %pad_add_fusion.3.plan, s32[4]{0:T(128)} %get-tuple-element.152.index, bf16[2,1152,1024]{2,1,0:T(8,128)(2,1)} %get-tuple-element.56.refs_0_, ...), custom_call_target="tpu_custom_call" | custom-call | flops 9663676416 | bytes 8847360 | tf_op jit(solution)/shard_map/attend/pallas_call | solution.py:152
  248.9 4.8 collective-permute-start.5
  257.6 87.2 %all-gather.7.cloned.1.call-done = bf16[13824,1280]{1,0:T(8,128)(2,1)} async-done(((bf16[432,1280]{1,0:T(8,128)(2,1)}), bf16[13824,1280]{1,0:T(8,128)(2,1)}) %all-gather.7.cloned.1.call-update) | async-done | bytes 35389456 | tf_op jit(solution)/shard_map/all_gather | solution.py:1139
  344.8 5.4 assemble.1
  353.2 23.8 %out_project.1 = (bf16[1152,1280]{1,0:T(8,128)(2,1)}, f32[1152,1280]{1,0:T(8,128)}, bf16[1152,1280]{1,0:T(8,128)(2,1)}, bf16[1152,128]{1,0:T(8,128)(2,1)}, bf16[1152,128]{1,0:T(8,128)(2,1)}) custom-call(s32[3]{0:T(128)} %broadcast_select_fusion.4.sets, f32[3]{0:T(128)} %broadcast_select_fusion.3.scales, s32[36]{0:T(128)} %reshape.387.code, ...), custom_call_target="tpu_custom_call" | custom-call | flops 5662310400 | bytes 20971520 | tf_op jit(solution)/shard_map/out_project/pallas_call | solution.py:599
  377.0 104.8 %mlp.1 = (bf16[1152,1280]{1,0:T(8,128)(2,1)}, f32[1152,1280]{1,0:T(8,128)}, bf16[1152,1280]{1,0:T(8,128)(2,1)}, bf16[8,4,160,128]{3,2,1,0:T(8,128)(2,1)}, bf16[8...) custom-call(s32[3]{0:T(128)} %broadcast_select_fusion.4.sets, ...), custom_call_target="tpu_custom_call" | custom-call | flops 72477573120 | bytes 70451200 | tf_op jit(solution)/shard_map/mlp/pallas_call | solution.py:806
  481.9 2.8 constant_dynamic-update-slice_fusion.8
  486.0 18.1 %out_back.1 = (bf16[2,1152,384]{2,1,0:T(8,128)(2,1)}, bf16[2,1152,384]{2,1,0:T(8,128)(2,1)}, bf16[1280,128]{1,0:T(8,128)(2,1)}, bf16[8,4,48,128]{3,2,1,0:T(8,128)(2,1)}) custom-call(s32[3]{0:T(128)} %broadcast_select_fusion.4.sets, f32[3]{0:T(128)} %broadcast_select_fusion.3.scales, s32[1]{0:T(128)} %bitcast.26.side, ...), custom_call_target="tpu_custom_call" | custom-call | flops 5662310400 | bytes 12124160 | tf_op jit(solution)/shard_map/out_back/pallas_call | solution.py:683
  513.5 8.9 %collective-permute-done.8.refs_2_ = bf16[1,768,384]{2,1,0:T(8,128)(2,1)S(1)} collective-permute-done((bf16[1,768,384]{2,1,0:T(8,128)(2,1)S(1)}, bf16[1,768,384]{2,1,0:T(8,128)(2,1)S(1)}, u32[]{:S(2)}, u32[]{:S(2)}) %collective-permute-start.8) | collective-permute-done | bytes 589856 | tf_op jit(solution)/shard_map/ppermute | solution.py:977
  523.3 20.9 %attend_back.2.refs_1_ = bf16[1,1536,1024]{2,1,0:T(8,128)(2,1)} custom-call(s32[1]{0:T(128)} %get-tuple-element.60.lens, s32[8]{0:T(128)} %pad_add_fusion.3.plan, s32[4]{0:T(128)} %get-tuple-element.152.index, bf16[2,1152,384]{2,1,0:T(8,128)(2,1)} %get-tuple-element.80.refs_0_, bf16[2,1152,384]{2,1,0:T(8,128)(2,1)} %collective-permute-done.7.refs_1_, ...), custom_call_target="tpu_custom_call" | custom-call | flops 24159191040 | bytes 8847360 | tf_op jit(solution)/shard_map/attend_back/pallas_call | solution.py:258
  544.2 67.5 %attend_back.3.refs_0_ = bf16[2,1536,1024]{2,1,0:T(8,128)(2,1)} custom-call(s32[2]{0:T(128)} %pad_add_fusion.1.lens, s32[8]{0:T(128)} %pad_add_fusion.2.plan, s32[4]{0:T(128)} %constant.181.clone.index, bf16[2,1152,384]{2,1,0:T(8,128)(2,1)} %get-tuple-element.80.refs_0_, bf16[2,1152,384]{2,1,0:T(8,128)(2,1)} %collective-permute-done.7.refs_1_, ...), custom_call_target="tpu_custom_call" | custom-call | flops 48318382080 | bytes 17694720 | tf_op jit(solution)/shard_map/attend_back/pallas_call | solution.py:258
  611.7 8.8 %collective-permute-start.10 = (bf16[2,1536,1024]{2,1,0:T(8,128)(2,1)}, bf16[2,1536,1024]{2,1,0:T(8,128)(2,1)}, u32[]{:S(2)}, u32[]{:S(2)}) collective-permute-start(bf16[2,1536,1024]{2,1,0:T(8,128)(2,1)} %attend_back.3.refs_0_), channel_id=1, source_target_pairs={{0,1},{1,0},{2,3},{3,2},{4,5},{5,4},{6,7},{7,6},{8,9},{9,8},{10,11... | collective-permute-start | bytes 18874376 | tf_op jit(solution)/shard_map/ppermute | solution.py:993
  620.7 4.0 collective-permute-start.12
  625.5 42.0 %collective-permute-done.12.refs_4_ = bf16[1,768,1024]{2,1,0:T(8,128)(2,1)S(1)} collective-permute-done((bf16[1,768,1024]{2,1,0:T(8,128)(2,1)S(1)}, bf16[1,768,1024]{2,1,0:T(8,128)(2,1)S(1)}, u32[]{:S(2)}, u32[]{:S(2)}) %collective-permute-start.12) | collective-permute-done | bytes 1572896 | tf_op jit(solution)/shard_map/ppermute | solution.py:990
  670.1 26.9 %adapt_back.1 = (bf16[4,1152,960]{2,1,0:T(8,128)(2,1)}, bf16[1152,384]{1,0:T(8,128)(2,1)}, bf16[8,4,144,128]{3,2,1,0:T(8,128)(2,1)}, bf16[3,1280,128]{2,1,0:T(8,128)(2,1)}) custom-call(s32[3]{0:T(128)} %broadcast_select_fusion.4.sets, f32[3]{0:T(128)} %broadcast_select_fusion.3.scales, s32[36]{0:T(128)} %reshape.387.code, ...), custom_call_target="tpu_custom_call" | custom-call | flops 3397386240 | bytes 17694720 | tf_op jit(solution)/shard_map/adapt_back/pallas_call | solution.py:481
  701.1 2.1 collective-permute-start.16
  707.6 28.6 %project_back.1 = bf16[1152,1280]{1,0:T(8,128)(2,1)} custom-call(bf16[4,1152,960]{2,1,0:T(8,128)(2,1)} %get-tuple-element.91.dy_ref, bf16[8,4,240,960]{3,2,1,0:T(8,128)(2,1)} %bitcast.138, bf16[1152,384]{1,0:T(8,128)(2,1)} %get-tuple-element.92.grank_ref, bf16[1280,768]{1,0:T(8,128)(2,1)} %bitcast.146, bf16[1152,1280]{1,0:T(8,128)(2,1)} %x_ref.3, ...), custom_call_target="tpu_custom_call" | custom-call | flops 12457082880 | bytes 30474240 | tf_op jit(solution)/shard_map/project_back/pallas_call | solution.py:546
  736.2 63.7 %reduce-scatter.8.cloned.1.call-done = bf16[264,128]{1,0:T(8,128)(2,1)} async-done(((bf16[8448,128]{1,0:T(8,128)(2,1)}), bf16[264,128]{1,0:T(8,128)(2,1)}) %reduce-scatter.8.cloned.1.call-update) | async-done | bytes 67600
  807.8 2.3 collective-permute-done.15
  (239 shorter events, 65.9 us)
Async XLA Ops:
  7.3 120.1 %all-gather.5.cloned.1.call-start = ((), (), s32[]{:S(2)}) async-start(), calls=%async_computation.2 | async-start | bytes 16220160 | tf_op jit(solution)/shard_map/all_gather | solution.py:1111
  15.0 329.8 %all-gather.7.cloned.1.call-start = ((), (), s32[]{:S(2)}) async-start(), calls=%async_computation.3 | async-start | bytes 36495360 | tf_op jit(solution)/shard_map/all_gather | solution.py:1139
  15.2 113.7 %copy-start.23 = (f32[1280]{0:T(1024)S(1)}, f32[1280]{0:T(1024)}, u32[]{:S(2)}) copy-start(f32[1280]{0:T(1024)} %param.38) | copy-start | bytes 15364
  15.2 114.3 %copy-start.24 = (f32[1280]{0:T(1024)S(1)}, f32[1280]{0:T(1024)}, u32[]{:S(2)}) copy-start(f32[1280]{0:T(1024)} %param.39) | copy-start | bytes 15364
  127.4 572.7 %reduce-scatter.10.cloned.1.call-start = ((), (), s32[]{:S(2)}) async-start(), calls=%async_computation.5 | async-start | bytes 4122624
  165.7 9.8 %collective-permute-start = (bf16[2,1152,1024]{2,1,0:T(8,128)(2,1)}, bf16[2,1152,1024]{2,1,0:T(8,128)(2,1)}, u32[]{:S(2)}, u32[]{:S(2)}) collective-permute-start(bf16[2,1152,1024]{2,1,0:T(8,128)(2,1)} %get-tuple-element.57), channel_id=1, source_target_pairs={{0,1},{1,0},{2,3},{3,2},{4,5},{5,4},{6,7},{7,6},{8,9},{9,8},{10,11... | collective-permute-start | bytes 14155784 | tf_op jit(solution)/shard_map/ppermute | solution.py:974
  170.6 56.2 %collective-permute-start.1 = (bf16[1,768,1024]{2,1,0:T(8,128)(2,1)S(1)}, bf16[1,768,1024]{2,1,0:T(8,128)(2,1)}, u32[]{:S(2)}, u32[]{:S(2)}) collective-permute-start(bf16[1,768,1024]{2,1,0:T(8,128)(2,1)S(1)} %constant_dynamic-slice_fusion.9), channel_id=1, source_target_pairs={{1,3},{2,0},{5,7},{6,4},{9,11},{10,8},{13,15},{14,12},{17,19},{18,... | collective-permute-start | bytes 4718600 | tf_op jit(solution)/shard_map/ppermute | solution.py:977
  173.6 53.2 %collective-permute-start.2 = (bf16[1,768,1024]{2,1,0:T(8,128)(2,1)S(1)}, bf16[1,768,1024]{2,1,0:T(8,128)(2,1)}, u32[]{:S(2)}, u32[]{:S(2)}) collective-permute-start(bf16[1,768,1024]{2,1,0:T(8,128)(2,1)S(1)} %constant_dynamic-slice_fusion.8), channel_id=1, source_target_pairs={{1,2},{2,1},{5,6},{6,5},{9,10},{10,9},{13,14},{14,13},{17,18},{18,... | collective-permute-start | bytes 4718600 | tf_op jit(solution)/shard_map/ppermute | solution.py:978
  221.7 130.2 %collective-permute-start.3 = (bf16[2,1536,384]{2,1,0:T(8,128)(2,1)}, bf16[2,1536,384]{2,1,0:T(8,128)(2,1)}, u32[]{:S(2)}, u32[]{:S(2)}) collective-permute-start(bf16[2,1536,384]{2,1,0:T(8,128)(2,1)} %get-tuple-element.58.refs_0_.refs_3_), channel_id=1, source_target_pairs={{0,1},{1,0},{2,3},{3,2},{4,5},{5,4},{6,7},{7,6},{8,9},{9,8},{10,11... | collective-permute-start | bytes 7077896 | tf_op jit(solution)/shard_map/ppermute | solution.py:993
  247.7 104.1 %collective-permute-start.4 = (bf16[1,1536,384]{2,1,0:T(8,128)(2,1)}, bf16[1,1536,384]{2,1,0:T(8,128)(2,1)S(1)}, u32[]{:S(2)}, u32[]{:S(2)}) collective-permute-start(bf16[1,1536,384]{2,1,0:T(8,128)(2,1)} %get-tuple-element.61.refs_1_.refs_5_), channel_id=1, source_target_pairs={{0,1},{1,0},{2,3},{3,2},{4,5},{5,4},{6,7},{7,6},{8,9},{9,8},{10,11... | collective-permute-start | bytes 3538952 | tf_op jit(solution)/shard_map/ppermute | solution.py:992
  248.9 102.9 %collective-permute-start.5 = (bf16[1,768,384]{2,1,0:T(8,128)(2,1)S(1)}, bf16[1,768,384]{2,1,0:T(8,128)(2,1)S(1)}, u32[]{:S(2)}, u32[]{:S(2)}) collective-permute-start(bf16[1,768,384]{2,1,0:T(8,128)(2,1)S(1)} %constant_dynamic-slice_fusion.7), channel_id=1, source_target_pairs={{3,1},{0,2},{7,5},{4,6},{11,9},{8,10},{15,13},{12,14},{19,17},{16,... | collective-permute-start | bytes 1769480 | tf_op jit(solution)/shard_map/ppermute | solution.py:990
  253.7 98.1 %collective-permute-start.6 = (bf16[1,768,384]{2,1,0:T(8,128)(2,1)S(1)}, bf16[1,768,384]{2,1,0:T(8,128)(2,1)S(1)}, u32[]{:S(2)}, u32[]{:S(2)}) collective-permute-start(bf16[1,768,384]{2,1,0:T(8,128)(2,1)S(1)} %constant_dynamic-slice_fusion.7), channel_id=1, source_target_pairs={{2,1},{1,2},{6,5},{5,6},{10,9},{9,10},{14,13},{13,14},{18,17},{17,... | collective-permute-start | bytes 1769480 | tf_op jit(solution)/shard_map/ppermute | solution.py:991
  509.5 13.0 %collective-permute-start.7 = (bf16[2,1152,384]{2,1,0:T(8,128)(2,1)S(1)}, bf16[2,1152,384]{2,1,0:T(8,128)(2,1)}, u32[]{:S(2)}, u32[]{:S(2)}) collective-permute-start(bf16[2,1152,384]{2,1,0:T(8,128)(2,1)S(1)} %copy-done.14), channel_id=1, source_target_pairs={{0,1},{1,0},{2,3},{3,2},{4,5},{5,4},{6,7},{7,6},{8,9},{9,8},{10,11... | collective-permute-start | bytes 5308424 | tf_op jit(solution)/shard_map/ppermute | solution.py:974
  510.7 11.8 %collective-permute-start.8 = (bf16[1,768,384]{2,1,0:T(8,128)(2,1)S(1)}, bf16[1,768,384]{2,1,0:T(8,128)(2,1)S(1)}, u32[]{:S(2)}, u32[]{:S(2)}) collective-permute-start(bf16[1,768,384]{2,1,0:T(8,128)(2,1)S(1)} %constant_dynamic-slice_fusion.6), channel_id=1, source_target_pairs={{1,3},{2,0},{5,7},{6,4},{9,11},{10,8},{13,15},{14,12},{17,19},{18,... | collective-permute-start | bytes 1769480 | tf_op jit(solution)/shard_map/ppermute | solution.py:977
  512.0 10.5 %collective-permute-start.9 = (bf16[1,768,384]{2,1,0:T(8,128)(2,1)S(1)}, bf16[1,768,384]{2,1,0:T(8,128)(2,1)}, u32[]{:S(2)}, u32[]{:S(2)}) collective-permute-start(bf16[1,768,384]{2,1,0:T(8,128)(2,1)S(1)} %constant_dynamic-slice_fusion.5), channel_id=1, source_target_pairs={{1,2},{2,1},{5,6},{6,5},{9,10},{10,9},{13,14},{14,13},{17,18},{18,... | collective-permute-start | bytes 1769480 | tf_op jit(solution)/shard_map/ppermute | solution.py:978
  513.5 286.4 %reduce-scatter.8.cloned.1.call-start = ((), (), s32[]{:S(2)}) async-start(), calls=%async_computation.4 | async-start | bytes 2230272
  611.7 57.5 %collective-permute-start.10 = (bf16[2,1536,1024]{2,1,0:T(8,128)(2,1)}, bf16[2,1536,1024]{2,1,0:T(8,128)(2,1)}, u32[]{:S(2)}, u32[]{:S(2)}) collective-permute-start(bf16[2,1536,1024]{2,1,0:T(8,128)(2,1)} %attend_back.3.refs_0_), channel_id=1, source_target_pairs={{0,1},{1,0},{2,3},{3,2},{4,5},{5,4},{6,7},{7,6},{8,9},{9,8},{10,11... | collective-permute-start | bytes 18874376 | tf_op jit(solution)/shard_map/ppermute | solution.py:993
  620.5 47.0 %collective-permute-start.11 = (bf16[1,1536,1024]{2,1,0:T(8,128)(2,1)S(1)}, bf16[1,1536,1024]{2,1,0:T(8,128)(2,1)S(1)}, u32[]{:S(2)}, u32[]{:S(2)}) collective-permute-start(bf16[1,1536,1024]{2,1,0:T(8,128)(2,1)S(1)} %copy-done.2), channel_id=1, source_target_pairs={{0,1},{1,0},{2,3},{3,2},{4,5},{5,4},{6,7},{7,6},{8,9},{9,8},{10,11... | collective-permute-start | bytes 9437192 | tf_op jit(solution)/shard_map/ppermute | solution.py:992
  620.7 46.8 %collective-permute-start.12 = (bf16[1,768,1024]{2,1,0:T(8,128)(2,1)S(1)}, bf16[1,768,1024]{2,1,0:T(8,128)(2,1)S(1)}, u32[]{:S(2)}, u32[]{:S(2)}) collective-permute-start(bf16[1,768,1024]{2,1,0:T(8,128)(2,1)S(1)} %constant_dynamic-slice_fusion.4), channel_id=1, source_target_pairs={{3,1},{0,2},{7,5},{4,6},{11,9},{8,10},{15,13},{12,14},{19,17},{16,... | collective-permute-start | bytes 4718600 | tf_op jit(solution)/shard_map/ppermute | solution.py:990
  624.7 42.8 %collective-permute-start.13 = (bf16[1,768,1024]{2,1,0:T(8,128)(2,1)S(1)}, bf16[1,768,1024]{2,1,0:T(8,128)(2,1)S(1)}, u32[]{:S(2)}, u32[]{:S(2)}) collective-permute-start(bf16[1,768,1024]{2,1,0:T(8,128)(2,1)S(1)} %constant_dynamic-slice_fusion.4), channel_id=1, source_target_pairs={{2,1},{1,2},{6,5},{5,6},{10,9},{9,10},{14,13},{13,14},{18,17},{17,... | collective-permute-start | bytes 4718600 | tf_op jit(solution)/shard_map/ppermute | solution.py:991
  701.1 5.7 collective-permute-start.16
  706.9 29.3 %collective-permute-start.17 = (f32[2,120,128]{2,1,0:T(8,128)S(1)}, f32[2,120,128]{2,1,0:T(8,128)S(1)}, u32[]{:S(2)}, u32[]{:S(2)}) collective-permute-start(f32[2,120,128]{2,1,0:T(8,128)S(1)} %constant_dynamic-slice_fusion), channel_id=1, source_target_pairs={{0,2},{1,3},{2,0},{3,1},{4,6},{5,7},{6,4},{7,5},{8,10},{9,11},{10,... | collective-permute-start | bytes 368648 | tf_op jit(solution)/shard_map/ppermute | solution.py:1024
  800.9 3.4 collective-permute-start.14
  804.3 5.8 collective-permute-start.15
  (32 other events, 703.7 us)
Sparse Core Ops, SparseCore 0:
  15.1 112.2 all-gather.4
  130.9 213.9 all-gather.6
  513.6 150.7 reduce-scatter.9
  700.2 99.6 reduce-scatter.7

commit v3 on v2

--- a/solution.py
+++ b/solution.py
@@ -406,9 +406,18 @@
         ref[:, 0, at : at + group, :] = tile.astype(BF)
 
 
-def adapt_back_kernel(tm, width, group, per, ns, nm, sets, scales, code, *refs):
+def fold_sets(turned, group, per):
+    wide = turned.shape[0]
+    row = lax.broadcasted_iota(jnp.int32, (RANK, wide), 0)
+    column = lax.broadcasted_iota(jnp.int32, (RANK, wide), 1)
+    match = (column // group == row // per) & (column % per == row % per)
+    return dot(jnp.where(match, 1.0, 0.0).astype(BF), turned).astype(BF)
+
+
+def adapt_back_kernel(tm, width, group, per, ns, nm, sets, scales, slots, code, *refs):
     sources = refs[:ns]
     up, normed_ref, ranks_ref, dy_ref, grank_ref, gup_ref, gdown_ref, racc, gup, gdown = refs[ns:]
+    slot = slots[pl.program_id(1)]
     c = pl.program_id(0)
     m = pl.program_id(1)
     last = c == pl.num_programs(0) - 1
@@ -431,45 +440,48 @@
         racc[rows, :] += rpart
 
     turned = ranks_ref[...].T
+
+    @pl.when(m == 0)
+    def _():
+        gup[...] = jnp.zeros_like(gup)
+
     for j in range(3):
-        part = dot(turned[j * wide : (j + 1) * wide], pieces[j])
-
-        @pl.when(m == 0)
-        def _(j=j, part=part):
-            gup[j] = part
-
-        @pl.when(m > 0)
-        def _(j=j, part=part):
-            gup[j] += part
+        gup[slot, j] += dot(fold_sets(turned[j * wide : (j + 1) * wide], group, per), pieces[j])
 
     @pl.when(m == nm - 1)
     def _():
         tiles = -(-width // 128)
-        for j in range(3):
-            put_tiles(gup_ref, j * tiles, gup[j], group)
+        clips = gup.shape[0]
+        for i in range(clips):
+            for j in range(3):
+                for t, tile in enumerate(lane_tiles(gup[i, j], RANK)):
+                    gup_ref[0, (i * 3 + j) * tiles + t] = tile[0].astype(BF)
 
     @pl.when(last)
     def _():
         grank = racc[rows, :] * scales[m]
         grank = jnp.where(set_mask(grank.shape, sets[m], group, per), grank, 0.0)
         grank_ref[...] = grank.astype(BF)
-        part = token_sum(grank, normed_ref[...])
+        turned = grank.T.astype(BF)
 
         @pl.when(m == 0)
         def _():
-            gdown[...] = part
-
-        @pl.when(m > 0)
-        def _():
-            gdown[...] += part
+            gdown[...] = jnp.zeros_like(gdown)
+
+        for j in range(3):
+            part = dot(fold_sets(turned[j * wide : (j + 1) * wide], group, per), normed_ref[...])
+            gdown[slot, j * RANK : (j + 1) * RANK] += part
 
         @pl.when(m == nm - 1)
         def _():
-            for j in range(3):
-                gdown_ref[j] = gdown[j * wide : (j + 1) * wide, :].T.astype(BF)
-
-
-def adapt_back(sources, code, gathered, normed, ranks, sets, scales, tm, per):
+            whole = gdown[...].reshape(-1, D)
+            pad = gdown_ref.shape[0] * 128 - whole.shape[0]
+            whole = jnp.concatenate([whole, jnp.zeros((pad, D), F32)], axis=0)
+            for i in range(gdown_ref.shape[0]):
+                gdown_ref[i] = whole[i * 128 : (i + 1) * 128].T.astype(BF)
+
+
+def adapt_back(sources, code, gathered, normed, ranks, sets, scales, slots, clips, tm, per):
     own = normed.shape[0]
     rr, nc, _, w3 = gathered.shape
     width = w3 // 3
@@ -477,19 +489,20 @@
     wide = group * rr
     nm = own // tm
     tiles = 3 * -(-width // 128)
+    folded = -(-clips * 3 * RANK // 128)
     final = lambda c, m, *_: (jnp.where(c == nc - 1, m, 0), 0)
     return pl.pallas_call(
         functools.partial(adapt_back_kernel, tm, width, group, per, len(sources), nm),
         out_shape=(
             jax.ShapeDtypeStruct((nc, own, w3), BF),
             jax.ShapeDtypeStruct((own, 3 * wide), BF),
-            jax.ShapeDtypeStruct((rr, nc, tiles * group, 128), BF),
-            jax.ShapeDtypeStruct((3, D, wide), BF),
+            jax.ShapeDtypeStruct((nc, clips * tiles, RANK, 128), BF),
+            jax.ShapeDtypeStruct((folded, D, 128), BF),
         ),
         grid_spec=pltpu.PrefetchScalarGridSpec(
-            num_scalar_prefetch=3,
+            num_scalar_prefetch=4,
             grid=(nc, nm),
-            in_specs=piece_specs(sources, tm, lambda c, m, s, a: c * nm + m)
+            in_specs=piece_specs(sources, tm, lambda c, m, s, a, i: c * nm + m)
             + [
                 pl.BlockSpec((rr, 1, group, w3), lambda c, m, *_: (0, c, D // rr // group, 0)),
                 pl.BlockSpec((tm, D), final),
@@ -498,19 +511,19 @@
             out_specs=[
                 pl.BlockSpec((1, tm, w3), lambda c, m, *_: (c, m, 0)),
                 pl.BlockSpec((tm, 3 * wide), final),
-                pl.BlockSpec((rr, 1, tiles * group, 128), lambda c, m, *_: (0, c, 0, 0)),
-                pl.BlockSpec((3, D, wide), lambda c, m, *_: (0, 0, 0)),
+                pl.BlockSpec((1, clips * tiles, RANK, 128), lambda c, m, *_: (c, 0, 0, 0)),
+                pl.BlockSpec((folded, D, 128), lambda c, m, *_: (0, 0, 0)),
             ],
             scratch_shapes=[
                 pltpu.VMEM((own, 3 * wide), F32),
-                pltpu.VMEM((3, wide, width), F32),
-                pltpu.VMEM((3 * wide, D), F32),
+                pltpu.VMEM((clips, 3, RANK, width), F32),
+                pltpu.VMEM((clips, 3 * RANK, D), F32),
             ],
         ),
         compiler_params=params(2),
         cost_estimate=cost(own * D * nc * w3 * 0.6, own * nc * w3 * 4),
         name="adapt_back",
-    )(sets, scales, code, *sources, gathered, normed, ranks)
+    )(sets, scales, slots, code, *sources, gathered, normed, ranks)
 
 
 def project_back_kernel(tm, width, dy_ref, w_ref, grank_ref, down, x_ref, gm_ref, gain, gt_ref, acc):
@@ -1094,16 +1107,21 @@
     qh, ql = halves(query_bias)
     vh, vl = halves(value_bias)
     none = jnp.zeros_like(qh)
+    ids = jnp.pad(clip_sets.astype(BF), (0, lanes - clips))
     natural = lanes >= 6 * wide
     small = rows_padded(tables, dc, lanes) if natural else tables.reshape(-1, lanes)
     small_rows = small.shape[0]
     at_bias = dr + group
-    at_table = up_to(at_bias + 2, 16)
+    at_table = up_to(at_bias + 3, 16)
     packed = jnp.concatenate(
         [
             jnp.concatenate([w_query, w_key, w_value], axis=1),
             jnp.concatenate([v.reshape(group, width) for v in (query_up, key_up, value_up)], axis=1),
-            rows_padded(jnp.stack([jnp.concatenate([qh, none, vh]), jnp.concatenate([ql, none, vl])]), at_table - at_bias, lanes),
+            rows_padded(
+                jnp.stack([jnp.concatenate([qh, none, vh]), jnp.concatenate([ql, none, vl]), ids]),
+                at_table - at_bias,
+                lanes,
+            ),
             rows_padded(small, up_to(small_rows, 16), lanes),
         ],
         axis=0,
@@ -1113,6 +1131,7 @@
     if natural:
         tables = tables[..., : 6 * wide]
     tables = tables.reshape(D, 6 * wide)
+    every_set = g1[:, 0, at_bias + 2, :clips].astype(jnp.int32)
     bias_qkv = jnp.sum(g1[0, :, at_bias : at_bias + 2].astype(F32), axis=1, keepdims=True)
 
     parts = hidden // width
@@ -1168,7 +1187,7 @@
     by_model = lambda v: v.reshape(nr, nc, dc, wide)
     late = scatter_sum([gup1, gdown2, godown, by_model(gdown1), by_model(goup), by_model(gup2)])
     late, away, mine = lax.optimization_barrier((late, away, mine))
-    summed = lax.psum_scatter(late, BOTH, scatter_dimension=0, tiled=True).astype(F32)
+    late = lax.psum_scatter(late, BOTH, scatter_dimension=0, tiled=True)
 
     def untile(v, n):
         t = v.shape[0] // group
@@ -1182,14 +1201,6 @@
     as_down = lambda v: v.transpose(2, 0, 1, 3).reshape(SETS, dr, RANK)
     as_up = lambda v: v.transpose(2, 1, 3, 0).reshape(SETS, RANK, dr)
     flip = lambda v: jnp.swapaxes(v, 1, 2)
-    a = gup1.shape[2]
-    b = godown.shape[2]
-    grad_fc1_up = untile(summed[:a], hidden)
-    grad_fc2_down = flip(untile(summed[a : 2 * a], hidden))
-    grad_out_down = flip(untile(summed[2 * a : 2 * a + b], width))
-    model = model_tables(summed[2 * a + b : 2 * a + b + 3 * dc])
-    grad_fc1_down, grad_out_up, grad_fc2_up = as_down(model[0]), as_up(model[1]), as_up(model[2])
-
     calls = list(
         zip(exchange.to_heads(away, mine), exchange.plans, exchange.indices, results, lens)
     )
@@ -1200,16 +1211,41 @@
         backs.append(attend_back(sources, plan, index, x, o, lse, n, hh))
     pieces = exchange.from_heads(backs[::-1])
     dy, grank, gup, gdown = adapt_back(
-        pieces, exchange.code, g1, normed, ranks, sets, scales, tm, per
+        pieces, exchange.code, g1, normed, ranks, sets, scales, block_clip, clips, tm, per
     )
-    last = scatter_sum([gup] + [by_model(gdown[j]) for j in range(3)])
+    tiles = gup.shape[1] // (3 * clips)
+    folded = gdown.shape[0]
+    ups = gup.reshape(nc, clips * 3 * tiles, nr, per, 128).transpose(2, 0, 1, 3, 4)
+    ups = ups.reshape(nr, nc, -1, 128)
+    downs = [gdown[i].reshape(nr, nc, dc, 128) for i in range(folded)]
+    last = scatter_sum([ups] + downs).reshape(nr * nc, -1, 128)
     last, dy = lax.optimization_barrier((last, dy))
-    summed = lax.psum_scatter(last, BOTH, scatter_dimension=0, tiled=True).astype(F32)
+    got = lax.all_to_all(last, BOTH, 0, 0, tiled=True)
     grad_tokens = project_back(dy, g1, grank, tables, tokens, grad_middle, gain1, tm)
-    a = gup.shape[2] // 3
-    up = [untile(summed[j * a : (j + 1) * a], width) for j in range(3)]
-    model = model_tables(summed[3 * a : 3 * a + 3 * dc])
-    down = [as_down(model[j]) for j in range(3)]
+    late, grad_tokens = lax.optimization_barrier((late, grad_tokens))
+    summed = late.astype(F32)
+    a = gup1.shape[2]
+    b = godown.shape[2]
+    grad_fc1_up = untile(summed[:a], hidden)
+    grad_fc2_down = flip(untile(summed[a : 2 * a], hidden))
+    grad_out_down = flip(untile(summed[2 * a : 2 * a + b], width))
+    model = model_tables(summed[2 * a + b : 2 * a + b + 3 * dc])
+    grad_fc1_down, grad_out_up, grad_fc2_up = as_down(model[0]), as_up(model[1]), as_up(model[2])
+
+    got = jnp.sum(got.reshape(nr, nc, -1, 128).astype(F32), axis=1)
+    onehot = (every_set[:, :, None] == jnp.arange(SETS, dtype=jnp.int32)).astype(F32)
+    n = ups.shape[2]
+    per_clip = got[:, :n].reshape(nr, clips, -1, 128)
+    per_set = jnp.sum(onehot[:, :, :, None, None] * per_clip[:, :, None], axis=(0, 1))
+    per_set = per_set.reshape(SETS, 3, tiles, per, 128).transpose(1, 0, 3, 2, 4)
+    up = per_set.reshape(3, SETS, per, tiles * 128)[..., :width]
+    side = got[:, n : n + folded * dc].reshape(nr, folded, dc, 128).transpose(0, 2, 1, 3)
+    side = side.reshape(nr, dc, folded * 128)[..., : clips * 3 * RANK]
+    side = side.reshape(nr, dc, clips, 3 * RANK).transpose(0, 2, 1, 3)
+    side = jnp.sum(onehot[:, :, :, None, None] * side[:, :, None], axis=(0, 1))
+    side = side.transpose(1, 0, 2).reshape(dc, SETS * 3 * RANK)
+    side = lax.all_gather(side, "cols", axis=0, tiled=True).reshape(dr, SETS, 3, RANK)
+    down = side.transpose(2, 1, 0, 3)
     return (
         output,
         grad_tokens,

time: 826 us -> 819 us (level)
  waiting for transfers between devices: 316 us -> 283 us
  starting transfers between devices: 34 us -> 59.5 us
    unnamed x6 -> x3, waiting for transfers between devices: 63.8 us -> 0.05 us
    optimization_barrier x0 -> x1, waiting for transfers between devices: none -> 31 us  [body(): late, grad_tokens = lax.optimization_barrier((late, grad_tokens))]
    all_to_all x0 -> x1, starting transfers between devices: none -> 30.9 us  [body(): got = lax.all_to_all(last, BOTH, 0, 0, tiled=True)]
    unnamed x85 -> x94, local copies, waits for them, and re-layouts: 18 us -> 16.5 us
  transfers between devices with their start and end apart: 22 -> 20, of which waited for: 6 -> 7; matrix products, arithmetic and copies ran while one was open for 4% -> 4% of each run, Pallas kernels for 30% -> 19%
where the time goes in v3:
time: 819 us; the launch traced here: 813 us
  Pallas kernels  391 us (48%)
  waiting for transfers between devices  283 us (35%)
  starting transfers between devices  59.5 us (7%)
  local copies, waits for them, and re-layouts  47.4 us (6%)
  between operations  16.6 us (2%)
  other arithmetic  10.4 us (1%)
    all_gather x1, waiting for transfers between devices, body(): g1 = lax.all_gather(packed, BOTH, axis=0).reshape(nr, nc, -1, lanes)  112 us
    pallas_call x1, Pallas kernels, mlp(): pl.pallas_call(functools.partial(mlp_kernel, tm, nm, group, per), out_sha...  105 us
    pallas_call x2, Pallas kernels, attend_back(): pl.pallas_call(functools.partial(attend_back_kernel, hh, length, qb, kb,...  88.4 us
    all_gather x1, waiting for transfers between devices, body(): g2 = lax.all_gather(packed, BOTH, axis=0).reshape(nr, nc, -1, hidden)  87.1 us
    pallas_call x2, Pallas kernels, attend(): pl.pallas_call(functools.partial(attend_kernel, hh, length, qb, kb, len(s...  67.1 us
    ppermute x2, waiting for transfers between devices, from_heads(): got_one = lax.ppermute(far, 'cols', [(3, 1), (0, 2)])  39.9 us
    optimization_barrier x1, waiting for transfers between devices, body(): late, grad_tokens = lax.optimization_barrier((late, grad_tokens))  31 us
    all_to_all x1, starting transfers between devices, body(): got = lax.all_to_all(last, BOTH, 0, 0, tiled=True)  30.9 us
  transfers between devices with their start and end apart: 20, of which 7 were waited for; matrix products, arithmetic and copies ran while one was open for 4% of the time, Pallas kernels for 19%

profile of v3, /device:TPU:0, one launch (start us, length us, event | category | flops | bytes accessed | tf_op | source)
XLA Modules:
  0.0 813.0 jit_solution(5898543405118795297)
XLA Ops:
  12.9 111.8 %all-gather.5.cloned.1.call-done = bf16[7680,960]{1,0:T(8,128)(2,1)} async-done(((bf16[240,960]{1,0:T(8,128)(2,1)}), bf16[7680,960]{1,0:T(8,128)(2,1)}) %all-gather.5.cloned.1.call-update) | async-done | bytes 14745616 | tf_op jit(solution)/shard_map/all_gather | solution.py:1129
  128.9 3.0 slice.118
  133.4 29.7 %project.1 = (bf16[1152,1280]{1,0:T(8,128)(2,1)}, bf16[1152,384]{1,0:T(8,128)(2,1)}, bf16[2,1152,1024]{2,1,0:T(8,128)(2,1)}, bf16[2,1152,1024]{2,1,0:T(8,128)(2,1)}) custom-call(s32[3]{0:T(128)} %broadcast_select_fusion.4.sets, f32[3]{0:T(128)} %broadcast_select_fusion.3.scales, s32[4]{0:T(128)} %and_select_fusion.4.order, bf16[1152,1280]{1,0:T(8,128)(2,1)} %x_ref.3, ...), custom_call_target="tpu_custom_call" | custom-call | flops 14722007040 | bytes 24576000 | tf_op jit(solution)/shard_map/project/pallas_call | solution.py:338
  172.9 46.1 %attend.2 = (bf16[2,1536,384]{2,1,0:T(8,128)(2,1)}, f32[2,4,1536]{2,1,0:T(4,128)}, bf16[2,1536,960]{2,1,0:T(8,128)(2,1)}) custom-call(s32[2]{0:T(128)} %pad_add_fusion.1.lens, s32[8]{0:T(128)} %pad_add_fusion.2.plan, s32[4]{0:T(128)} %constant.177.clone.index, bf16[2,1152,1024]{2,1,0:T(8,128)(2,1)} %get-tuple-element.58.refs_0_, ...), custom_call_target="tpu_custom_call" | custom-call | flops 19327352832 | bytes 17694720 | tf_op jit(solution)/shard_map/attend/pallas_call | solution.py:152
  219.0 4.0 collective-permute-start.3
  224.2 21.0 %attend.3 = (bf16[1,1536,384]{2,1,0:T(8,128)(2,1)}, f32[1,4,1536]{2,1,0:T(4,128)}, bf16[1,1536,960]{2,1,0:T(8,128)(2,1)}) custom-call(s32[1]{0:T(128)} %get-tuple-element.62.lens, s32[8]{0:T(128)} %pad_add_fusion.3.plan, s32[4]{0:T(128)} %get-tuple-element.197.index, bf16[2,1152,1024]{2,1,0:T(8,128)(2,1)} %get-tuple-element.58.refs_0_, ...), custom_call_target="tpu_custom_call" | custom-call | flops 9663676416 | bytes 8847360 | tf_op jit(solution)/shard_map/attend/pallas_call | solution.py:152
  246.3 4.8 collective-permute-start.5
  255.0 87.1 %all-gather.7.cloned.1.call-done = bf16[13824,1280]{1,0:T(8,128)(2,1)} async-done(((bf16[432,1280]{1,0:T(8,128)(2,1)}), bf16[13824,1280]{1,0:T(8,128)(2,1)}) %all-gather.7.cloned.1.call-update) | async-done | bytes 35389456 | tf_op jit(solution)/shard_map/all_gather | solution.py:1158
  342.1 5.3 assemble.1
  350.4 23.9 %out_project.1 = (bf16[1152,1280]{1,0:T(8,128)(2,1)}, f32[1152,1280]{1,0:T(8,128)}, bf16[1152,1280]{1,0:T(8,128)(2,1)}, bf16[1152,128]{1,0:T(8,128)(2,1)}, bf16[1152,128]{1,0:T(8,128)(2,1)}) custom-call(s32[3]{0:T(128)} %broadcast_select_fusion.4.sets, f32[3]{0:T(128)} %broadcast_select_fusion.3.scales, s32[36]{0:T(128)} %reshape.381.code, ...), custom_call_target="tpu_custom_call" | custom-call | flops 5662310400 | bytes 20971520 | tf_op jit(solution)/shard_map/out_project/pallas_call | solution.py:612
  374.3 104.9 %mlp.1 = (bf16[1152,1280]{1,0:T(8,128)(2,1)}, f32[1152,1280]{1,0:T(8,128)}, bf16[1152,1280]{1,0:T(8,128)(2,1)}, bf16[8,4,160,128]{3,2,1,0:T(8,128)(2,1)}, bf16[8...) custom-call(s32[3]{0:T(128)} %broadcast_select_fusion.4.sets, ...), custom_call_target="tpu_custom_call" | custom-call | flops 72477573120 | bytes 70451200 | tf_op jit(solution)/shard_map/mlp/pallas_call | solution.py:819
  479.2 2.7 constant_dynamic-update-slice_fusion.8
  483.2 18.1 %out_back.1 = (bf16[2,1152,384]{2,1,0:T(8,128)(2,1)}, bf16[2,1152,384]{2,1,0:T(8,128)(2,1)}, bf16[1280,128]{1,0:T(8,128)(2,1)}, bf16[8,4,48,128]{3,2,1,0:T(8,128)(2,1)}) custom-call(s32[3]{0:T(128)} %broadcast_select_fusion.4.sets, f32[3]{0:T(128)} %broadcast_select_fusion.3.scales, s32[1]{0:T(128)} %bitcast.26.side, ...), custom_call_target="tpu_custom_call" | custom-call | flops 5662310400 | bytes 12124160 | tf_op jit(solution)/shard_map/out_back/pallas_call | solution.py:696
  510.0 9.8 %collective-permute-done.8.refs_2_ = bf16[1,768,384]{2,1,0:T(8,128)(2,1)S(1)} collective-permute-done((bf16[1,768,384]{2,1,0:T(8,128)(2,1)S(1)}, bf16[1,768,384]{2,1,0:T(8,128)(2,1)S(1)}, u32[]{:S(2)}, u32[]{:S(2)}) %collective-permute-start.8) | collective-permute-done | bytes 589856 | tf_op jit(solution)/shard_map/ppermute | solution.py:990
  521.9 21.0 %attend_back.2.refs_1_ = bf16[1,1536,1024]{2,1,0:T(8,128)(2,1)} custom-call(s32[1]{0:T(128)} %get-tuple-element.62.lens, s32[8]{0:T(128)} %pad_add_fusion.3.plan, s32[4]{0:T(128)} %get-tuple-element.197.index, bf16[2,1152,384]{2,1,0:T(8,128)(2,1)} %get-tuple-element.83.refs_0_, bf16[2,1152,384]{2,1,0:T(8,128)(2,1)} %copy-done.32, ...), custom_call_target="tpu_custom_call" | custom-call | flops 24159191040 | bytes 8847360 | tf_op jit(solution)/shard_map/attend_back/pallas_call | solution.py:258
  542.9 67.3 %attend_back.3.refs_0_ = bf16[2,1536,1024]{2,1,0:T(8,128)(2,1)} custom-call(s32[2]{0:T(128)} %pad_add_fusion.1.lens, s32[8]{0:T(128)} %pad_add_fusion.2.plan, s32[4]{0:T(128)} %constant.177.clone.index, bf16[2,1152,384]{2,1,0:T(8,128)(2,1)} %get-tuple-element.83.refs_0_, bf16[2,1152,384]{2,1,0:T(8,128)(2,1)} %copy-done.32, ...), custom_call_target="tpu_custom_call" | custom-call | flops 48318382080 | bytes 17694720 | tf_op jit(solution)/shard_map/attend_back/pallas_call | solution.py:258
  610.2 5.5 collective-permute-start.10
  618.8 4.2 collective-permute-start.12
  626.1 39.9 %collective-permute-done.12.refs_4_ = bf16[1,768,1024]{2,1,0:T(8,128)(2,1)} collective-permute-done((bf16[1,768,1024]{2,1,0:T(8,128)(2,1)}, bf16[1,768,1024]{2,1,0:T(8,128)(2,1)}, u32[]{:S(2)}, u32[]{:S(2)}) %collective-permute-start.12) | collective-permute-done | bytes 1572896 | tf_op jit(solution)/shard_map/ppermute | solution.py:1003
  666.0 25.0 %adapt_back.1 = (bf16[4,1152,960]{2,1,0:T(8,128)(2,1)}, bf16[1152,384]{1,0:T(8,128)(2,1)}, bf16[4,27,16,128]{3,2,1,0:T(8,128)(2,1)}, bf16[2,1280,128]{2,1,0:T(8,128)(2,1)}) custom-call(s32[3]{0:T(128)} %broadcast_select_fusion.4.sets, f32[3]{0:T(128)} %broadcast_select_fusion.3.scales, s32[3]{0:T(128)} %and_select_fusion.12.slots, s32[36]{0:T(128)} %reshape.381.code, ...), custom_call_target="tpu_custom_call" | custom-call | flops 3397386240 | bytes 17694720 | tf_op jit(solution)/shard_map/adapt_back/pallas_call | solution.py:494
  693.9 30.9 %all-to-all-start = ((bf16[32,136,128]{2,1,0:T(8,128)(2,1)}), bf16[32,136,128]{2,1,0:T(8,128)(2,1)S(1)}, u32[]{:S(2)}, u32[]{:S(2)}) async-start(bf16[32,136,128]{2,1,0:T(8,128)(2,1)} %bitcast.36), calls=%async_computation | async-start | bytes 2228224 | tf_op jit(solution)/shard_map/all_to_all | solution.py:1223
  724.9 28.5 %project_back.1 = bf16[1152,1280]{1,0:T(8,128)(2,1)} custom-call(bf16[4,1152,960]{2,1,0:T(8,128)(2,1)} %get-tuple-element.94.dy_ref, bf16[8,4,240,960]{3,2,1,0:T(8,128)(2,1)} %bitcast.133, bf16[1152,384]{1,0:T(8,128)(2,1)} %get-tuple-element.95.grank_ref, bf16[1280,768]{1,0:T(8,128)(2,1)} %bitcast.141, bf16[1152,1280]{1,0:T(8,128)(2,1)} %x_ref.3, ...), custom_call_target="tpu_custom_call" | custom-call | flops 12457082880 | bytes 30474240 | tf_op jit(solution)/shard_map/project_back/pallas_call | solution.py:559
  753.4 31.0 %reduce-scatter.5.cloned.1.call-done = bf16[488,128]{1,0:T(8,128)(2,1)} async-done(((bf16[15616,128]{1,0:T(8,128)(2,1)}), bf16[488,128]{1,0:T(8,128)(2,1)}) %reduce-scatter.5.cloned.1.call-update) | async-done | bytes 124944 | tf_op jit(solution)/shard_map/optimization_barrier | solution.py:1225
  797.1 5.7 all_gather.19
  (248 shorter events, 65.2 us)
Async XLA Ops:
  7.3 117.4 %all-gather.5.cloned.1.call-start = ((), (), s32[]{:S(2)}) async-start(), calls=%async_computation.2 | async-start | bytes 16220160 | tf_op jit(solution)/shard_map/all_gather | solution.py:1129
  12.3 329.9 %all-gather.7.cloned.1.call-start = ((), (), s32[]{:S(2)}) async-start(), calls=%async_computation.3 | async-start | bytes 36495360 | tf_op jit(solution)/shard_map/all_gather | solution.py:1158
  12.7 112.8 %copy-start.1 = (f32[3]{0:T(128)S(1)}, f32[3]{0:T(128)}, u32[]{:S(2)}) copy-start(f32[3]{0:T(128)} %param.37) | copy-start | bytes 40
  12.7 113.4 %copy-start.23 = (f32[1280]{0:T(1024)S(1)}, f32[1280]{0:T(1024)}, u32[]{:S(2)}) copy-start(f32[1280]{0:T(1024)} %param.38) | copy-start | bytes 15364
  12.7 113.9 %copy-start.24 = (f32[1280]{0:T(1024)S(1)}, f32[1280]{0:T(1024)}, u32[]{:S(2)}) copy-start(f32[1280]{0:T(1024)} %param.39) | copy-start | bytes 15364
  12.9 111.8 %copy-start.4 = (bf16[432,1280]{1,0:T(8,128)(2,1)}, bf16[432,1280]{1,0:T(8,128)(2,1)S(1)}, u32[]{:S(2)}) copy-start(bf16[432,1280]{1,0:T(8,128)(2,1)S(1)} %fusion.16) | copy-start | bytes 3317764
  124.7 659.7 %reduce-scatter.5.cloned.1.call-start = ((), (), s32[]{:S(2)}) async-start(), calls=%async_computation.4 | async-start | bytes 4122624
  163.0 9.8 %collective-permute-start = (bf16[2,1152,1024]{2,1,0:T(8,128)(2,1)}, bf16[2,1152,1024]{2,1,0:T(8,128)(2,1)}, u32[]{:S(2)}, u32[]{:S(2)}) collective-permute-start(bf16[2,1152,1024]{2,1,0:T(8,128)(2,1)} %get-tuple-element.59), channel_id=1, source_target_pairs={{0,1},{1,0},{2,3},{3,2},{4,5},{5,4},{6,7},{7,6},{8,9},{9,8},{10,11... | collective-permute-start | bytes 14155784 | tf_op jit(solution)/shard_map/ppermute | solution.py:987
  168.0 56.2 %collective-permute-start.1 = (bf16[1,768,1024]{2,1,0:T(8,128)(2,1)S(1)}, bf16[1,768,1024]{2,1,0:T(8,128)(2,1)}, u32[]{:S(2)}, u32[]{:S(2)}) collective-permute-start(bf16[1,768,1024]{2,1,0:T(8,128)(2,1)S(1)} %constant_dynamic-slice_fusion.7), channel_id=1, source_target_pairs={{1,3},{2,0},{5,7},{6,4},{9,11},{10,8},{13,15},{14,12},{17,19},{18,... | collective-permute-start | bytes 4718600 | tf_op jit(solution)/shard_map/ppermute | solution.py:990
  170.9 53.3 %collective-permute-start.2 = (bf16[1,768,1024]{2,1,0:T(8,128)(2,1)S(1)}, bf16[1,768,1024]{2,1,0:T(8,128)(2,1)}, u32[]{:S(2)}, u32[]{:S(2)}) collective-permute-start(bf16[1,768,1024]{2,1,0:T(8,128)(2,1)S(1)} %constant_dynamic-slice_fusion.6), channel_id=1, source_target_pairs={{1,2},{2,1},{5,6},{6,5},{9,10},{10,9},{13,14},{14,13},{17,18},{18,... | collective-permute-start | bytes 4718600 | tf_op jit(solution)/shard_map/ppermute | solution.py:991
  219.0 130.1 %collective-permute-start.3 = (bf16[2,1536,384]{2,1,0:T(8,128)(2,1)}, bf16[2,1536,384]{2,1,0:T(8,128)(2,1)}, u32[]{:S(2)}, u32[]{:S(2)}) collective-permute-start(bf16[2,1536,384]{2,1,0:T(8,128)(2,1)} %get-tuple-element.60.refs_0_.refs_3_), channel_id=1, source_target_pairs={{0,1},{1,0},{2,3},{3,2},{4,5},{5,4},{6,7},{7,6},{8,9},{9,8},{10,11... | collective-permute-start | bytes 7077896 | tf_op jit(solution)/shard_map/ppermute | solution.py:1006
  245.2 103.9 %collective-permute-start.4 = (bf16[1,1536,384]{2,1,0:T(8,128)(2,1)}, bf16[1,1536,384]{2,1,0:T(8,128)(2,1)S(1)}, u32[]{:S(2)}, u32[]{:S(2)}) collective-permute-start(bf16[1,1536,384]{2,1,0:T(8,128)(2,1)} %get-tuple-element.63.refs_1_.refs_5_), channel_id=1, source_target_pairs={{0,1},{1,0},{2,3},{3,2},{4,5},{5,4},{6,7},{7,6},{8,9},{9,8},{10,11... | collective-permute-start | bytes 3538952 | tf_op jit(solution)/shard_map/ppermute | solution.py:1005
  246.3 102.7 %collective-permute-start.5 = (bf16[1,768,384]{2,1,0:T(8,128)(2,1)S(1)}, bf16[1,768,384]{2,1,0:T(8,128)(2,1)S(1)}, u32[]{:S(2)}, u32[]{:S(2)}) collective-permute-start(bf16[1,768,384]{2,1,0:T(8,128)(2,1)S(1)} %constant_dynamic-slice_fusion.5), channel_id=1, source_target_pairs={{3,1},{0,2},{7,5},{4,6},{11,9},{8,10},{15,13},{12,14},{19,17},{16,... | collective-permute-start | bytes 1769480 | tf_op jit(solution)/shard_map/ppermute | solution.py:1003
  251.1 97.9 %collective-permute-start.6 = (bf16[1,768,384]{2,1,0:T(8,128)(2,1)S(1)}, bf16[1,768,384]{2,1,0:T(8,128)(2,1)S(1)}, u32[]{:S(2)}, u32[]{:S(2)}) collective-permute-start(bf16[1,768,384]{2,1,0:T(8,128)(2,1)S(1)} %constant_dynamic-slice_fusion.5), channel_id=1, source_target_pairs={{2,1},{1,2},{6,5},{5,6},{10,9},{9,10},{14,13},{13,14},{18,17},{17,... | collective-permute-start | bytes 1769480 | tf_op jit(solution)/shard_map/ppermute | solution.py:1004
  506.8 13.0 %collective-permute-start.7 = (bf16[2,1152,384]{2,1,0:T(8,128)(2,1)S(1)}, bf16[2,1152,384]{2,1,0:T(8,128)(2,1)S(1)}, u32[]{:S(2)}, u32[]{:S(2)}) collective-permute-start(bf16[2,1152,384]{2,1,0:T(8,128)(2,1)S(1)} %copy-done.11), channel_id=1, source_target_pairs={{0,1},{1,0},{2,3},{3,2},{4,5},{5,4},{6,7},{7,6},{8,9},{9,8},{10,11... | collective-permute-start | bytes 5308424 | tf_op jit(solution)/shard_map/ppermute | solution.py:987
  508.0 11.8 %collective-permute-start.8 = (bf16[1,768,384]{2,1,0:T(8,128)(2,1)S(1)}, bf16[1,768,384]{2,1,0:T(8,128)(2,1)S(1)}, u32[]{:S(2)}, u32[]{:S(2)}) collective-permute-start(bf16[1,768,384]{2,1,0:T(8,128)(2,1)S(1)} %constant_dynamic-slice_fusion.4), channel_id=1, source_target_pairs={{1,3},{2,0},{5,7},{6,4},{9,11},{10,8},{13,15},{14,12},{17,19},{18,... | collective-permute-start | bytes 1769480 | tf_op jit(solution)/shard_map/ppermute | solution.py:990
  509.3 10.5 %collective-permute-start.9 = (bf16[1,768,384]{2,1,0:T(8,128)(2,1)S(1)}, bf16[1,768,384]{2,1,0:T(8,128)(2,1)S(1)}, u32[]{:S(2)}, u32[]{:S(2)}) collective-permute-start(bf16[1,768,384]{2,1,0:T(8,128)(2,1)S(1)} %constant_dynamic-slice_fusion.3), channel_id=1, source_target_pairs={{1,2},{2,1},{5,6},{6,5},{9,10},{10,9},{13,14},{14,13},{17,18},{18,... | collective-permute-start | bytes 1769480 | tf_op jit(solution)/shard_map/ppermute | solution.py:991
  610.2 55.7 %collective-permute-start.10 = (bf16[2,1536,1024]{2,1,0:T(8,128)(2,1)}, bf16[2,1536,1024]{2,1,0:T(8,128)(2,1)}, u32[]{:S(2)}, u32[]{:S(2)}) collective-permute-start(bf16[2,1536,1024]{2,1,0:T(8,128)(2,1)} %attend_back.3.refs_0_), channel_id=1, source_target_pairs={{0,1},{1,0},{2,3},{3,2},{4,5},{5,4},{6,7},{7,6},{8,9},{9,8},{10,11... | collective-permute-start | bytes 18874376 | tf_op jit(solution)/shard_map/ppermute | solution.py:1006
  615.7 50.2 %collective-permute-start.11 = (bf16[1,1536,1024]{2,1,0:T(8,128)(2,1)S(1)}, bf16[1,1536,1024]{2,1,0:T(8,128)(2,1)}, u32[]{:S(2)}, u32[]{:S(2)}) collective-permute-start(bf16[1,1536,1024]{2,1,0:T(8,128)(2,1)S(1)} %copy-done.2), channel_id=1, source_target_pairs={{0,1},{1,0},{2,3},{3,2},{4,5},{5,4},{6,7},{7,6},{8,9},{9,8},{10,11... | collective-permute-start | bytes 9437192 | tf_op jit(solution)/shard_map/ppermute | solution.py:1005
  618.8 47.1 %collective-permute-start.12 = (bf16[1,768,1024]{2,1,0:T(8,128)(2,1)}, bf16[1,768,1024]{2,1,0:T(8,128)(2,1)}, u32[]{:S(2)}, u32[]{:S(2)}) collective-permute-start(bf16[1,768,1024]{2,1,0:T(8,128)(2,1)} %constant_dynamic-slice_fusion.2), channel_id=1, source_target_pairs={{3,1},{0,2},{7,5},{4,6},{11,9},{8,10},{15,13},{12,14},{19,17},{16,... | collective-permute-start | bytes 4718600 | tf_op jit(solution)/shard_map/ppermute | solution.py:1003
  623.0 42.9 %collective-permute-start.13 = (bf16[1,768,1024]{2,1,0:T(8,128)(2,1)}, bf16[1,768,1024]{2,1,0:T(8,128)(2,1)}, u32[]{:S(2)}, u32[]{:S(2)}) collective-permute-start(bf16[1,768,1024]{2,1,0:T(8,128)(2,1)} %constant_dynamic-slice_fusion.2), channel_id=1, source_target_pairs={{2,1},{1,2},{6,5},{5,6},{10,9},{9,10},{14,13},{13,14},{18,17},{17,... | collective-permute-start | bytes 4718600 | tf_op jit(solution)/shard_map/ppermute | solution.py:1004
  693.9 101.6 %all-to-all-start = ((bf16[32,136,128]{2,1,0:T(8,128)(2,1)}), bf16[32,136,128]{2,1,0:T(8,128)(2,1)S(1)}, u32[]{:S(2)}, u32[]{:S(2)}) async-start(bf16[32,136,128]{2,1,0:T(8,128)(2,1)} %bitcast.36), calls=%async_computation | async-start | bytes 2228224 | tf_op jit(solution)/shard_map/all_to_all | solution.py:1223
  785.4 1.3 collective-permute-start.14
  786.7 5.4 collective-permute-start.15
  (35 other events, 258.9 us)
Sparse Core Ops, SparseCore 0:
  12.4 112.2 all-gather.4
  128.2 213.9 all-gather.6
  615.8 168.5 reduce-scatter.4

commit v4 on v3

--- a/solution.py
+++ b/solution.py
@@ -577,74 +577,91 @@
     )(dy, gathered, grank, tables, tokens, grad_middle, gain)
 
 
-def out_kernel(nc, nm, group, per, ns, sets, scales, code, *refs):
+def collect_kernel(nc, nm, ns, code, *refs):
     sources = refs[:ns]
-    x_ref, w_ref, bias, odown, oup, gain, shift, fdown = refs[ns : ns + 8]
-    att_out, middle_ref, normed_ref, ro_ref, r1_ref, a_scr = refs[ns + 8 :]
+    att_ref, a_scr = refs[ns:]
     m = pl.program_id(0)
     c = pl.program_id(1)
     choose(code[3 * (c * nm + m)], sources, a_scr, c)
 
     @pl.when(c == nc - 1)
     def _():
-        att = jnp.concatenate([a_scr[i] for i in range(nc)], axis=1)
-        att_out[...] = att
-        ro = dot_t(att, odown[...]) * scales[m]
-        keep = set_mask(ro.shape, sets[m], group, per)
-        ro = jnp.where(keep, ro, 0.0).astype(BF)
-        ro_ref[...] = ro
-        middle = x_ref[...].astype(F32) + dot_t(att, w_ref[...]) + dot_t(ro, oup[...]) + bias[...]
-        middle_ref[...] = middle
-        unit, _ = norm_parts(middle)
-        normed = (unit * gain[...] + shift[...]).astype(BF)
-        normed_ref[...] = normed
-        r1_ref[...] = jnp.where(keep, dot(normed, fdown[...]) * scales[m], 0.0).astype(BF)
-
-
-def out_project(sources, code, tokens, wo_t, bias, odown, tables, gain, shift, sets, scales, tm, nc, per, rr):
+        att_ref[...] = jnp.concatenate([a_scr[i] for i in range(nc)], axis=1)
+
+
+def collect(sources, code, own, tm, nc):
+    nm = own // tm
+    return pl.pallas_call(
+        functools.partial(collect_kernel, nc, nm, len(sources)),
+        out_shape=jax.ShapeDtypeStruct((own, D), BF),
+        grid_spec=pltpu.PrefetchScalarGridSpec(
+            num_scalar_prefetch=1,
+            grid=(nm, nc),
+            in_specs=piece_specs(sources, tm, lambda m, c: c * nm + m),
+            out_specs=pl.BlockSpec((tm, D), lambda m, c, *_: (m, 0)),
+            scratch_shapes=[pltpu.VMEM((nc, tm, D // nc), BF)],
+        ),
+        compiler_params=params(2),
+        cost_estimate=cost(own * D, own * D * 10),
+        name="collect",
+    )(code, *sources)
+
+
+def out_kernel(group, per, sets, scales, *refs):
+    att_ref, x_ref, w_ref, bias, odown, oup, gain, shift, fdown = refs[:9]
+    middle_ref, normed_ref, ro_ref, r1_ref = refs[9:]
+    m = pl.program_id(0)
+    att = att_ref[...]
+    ro = dot_t(att, odown[...]) * scales[m]
+    keep = set_mask(ro.shape, sets[m], group, per)
+    ro = jnp.where(keep, ro, 0.0).astype(BF)
+    ro_ref[...] = ro
+    middle = x_ref[...].astype(F32) + dot_t(att, w_ref[...]) + dot_t(ro, oup[...]) + bias[...]
+    middle_ref[...] = middle
+    unit, _ = norm_parts(middle)
+    normed = (unit * gain[...] + shift[...]).astype(BF)
+    normed_ref[...] = normed
+    r1_ref[...] = jnp.where(keep, dot(normed, fdown[...]) * scales[m], 0.0).astype(BF)
+
+
+def out_project(att, tokens, wo_t, bias, odown, tables, gain, shift, sets, scales, tm, per):
     own = tokens.shape[0]
-    width = D // nc
-    group = SETS * per
-    wide = group * rr
-    nm = own // tm
-    row = lambda m, c, *_: (m, 0)
-    flat = lambda m, c, *_: (0, 0)
+    wide = odown.shape[0]
+    row = lambda m, *_: (m, 0)
+    flat = lambda m, *_: (0, 0)
     return pl.pallas_call(
-        functools.partial(out_kernel, nc, nm, group, per, len(sources)),
+        functools.partial(out_kernel, SETS * per, per),
         out_shape=(
-            jax.ShapeDtypeStruct((own, D), BF),
             jax.ShapeDtypeStruct((own, D), F32),
             jax.ShapeDtypeStruct((own, D), BF),
             jax.ShapeDtypeStruct((own, wide), BF),
             jax.ShapeDtypeStruct((own, wide), BF),
         ),
         grid_spec=pltpu.PrefetchScalarGridSpec(
-            num_scalar_prefetch=3,
-            grid=(nm, nc),
-            in_specs=piece_specs(sources, tm, lambda m, c, s, a: c * nm + m)
-            + [
+            num_scalar_prefetch=2,
+            grid=(own // tm,),
+            in_specs=[
+                pl.BlockSpec((tm, D), row),
                 pl.BlockSpec((tm, D), row),
                 pl.BlockSpec((D, D), flat),
                 pl.BlockSpec((1, D), flat),
                 pl.BlockSpec((wide, D), flat),
-                pl.BlockSpec((D, wide), lambda m, c, *_: (0, 4)),
+                pl.BlockSpec((D, wide), lambda m, *_: (0, 4)),
                 pl.BlockSpec((1, D), flat),
                 pl.BlockSpec((1, D), flat),
-                pl.BlockSpec((D, wide), lambda m, c, *_: (0, 3)),
+                pl.BlockSpec((D, wide), lambda m, *_: (0, 3)),
             ],
             out_specs=[
-                pl.BlockSpec((tm, D), row),
                 pl.BlockSpec((tm, D), row),
                 pl.BlockSpec((tm, D), row),
                 pl.BlockSpec((tm, wide), row),
                 pl.BlockSpec((tm, wide), row),
             ],
-            scratch_shapes=[pltpu.VMEM((nc, tm, width), BF)],
-        ),
-        compiler_params=params(2),
+        ),
+        compiler_params=params(1),
         cost_estimate=cost(2 * own * D * D * 1.5, D * D * 2 + own * D * 12),
         name="out_project",
-    )(sets, scales, code, *sources, tokens, wo_t, bias, odown, tables, gain, shift, tables)
+    )(sets, scales, att, tokens, wo_t, bias, odown, tables, gain, shift, tables)
 
 
 def out_back_kernel(nc, width, group, per, sets, scales, side, gb_ref, w_ref, oup, odown, att_ref, ro_ref, *outs):
@@ -1174,8 +1191,9 @@
             n, _ = lax.optimization_barrier((n, results[-1][1]))
         results.append(attend(sources, plan, index, n, clip_len, hh))
     pieces = exchange.from_heads([r[0] for r in results])
-    att, middle, normed_mlp, ro, r1 = out_project(
-        pieces, exchange.code, tokens, wo_t, out_bias[None], odown, tables, gain2, shift2, sets, scales, tm, nc, per, nr
+    att = collect(pieces, exchange.code, own, tm, nc)
+    middle, normed_mlp, ro, r1 = out_project(
+        att, tokens, wo_t, out_bias[None], odown, tables, gain2, shift2, sets, scales, tm, per
     )
     output, grad_middle, grad_branch, gup1, gdown2, gup2, gdown1 = mlp(
         normed_mlp, cotangent, middle, g2, b1, tables, r1, fc2_bias[None], gain2, sets, scales, tm, per, at_f

time: 819 us -> 808 us (0.987)
  waiting for transfers between devices: 283 us -> 263 us
    all_gather x1, waiting for transfers between devices: 87.1 us -> 49.5 us  [body(): g2 = lax.all_gather(packed, BOTH, axis=0).reshape(nr, nc, -1, hidden)]
    ppermute x2, waiting for transfers between devices: 39.9 us -> 57.7 us  [from_heads(): got_one = lax.ppermute(far, 'cols', [(3, 1), (0, 2)])]
    pallas_call x1 -> x2, Pallas kernels: 23.9 us -> 24.8 us  [the longest x1 14.4 us: out_project(): pl.pallas_call(functools.partial(out_kernel, SETS * per, per), out_shape=...]
    unnamed x94 -> x84, local copies, waits for them, and re-layouts: 16.5 us -> 17.4 us
  transfers between devices with their start and end apart: 20 -> 20, of which waited for: 7 -> 8; matrix products, arithmetic and copies ran while one was open for 4% -> 5% of each run, Pallas kernels for 19% -> 20%
where the time goes in v4:
time: 808 us; the launch traced here: 802 us
  Pallas kernels  390 us (48%)
  waiting for transfers between devices  263 us (33%)
  starting transfers between devices  61.9 us (8%)
  local copies, waits for them, and re-layouts  54.1 us (7%)
  between operations  16.5 us (2%)
  other arithmetic  10.6 us (1%)
    all_gather x1, waiting for transfers between devices, body(): g1 = lax.all_gather(packed, BOTH, axis=0).reshape(nr, nc, -1, lanes)  112 us
    pallas_call x1, Pallas kernels, mlp(): pl.pallas_call(functools.partial(mlp_kernel, tm, nm, group, per), out_sha...  105 us
    pallas_call x2, Pallas kernels, attend_back(): pl.pallas_call(functools.partial(attend_back_kernel, hh, length, qb, kb,...  88.3 us
    pallas_call x2, Pallas kernels, attend(): pl.pallas_call(functools.partial(attend_kernel, hh, length, qb, kb, len(s...  65.2 us
    ppermute x2, waiting for transfers between devices, from_heads(): got_one = lax.ppermute(far, 'cols', [(3, 1), (0, 2)])  57.7 us
    all_gather x1, waiting for transfers between devices, body(): g2 = lax.all_gather(packed, BOTH, axis=0).reshape(nr, nc, -1, hidden)  49.5 us
    all_to_all x1, starting transfers between devices, body(): got = lax.all_to_all(last, BOTH, 0, 0, tiled=True)  31.2 us
    optimization_barrier x1, waiting for transfers between devices, body(): late, grad_tokens = lax.optimization_barrier((late, grad_tokens))  31.2 us
  transfers between devices with their start and end apart: 20, of which 8 were waited for; matrix products, arithmetic and copies ran while one was open for 5% of the time, Pallas kernels for 20%

profile of v4, /device:TPU:0, one launch (start us, length us, event | category | flops | bytes accessed | tf_op | source)
XLA Modules:
  0.0 802.1 jit_solution(18167663089802106724)
XLA Ops:
  12.9 111.8 %all-gather.5.cloned.1.call-done = bf16[7680,960]{1,0:T(8,128)(2,1)} async-done(((bf16[240,960]{1,0:T(8,128)(2,1)}), bf16[7680,960]{1,0:T(8,128)(2,1)}) %all-gather.5.cloned.1.call-update) | async-done | bytes 14745616 | tf_op jit(solution)/shard_map/all_gather | solution.py:1146
  133.4 29.6 %project.1 = (bf16[1152,1280]{1,0:T(8,128)(2,1)}, bf16[1152,384]{1,0:T(8,128)(2,1)}, bf16[2,1152,1024]{2,1,0:T(8,128)(2,1)}, bf16[2,1152,1024]{2,1,0:T(8,128)(2,1)}) custom-call(s32[3]{0:T(128)} %broadcast_select_fusion.4.sets, f32[3]{0:T(128)} %broadcast_select_fusion.3.scales, s32[4]{0:T(128)} %and_select_fusion.4.order, bf16[1152,1280]{1,0:T(8,128)(2,1)} %x_ref.3, ...), custom_call_target="tpu_custom_call" | custom-call | flops 14722007040 | bytes 24576000 | tf_op jit(solution)/shard_map/project/pallas_call | solution.py:338
  175.1 46.1 %attend.2 = (bf16[2,1536,384]{2,1,0:T(8,128)(2,1)}, f32[2,4,1536]{2,1,0:T(4,128)}, bf16[2,1536,960]{2,1,0:T(8,128)(2,1)}) custom-call(s32[2]{0:T(128)} %pad_add_fusion.1.lens, s32[8]{0:T(128)} %pad_add_fusion.2.plan, s32[4]{0:T(128)} %constant.177.clone.index, bf16[2,1152,1024]{2,1,0:T(8,128)(2,1)} %get-tuple-element.57.refs_0_, ...), custom_call_target="tpu_custom_call" | custom-call | flops 19327352832 | bytes 17694720 | tf_op jit(solution)/shard_map/attend/pallas_call | solution.py:152
  221.2 4.0 collective-permute-start.3
  226.6 19.1 %attend.3 = (bf16[1,1536,384]{2,1,0:T(8,128)(2,1)}, f32[1,4,1536]{2,1,0:T(4,128)}, bf16[1,1536,960]{2,1,0:T(8,128)(2,1)}) custom-call(s32[1]{0:T(128)} %get-tuple-element.61.lens, s32[8]{0:T(128)} %pad_add_fusion.3.plan, s32[4]{0:T(128)} %get-tuple-element.195.index, bf16[2,1152,1024]{2,1,0:T(8,128)(2,1)} %get-tuple-element.57.refs_0_, ...), custom_call_target="tpu_custom_call" | custom-call | flops 9663676416 | bytes 8847360 | tf_op jit(solution)/shard_map/attend/pallas_call | solution.py:152
  248.5 5.0 collective-permute-start.5
  260.9 18.2 %collective-permute-done.5.refs_4_ = bf16[1,768,384]{2,1,0:T(8,128)(2,1)} collective-permute-done((bf16[1,768,384]{2,1,0:T(8,128)(2,1)}, bf16[1,768,384]{2,1,0:T(8,128)(2,1)}, u32[]{:S(2)}, u32[]{:S(2)}) %collective-permute-start.5) | collective-permute-done | bytes 589856 | tf_op jit(solution)/shard_map/ppermute | solution.py:1020
  281.6 10.4 %collect.1.refs_0_.att_ref = bf16[1152,1280]{1,0:T(8,128)(2,1)} custom-call(s32[36]{0:T(128)} %reshape.381.code, bf16[2,1536,384]{2,1,0:T(8,128)(2,1)} %get-tuple-element.59.refs_0_.refs_3_, bf16[1,1536,384]{2,1,0:T(8,128)(2,1)} %get-tuple-element.62.refs_1_.refs_5_, bf16[2,1536,384]{2,1,0:T(8,128)(2,1)} %copy-done.3, bf16[1,1536,384]{2,1,0:T(8,128)(2,1)} %copy-done.7, ...), custom_call_target="tpu_custom_call" | custom-call | flops 1474560 | bytes 14745600 | tf_op jit(solution)/shard_map/collect/pallas_call | solution.py:594
  292.1 49.5 %all-gather.7.cloned.1.call-done = bf16[13824,1280]{1,0:T(8,128)(2,1)} async-done(((bf16[432,1280]{1,0:T(8,128)(2,1)}), bf16[13824,1280]{1,0:T(8,128)(2,1)}) %all-gather.7.cloned.1.call-update) | async-done | bytes 35389456 | tf_op jit(solution)/shard_map/all_gather | solution.py:1175
  341.5 5.4 assemble.1
  348.5 14.4 %out_project.1 = (f32[1152,1280]{1,0:T(8,128)}, bf16[1152,1280]{1,0:T(8,128)(2,1)}, bf16[1152,128]{1,0:T(8,128)(2,1)}, bf16[1152,128]{1,0:T(8,128)(2,1)}) custom-call(s32[3]{0:T(128)} %broadcast_select_fusion.4.sets, f32[3]{0:T(128)} %broadcast_select_fusion.3.scales, bf16[1152,1280]{1,0:T(8,128)(2,1)} %collect.1.refs_0_.att_ref, bf16[1152,1280]{1,0:T(8,128)(2,1)} %x_ref.3, ...), custom_call_target="tpu_custom_call" | custom-call | flops 5662310400 | bytes 20971520 | tf_op jit(solution)/shard_map/out_project/pallas_call | solution.py:632
  362.9 105.3 %mlp.1 = (bf16[1152,1280]{1,0:T(8,128)(2,1)}, f32[1152,1280]{1,0:T(8,128)}, bf16[1152,1280]{1,0:T(8,128)(2,1)}, bf16[8,4,160,128]{3,2,1,0:T(8,128)(2,1)}, bf16[8...) custom-call(s32[3]{0:T(128)} %broadcast_select_fusion.4.sets, ...), custom_call_target="tpu_custom_call" | custom-call | flops 72477573120 | bytes 70451200 | tf_op jit(solution)/shard_map/mlp/pallas_call | solution.py:836
  472.2 18.1 %out_back.1 = (bf16[2,1152,384]{2,1,0:T(8,128)(2,1)}, bf16[2,1152,384]{2,1,0:T(8,128)(2,1)}, bf16[1280,128]{1,0:T(8,128)(2,1)}, bf16[8,4,48,128]{3,2,1,0:T(8,128)(2,1)}) custom-call(s32[3]{0:T(128)} %broadcast_select_fusion.4.sets, f32[3]{0:T(128)} %broadcast_select_fusion.3.scales, s32[1]{0:T(128)} %bitcast.26.side, ...), custom_call_target="tpu_custom_call" | custom-call | flops 5662310400 | bytes 12124160 | tf_op jit(solution)/shard_map/out_back/pallas_call | solution.py:713
  499.2 9.8 %collective-permute-done.8.refs_2_ = bf16[1,768,384]{2,1,0:T(8,128)(2,1)S(1)} collective-permute-done((bf16[1,768,384]{2,1,0:T(8,128)(2,1)S(1)}, bf16[1,768,384]{2,1,0:T(8,128)(2,1)S(1)}, u32[]{:S(2)}, u32[]{:S(2)}) %collective-permute-start.8) | collective-permute-done | bytes 589856 | tf_op jit(solution)/shard_map/ppermute | solution.py:1007
  511.0 21.0 %attend_back.2.refs_1_ = bf16[1,1536,1024]{2,1,0:T(8,128)(2,1)} custom-call(s32[1]{0:T(128)} %get-tuple-element.61.lens, s32[8]{0:T(128)} %pad_add_fusion.3.plan, s32[4]{0:T(128)} %get-tuple-element.195.index, bf16[2,1152,384]{2,1,0:T(8,128)(2,1)} %get-tuple-element.81.refs_0_, bf16[2,1152,384]{2,1,0:T(8,128)(2,1)} %copy-done.30, ...), custom_call_target="tpu_custom_call" | custom-call | flops 24159191040 | bytes 8847360 | tf_op jit(solution)/shard_map/attend_back/pallas_call | solution.py:258
  531.9 67.3 %attend_back.3.refs_0_ = bf16[2,1536,1024]{2,1,0:T(8,128)(2,1)} custom-call(s32[2]{0:T(128)} %pad_add_fusion.1.lens, s32[8]{0:T(128)} %pad_add_fusion.2.plan, s32[4]{0:T(128)} %constant.177.clone.index, bf16[2,1152,384]{2,1,0:T(8,128)(2,1)} %get-tuple-element.81.refs_0_, bf16[2,1152,384]{2,1,0:T(8,128)(2,1)} %copy-done.30, ...), custom_call_target="tpu_custom_call" | custom-call | flops 48318382080 | bytes 17694720 | tf_op jit(solution)/shard_map/attend_back/pallas_call | solution.py:258
  599.3 5.5 collective-permute-start.10
  608.0 4.1 collective-permute-start.12
  615.1 39.5 %collective-permute-done.12.refs_4_ = bf16[1,768,1024]{2,1,0:T(8,128)(2,1)} collective-permute-done((bf16[1,768,1024]{2,1,0:T(8,128)(2,1)}, bf16[1,768,1024]{2,1,0:T(8,128)(2,1)}, u32[]{:S(2)}, u32[]{:S(2)}) %collective-permute-start.12) | collective-permute-done | bytes 1572896 | tf_op jit(solution)/shard_map/ppermute | solution.py:1020
  654.6 25.0 %adapt_back.1 = (bf16[4,1152,960]{2,1,0:T(8,128)(2,1)}, bf16[1152,384]{1,0:T(8,128)(2,1)}, bf16[4,27,16,128]{3,2,1,0:T(8,128)(2,1)}, bf16[2,1280,128]{2,1,0:T(8,128)(2,1)}) custom-call(s32[3]{0:T(128)} %broadcast_select_fusion.4.sets, f32[3]{0:T(128)} %broadcast_select_fusion.3.scales, s32[3]{0:T(128)} %and_select_fusion.12.slots, s32[36]{0:T(128)} %reshape.381.code, ...), custom_call_target="tpu_custom_call" | custom-call | flops 3397386240 | bytes 17694720 | tf_op jit(solution)/shard_map/adapt_back/pallas_call | solution.py:494
  682.6 31.2 %all-to-all-start = ((bf16[32,136,128]{2,1,0:T(8,128)(2,1)}), bf16[32,136,128]{2,1,0:T(8,128)(2,1)S(1)}, u32[]{:S(2)}, u32[]{:S(2)}) async-start(bf16[32,136,128]{2,1,0:T(8,128)(2,1)} %bitcast.36), calls=%async_computation | async-start | bytes 2228224 | tf_op jit(solution)/shard_map/all_to_all | solution.py:1241
  713.8 28.5 %project_back.1 = bf16[1152,1280]{1,0:T(8,128)(2,1)} custom-call(bf16[4,1152,960]{2,1,0:T(8,128)(2,1)} %get-tuple-element.92.dy_ref, bf16[8,4,240,960]{3,2,1,0:T(8,128)(2,1)} %bitcast.133, bf16[1152,384]{1,0:T(8,128)(2,1)} %get-tuple-element.93.grank_ref, bf16[1280,768]{1,0:T(8,128)(2,1)} %bitcast.141, bf16[1152,1280]{1,0:T(8,128)(2,1)} %x_ref.3, ...), custom_call_target="tpu_custom_call" | custom-call | flops 12457082880 | bytes 30474240 | tf_op jit(solution)/shard_map/project_back/pallas_call | solution.py:559
  742.3 31.2 %reduce-scatter.5.cloned.1.call-done = bf16[488,128]{1,0:T(8,128)(2,1)} async-done(((bf16[15616,128]{1,0:T(8,128)(2,1)}), bf16[488,128]{1,0:T(8,128)(2,1)}) %reduce-scatter.5.cloned.1.call-update) | async-done | bytes 124944 | tf_op jit(solution)/shard_map/optimization_barrier | solution.py:1243
  786.3 5.7 all_gather.19
  (239 shorter events, 79.7 us)
Async XLA Ops:
  7.3 117.4 %all-gather.5.cloned.1.call-start = ((), (), s32[]{:S(2)}) async-start(), calls=%async_computation.2 | async-start | bytes 16220160 | tf_op jit(solution)/shard_map/all_gather | solution.py:1146
  12.3 329.3 %all-gather.7.cloned.1.call-start = ((), (), s32[]{:S(2)}) async-start(), calls=%async_computation.3 | async-start | bytes 36495360 | tf_op jit(solution)/shard_map/all_gather | solution.py:1175
  12.7 112.8 %copy-start.1 = (f32[3]{0:T(128)S(1)}, f32[3]{0:T(128)}, u32[]{:S(2)}) copy-start(f32[3]{0:T(128)} %param.37) | copy-start | bytes 40
  12.7 113.4 %copy-start.25 = (f32[1280]{0:T(1024)S(1)}, f32[1280]{0:T(1024)}, u32[]{:S(2)}) copy-start(f32[1280]{0:T(1024)} %param.38) | copy-start | bytes 15364
  12.7 113.9 %copy-start.26 = (f32[1280]{0:T(1024)S(1)}, f32[1280]{0:T(1024)}, u32[]{:S(2)}) copy-start(f32[1280]{0:T(1024)} %param.39) | copy-start | bytes 15364
  12.9 111.8 %copy-start.5 = (bf16[432,1280]{1,0:T(8,128)(2,1)}, bf16[432,1280]{1,0:T(8,128)(2,1)S(1)}, u32[]{:S(2)}) copy-start(bf16[432,1280]{1,0:T(8,128)(2,1)S(1)} %fusion.16) | copy-start | bytes 3317764
  124.7 648.8 %reduce-scatter.5.cloned.1.call-start = ((), (), s32[]{:S(2)}) async-start(), calls=%async_computation.4 | async-start | bytes 4122624
  163.0 12.1 %collective-permute-start = (bf16[2,1152,1024]{2,1,0:T(8,128)(2,1)}, bf16[2,1152,1024]{2,1,0:T(8,128)(2,1)}, u32[]{:S(2)}, u32[]{:S(2)}) collective-permute-start(bf16[2,1152,1024]{2,1,0:T(8,128)(2,1)} %get-tuple-element.58), channel_id=1, source_target_pairs={{0,1},{1,0},{2,3},{3,2},{4,5},{5,4},{6,7},{7,6},{8,9},{9,8},{10,11... | collective-permute-start | bytes 14155784 | tf_op jit(solution)/shard_map/ppermute | solution.py:1004
  169.1 57.5 %collective-permute-start.1 = (bf16[1,768,1024]{2,1,0:T(8,128)(2,1)}, bf16[1,768,1024]{2,1,0:T(8,128)(2,1)}, u32[]{:S(2)}, u32[]{:S(2)}) collective-permute-start(bf16[1,768,1024]{2,1,0:T(8,128)(2,1)} %constant_dynamic-slice_fusion.7), channel_id=1, source_target_pairs={{1,3},{2,0},{5,7},{6,4},{9,11},{10,8},{13,15},{14,12},{17,19},{18,... | collective-permute-start | bytes 4718600 | tf_op jit(solution)/shard_map/ppermute | solution.py:1007
  173.1 53.5 %collective-permute-start.2 = (bf16[1,768,1024]{2,1,0:T(8,128)(2,1)}, bf16[1,768,1024]{2,1,0:T(8,128)(2,1)}, u32[]{:S(2)}, u32[]{:S(2)}) collective-permute-start(bf16[1,768,1024]{2,1,0:T(8,128)(2,1)} %constant_dynamic-slice_fusion.6), channel_id=1, source_target_pairs={{1,2},{2,1},{5,6},{6,5},{9,10},{10,9},{13,14},{14,13},{17,18},{18,... | collective-permute-start | bytes 4718600 | tf_op jit(solution)/shard_map/ppermute | solution.py:1008
  221.2 58.0 %collective-permute-start.3 = (bf16[2,1536,384]{2,1,0:T(8,128)(2,1)}, bf16[2,1536,384]{2,1,0:T(8,128)(2,1)S(1)}, u32[]{:S(2)}, u32[]{:S(2)}) collective-permute-start(bf16[2,1536,384]{2,1,0:T(8,128)(2,1)} %get-tuple-element.59.refs_0_.refs_3_), channel_id=1, source_target_pairs={{0,1},{1,0},{2,3},{3,2},{4,5},{5,4},{6,7},{7,6},{8,9},{9,8},{10,11... | collective-permute-start | bytes 7077896 | tf_op jit(solution)/shard_map/ppermute | solution.py:1023
  245.7 33.5 %collective-permute-start.4 = (bf16[1,1536,384]{2,1,0:T(8,128)(2,1)}, bf16[1,1536,384]{2,1,0:T(8,128)(2,1)S(1)}, u32[]{:S(2)}, u32[]{:S(2)}) collective-permute-start(bf16[1,1536,384]{2,1,0:T(8,128)(2,1)} %get-tuple-element.62.refs_1_.refs_5_), channel_id=1, source_target_pairs={{0,1},{1,0},{2,3},{3,2},{4,5},{5,4},{6,7},{7,6},{8,9},{9,8},{10,11... | collective-permute-start | bytes 3538952 | tf_op jit(solution)/shard_map/ppermute | solution.py:1022
  248.5 30.7 %collective-permute-start.5 = (bf16[1,768,384]{2,1,0:T(8,128)(2,1)}, bf16[1,768,384]{2,1,0:T(8,128)(2,1)}, u32[]{:S(2)}, u32[]{:S(2)}) collective-permute-start(bf16[1,768,384]{2,1,0:T(8,128)(2,1)} %constant_dynamic-slice_fusion.5), channel_id=1, source_target_pairs={{3,1},{0,2},{7,5},{4,6},{11,9},{8,10},{15,13},{12,14},{19,17},{16,... | collective-permute-start | bytes 1769480 | tf_op jit(solution)/shard_map/ppermute | solution.py:1020
  253.5 25.7 %collective-permute-start.6 = (bf16[1,768,384]{2,1,0:T(8,128)(2,1)}, bf16[1,768,384]{2,1,0:T(8,128)(2,1)}, u32[]{:S(2)}, u32[]{:S(2)}) collective-permute-start(bf16[1,768,384]{2,1,0:T(8,128)(2,1)} %constant_dynamic-slice_fusion.5), channel_id=1, source_target_pairs={{2,1},{1,2},{6,5},{5,6},{10,9},{9,10},{14,13},{13,14},{18,17},{17,... | collective-permute-start | bytes 1769480 | tf_op jit(solution)/shard_map/ppermute | solution.py:1021
  495.7 13.2 %collective-permute-start.7 = (bf16[2,1152,384]{2,1,0:T(8,128)(2,1)S(1)}, bf16[2,1152,384]{2,1,0:T(8,128)(2,1)S(1)}, u32[]{:S(2)}, u32[]{:S(2)}) collective-permute-start(bf16[2,1152,384]{2,1,0:T(8,128)(2,1)S(1)} %copy-done.13), channel_id=1, source_target_pairs={{0,1},{1,0},{2,3},{3,2},{4,5},{5,4},{6,7},{7,6},{8,9},{9,8},{10,11... | collective-permute-start | bytes 5308424 | tf_op jit(solution)/shard_map/ppermute | solution.py:1004
  497.1 11.8 %collective-permute-start.8 = (bf16[1,768,384]{2,1,0:T(8,128)(2,1)S(1)}, bf16[1,768,384]{2,1,0:T(8,128)(2,1)S(1)}, u32[]{:S(2)}, u32[]{:S(2)}) collective-permute-start(bf16[1,768,384]{2,1,0:T(8,128)(2,1)S(1)} %constant_dynamic-slice_fusion.4), channel_id=1, source_target_pairs={{1,3},{2,0},{5,7},{6,4},{9,11},{10,8},{13,15},{14,12},{17,19},{18,... | collective-permute-start | bytes 1769480 | tf_op jit(solution)/shard_map/ppermute | solution.py:1007
  498.4 10.5 %collective-permute-start.9 = (bf16[1,768,384]{2,1,0:T(8,128)(2,1)S(1)}, bf16[1,768,384]{2,1,0:T(8,128)(2,1)S(1)}, u32[]{:S(2)}, u32[]{:S(2)}) collective-permute-start(bf16[1,768,384]{2,1,0:T(8,128)(2,1)S(1)} %constant_dynamic-slice_fusion.3), channel_id=1, source_target_pairs={{1,2},{2,1},{5,6},{6,5},{9,10},{10,9},{13,14},{14,13},{17,18},{18,... | collective-permute-start | bytes 1769480 | tf_op jit(solution)/shard_map/ppermute | solution.py:1008
  599.3 55.4 %collective-permute-start.10 = (bf16[2,1536,1024]{2,1,0:T(8,128)(2,1)}, bf16[2,1536,1024]{2,1,0:T(8,128)(2,1)}, u32[]{:S(2)}, u32[]{:S(2)}) collective-permute-start(bf16[2,1536,1024]{2,1,0:T(8,128)(2,1)} %attend_back.3.refs_0_), channel_id=1, source_target_pairs={{0,1},{1,0},{2,3},{3,2},{4,5},{5,4},{6,7},{7,6},{8,9},{9,8},{10,11... | collective-permute-start | bytes 18874376 | tf_op jit(solution)/shard_map/ppermute | solution.py:1023
  604.9 49.8 %collective-permute-start.11 = (bf16[1,1536,1024]{2,1,0:T(8,128)(2,1)S(1)}, bf16[1,1536,1024]{2,1,0:T(8,128)(2,1)}, u32[]{:S(2)}, u32[]{:S(2)}) collective-permute-start(bf16[1,1536,1024]{2,1,0:T(8,128)(2,1)S(1)} %copy-done.2), channel_id=1, source_target_pairs={{0,1},{1,0},{2,3},{3,2},{4,5},{5,4},{6,7},{7,6},{8,9},{9,8},{10,11... | collective-permute-start | bytes 9437192 | tf_op jit(solution)/shard_map/ppermute | solution.py:1022
  608.0 46.7 %collective-permute-start.12 = (bf16[1,768,1024]{2,1,0:T(8,128)(2,1)}, bf16[1,768,1024]{2,1,0:T(8,128)(2,1)}, u32[]{:S(2)}, u32[]{:S(2)}) collective-permute-start(bf16[1,768,1024]{2,1,0:T(8,128)(2,1)} %constant_dynamic-slice_fusion.2), channel_id=1, source_target_pairs={{3,1},{0,2},{7,5},{4,6},{11,9},{8,10},{15,13},{12,14},{19,17},{16,... | collective-permute-start | bytes 4718600 | tf_op jit(solution)/shard_map/ppermute | solution.py:1020
  612.1 42.5 %collective-permute-start.13 = (bf16[1,768,1024]{2,1,0:T(8,128)(2,1)}, bf16[1,768,1024]{2,1,0:T(8,128)(2,1)}, u32[]{:S(2)}, u32[]{:S(2)}) collective-permute-start(bf16[1,768,1024]{2,1,0:T(8,128)(2,1)} %constant_dynamic-slice_fusion.2), channel_id=1, source_target_pairs={{2,1},{1,2},{6,5},{5,6},{10,9},{9,10},{14,13},{13,14},{18,17},{17,... | collective-permute-start | bytes 4718600 | tf_op jit(solution)/shard_map/ppermute | solution.py:1021
  682.6 102.0 %all-to-all-start = ((bf16[32,136,128]{2,1,0:T(8,128)(2,1)}), bf16[32,136,128]{2,1,0:T(8,128)(2,1)S(1)}, u32[]{:S(2)}, u32[]{:S(2)}) async-start(bf16[32,136,128]{2,1,0:T(8,128)(2,1)} %bitcast.36), calls=%async_computation | async-start | bytes 2228224 | tf_op jit(solution)/shard_map/all_to_all | solution.py:1241
  774.5 1.3 collective-permute-start.14
  775.8 5.4 collective-permute-start.15
  (30 other events, 140.6 us)
Sparse Core Ops, SparseCore 0:
  12.4 112.2 all-gather.4
  127.6 213.8 all-gather.6
  605.0 168.4 reduce-scatter.4

commit v5 on v4

--- a/solution.py
+++ b/solution.py
@@ -307,8 +307,8 @@
         r_scr[rows, :] = rank
         ranks_ref[...] = rank
 
-    y = dot(n_scr[rows, :], w_ref[:, 0].reshape(D, 3 * width)) + bias[0]
-    table = up[:, 0].reshape(wide, 3 * width)
+    y = dot(n_scr[rows, :], w_ref[:, 0].reshape(D, 4 * width)[:, 0 : 3 * width]) + bias[0]
+    table = up[:, 0].reshape(wide, 4 * width)
     rank = r_scr[rows, :]
     extra = [
         dot(rank[:, j * wide : (j + 1) * wide], table[:, j * width : (j + 1) * width]) for j in range(3)
@@ -327,8 +327,9 @@
 
 def project(tokens, gain, shift, gathered, bias, tables, sets, scales, order, tm, per):
     own = tokens.shape[0]
-    rr, nc, _, w3 = gathered.shape
-    width = w3 // 3
+    rr, nc, _, w4 = gathered.shape
+    width = w4 // 4
+    w3 = 3 * width
     group = SETS * per
     wide = group * rr
     nm = own // tm
@@ -350,11 +351,11 @@
                 pl.BlockSpec((tm, D), first),
                 pl.BlockSpec((1, D), flat),
                 pl.BlockSpec((1, D), flat),
-                pl.BlockSpec((rr, 1, D // rr, w3), lambda c, m, s, a, o: (0, o[c], 0, 0)),
+                pl.BlockSpec((rr, 1, D // rr, w4), lambda c, m, s, a, o: (0, o[c], 0, 0)),
                 pl.BlockSpec((1, 1, w3), lambda c, m, s, a, o: (o[c], 0, 0)),
                 pl.BlockSpec((D, 3 * wide), flat),
                 pl.BlockSpec(
-                    (rr, 1, group, w3), lambda c, m, s, a, o: (0, o[c], D // rr // group, 0)
+                    (rr, 1, group, w4), lambda c, m, s, a, o: (0, o[c], D // rr // group, 0)
                 ),
             ],
             out_specs=[
@@ -425,7 +426,7 @@
     wide = group * up.shape[0]
     choose(code[3 * (c * nm + m)], sources, dy_ref, 0)
     dy = dy_ref[0]
-    table = up[:, 0].reshape(wide, 3 * width)
+    table = up[:, 0].reshape(wide, 4 * width)
     pieces = [dy[:, j * width : (j + 1) * width] for j in range(3)]
     rpart = jnp.concatenate(
         [dot_t(pieces[j], table[:, j * width : (j + 1) * width]) for j in range(3)], axis=1
@@ -483,8 +484,9 @@
 
 def adapt_back(sources, code, gathered, normed, ranks, sets, scales, slots, clips, tm, per):
     own = normed.shape[0]
-    rr, nc, _, w3 = gathered.shape
-    width = w3 // 3
+    rr, nc, _, w4 = gathered.shape
+    width = w4 // 4
+    w3 = 3 * width
     group = SETS * per
     wide = group * rr
     nm = own // tm
@@ -504,7 +506,7 @@
             grid=(nc, nm),
             in_specs=piece_specs(sources, tm, lambda c, m, s, a, i: c * nm + m)
             + [
-                pl.BlockSpec((rr, 1, group, w3), lambda c, m, *_: (0, c, D // rr // group, 0)),
+                pl.BlockSpec((rr, 1, group, w4), lambda c, m, *_: (0, c, D // rr // group, 0)),
                 pl.BlockSpec((tm, D), final),
                 pl.BlockSpec((tm, 3 * wide), lambda c, m, *_: (m, 0)),
             ],
@@ -530,7 +532,7 @@
     c = pl.program_id(0)
     m = pl.program_id(1)
     rows = pl.ds(pl.multiple_of(m * tm, tm), tm)
-    part = dot_t(dy_ref[0], w_ref[:, 0].reshape(D, 3 * width))
+    part = dot_t(dy_ref[0], w_ref[:, 0].reshape(D, 4 * width)[:, 0 : 3 * width])
 
     @pl.when(c == 0)
     def _():
@@ -551,8 +553,9 @@
 
 def project_back(dy, gathered, grank, tables, tokens, grad_middle, gain, tm):
     own = tokens.shape[0]
-    rr, nc, _, w3 = gathered.shape
-    width = w3 // 3
+    rr, nc, _, w4 = gathered.shape
+    width = w4 // 4
+    w3 = 3 * width
     wide3 = grank.shape[1]
     nm = own // tm
     final = lambda c, m: (jnp.where(c == nc - 1, m, 0), 0)
@@ -562,7 +565,7 @@
         grid=(nc, nm),
         in_specs=[
             pl.BlockSpec((1, tm, w3), lambda c, m: (c, m, 0)),
-            pl.BlockSpec((rr, 1, D // rr, w3), lambda c, m: (0, c, 0, 0)),
+            pl.BlockSpec((rr, 1, D // rr, w4), lambda c, m: (0, c, 0, 0)),
             pl.BlockSpec((tm, wide3), lambda c, m: (jnp.where(c == 0, m, nm - 1), 0)),
             pl.BlockSpec((D, wide3), lambda c, m: (0, 0)),
             pl.BlockSpec((tm, D), final),
@@ -891,32 +894,29 @@
     )
 
 
-def assemble_kernel(width, parts, w_ref, o_ref, w_out, o_out):
-    _, nc = w_ref.shape[:2]
-    columns, downs = [], []
-    for c in range(nc):
-        block = w_ref[:, c]
-        rows = [block[:, :, j * width : (j + 1) * width] for j in range(parts)]
-        columns.append(jnp.concatenate(rows, axis=1).reshape(D, width))
-        downs.append(o_ref[:, c, :, 0:width].reshape(-1, width))
+def assemble_kernel(width, w_ref, o_ref, w_out, o_out):
+    nc = w_ref.shape[1]
+    columns = [w_ref[:, c].reshape(D, 2 * width)[:, width:] for c in range(nc)]
+    downs = [o_ref[:, c].reshape(-1, 2 * width)[:, width:] for c in range(nc)]
     w_out[...] = jnp.concatenate(columns, axis=1)
     o_out[...] = jnp.concatenate(downs, axis=1)
 
 
-def assemble(gathered, at_w, rows_w, at_o, group, width):
-    nr, nc, _, hidden = gathered.shape
-    parts = hidden // width
-    if rows_w % 8 == 0 and at_w % rows_w == 0:
+def assemble(gathered, group):
+    nr, nc, _, w4 = gathered.shape
+    width = w4 // 4
+    rows = D // nr
+    if 2 * width % 128 == 0:
         return pl.pallas_call(
-            functools.partial(assemble_kernel, width, parts),
+            functools.partial(assemble_kernel, width),
             out_shape=(
                 jax.ShapeDtypeStruct((D, D), BF),
                 jax.ShapeDtypeStruct((nr * group, D), BF),
             ),
             grid=(1,),
             in_specs=[
-                pl.BlockSpec((nr, nc, rows_w, hidden), lambda i: (0, 0, at_w // rows_w, 0)),
-                pl.BlockSpec((nr, nc, group, hidden), lambda i: (0, 0, at_o // group, 0)),
+                pl.BlockSpec((nr, nc, rows, 2 * width), lambda i: (0, 0, 0, 1)),
+                pl.BlockSpec((nr, nc, group, 2 * width), lambda i: (0, 0, rows // group, 1)),
             ],
             out_specs=[
                 pl.BlockSpec((D, D), lambda i: (0, 0)),
@@ -925,10 +925,10 @@
             compiler_params=params(1),
             name="assemble",
         )(gathered, gathered)
-    w = gathered[:, :, at_w : at_w + rows_w].reshape(nr, nc, rows_w, parts, width)
-    o = gathered[:, :, at_o : at_o + group, :width]
+    w = gathered[:, :, :rows, 3 * width :]
+    o = gathered[:, :, rows : rows + group, 3 * width :]
     return (
-        w.transpose(0, 3, 2, 1, 4).reshape(D, D),
+        w.transpose(0, 2, 1, 3).reshape(D, D),
         o.transpose(0, 2, 1, 3).reshape(nr * group, D),
     )
 
@@ -1120,61 +1120,48 @@
     ups = ups.reshape(2, SETS, nr, per, dc).transpose(4, 0, 2, 1, 3).reshape(dc, 2 * wide)
     tables = jnp.concatenate([downs, ups], axis=1)
 
-    lanes = 3 * width
-    qh, ql = halves(query_bias)
-    vh, vl = halves(value_bias)
-    none = jnp.zeros_like(qh)
-    ids = jnp.pad(clip_sets.astype(BF), (0, lanes - clips))
-    natural = lanes >= 6 * wide
-    small = rows_padded(tables, dc, lanes) if natural else tables.reshape(-1, lanes)
+    lanes = 4 * width
+    turn = lambda v: jnp.swapaxes(v, 1, 2).reshape(group, -1)
+    extra = jnp.concatenate(
+        [*halves(query_bias), *halves(value_bias), *halves(fc1_bias), clip_sets.astype(BF)]
+    )
+    extra_lanes = up_to(-(-extra.shape[0] // dc), 128)
+    extra = jnp.pad(extra, (0, dc * extra_lanes - extra.shape[0])).reshape(dc, extra_lanes)
+    small = jnp.concatenate([tables, extra], axis=1)
+    small_lanes = small.shape[1]
+    natural = lanes >= small_lanes
+    small = rows_padded(small, dc, lanes) if natural else small.reshape(-1, lanes)
     small_rows = small.shape[0]
-    at_bias = dr + group
-    at_table = up_to(at_bias + 3, 16)
+    at_table = dr + group
     packed = jnp.concatenate(
         [
-            jnp.concatenate([w_query, w_key, w_value], axis=1),
-            jnp.concatenate([v.reshape(group, width) for v in (query_up, key_up, value_up)], axis=1),
-            rows_padded(
-                jnp.stack([jnp.concatenate([qh, none, vh]), jnp.concatenate([ql, none, vl]), ids]),
-                at_table - at_bias,
-                lanes,
+            jnp.concatenate([w_query, w_key, w_value, w_out.T], axis=1),
+            jnp.concatenate(
+                [v.reshape(group, width) for v in (query_up, key_up, value_up)] + [turn(out_down)], axis=1
             ),
-            rows_padded(small, up_to(small_rows, 16), lanes),
+            rows_padded(small, up_to(small_rows, 8), lanes),
         ],
         axis=0,
     )
     g1 = lax.all_gather(packed, BOTH, axis=0).reshape(nr, nc, -1, lanes)
-    tables = g1[:, :, at_table : at_table + small_rows]
-    if natural:
-        tables = tables[..., : 6 * wide]
-    tables = tables.reshape(D, 6 * wide)
-    every_set = g1[:, 0, at_bias + 2, :clips].astype(jnp.int32)
-    bias_qkv = jnp.sum(g1[0, :, at_bias : at_bias + 2].astype(F32), axis=1, keepdims=True)
-
-    parts = hidden // width
-    rows_w = dr // parts
-    at_w = 2 * dr
-    at_f = up_to(at_w + rows_w, 16)
-    at_o = at_f + 2 * group
-    at_b = at_o + group
-    wo = w_out.T.reshape(parts, rows_w, width).transpose(1, 0, 2).reshape(rows_w, hidden)
-    turn = lambda v: jnp.swapaxes(v, 1, 2).reshape(group, -1)
+    small = g1[:, :, at_table : at_table + small_rows]
+    small = small[..., :small_lanes] if natural else small.reshape(nr, nc, dc, small_lanes)
+    tables = small[..., : 6 * wide].reshape(D, 6 * wide)
+    extra = small[..., 6 * wide :].reshape(nr, nc, -1)
+    sums = extra[0].astype(F32)
+    both = lambda at, n: sums[:, at : at + n] + sums[:, at + n : at + 2 * n]
+    zeros = jnp.zeros((nc, width), F32)
+    bias_qkv = jnp.concatenate([both(0, width), zeros, both(2 * width, width)], axis=1)[:, None]
+    b1 = both(4 * width, hidden)[:, None]
+    every_set = extra[:, 0, 4 * width + 2 * hidden :][:, :clips].astype(jnp.int32)
+    wo_t, odown = assemble(g1, group)
+
     packed = jnp.concatenate(
-        [
-            w_fc1,
-            w_fc2.T,
-            rows_padded(wo, at_f - at_w, hidden),
-            fc1_up.reshape(group, hidden),
-            turn(fc2_down),
-            rows_padded(turn(out_down), group, hidden),
-            rows_padded(jnp.stack(halves(fc1_bias)), 16, hidden),
-        ],
-        axis=0,
+        [w_fc1, w_fc2.T, fc1_up.reshape(group, hidden), turn(fc2_down)], axis=0
     )
     packed, g1 = lax.optimization_barrier((packed, g1))
     g2 = lax.all_gather(packed, BOTH, axis=0).reshape(nr, nc, -1, hidden)
-    wo_t, odown = assemble(g2, at_w, rows_w, at_o, group, width)
-    b1 = jnp.sum(g2[0, :, at_b : at_b + 2].astype(F32), axis=1, keepdims=True)
+    at_f = 2 * dr
 
     gain1, shift1 = norm1_gain[None], norm1_shift[None]
     gain2, shift2 = norm2_gain[None], norm2_shift[None]
@@ -1204,7 +1191,6 @@
 
     by_model = lambda v: v.reshape(nr, nc, dc, wide)
     late = scatter_sum([gup1, gdown2, godown, by_model(gdown1), by_model(goup), by_model(gup2)])
-    late, away, mine = lax.optimization_barrier((late, away, mine))
     late = lax.psum_scatter(late, BOTH, scatter_dimension=0, tiled=True)
 
     def untile(v, n):

time: 808 us -> 761 us (0.942)
  waiting for transfers between devices: 263 us -> 212 us
    all_gather x1, waiting for transfers between devices: 49.5 us -> 5.76 us  [body(): g2 = lax.all_gather(packed, BOTH, axis=0).reshape(nr, nc, -1, hidden)]
    ppermute x2, waiting for transfers between devices: 57.7 us -> 46.5 us  [from_heads(): got_one = lax.ppermute(far, 'cols', [(3, 1), (0, 2)])]
    all_gather x1, waiting for transfers between devices: 112 us -> 120 us  [body(): g1 = lax.all_gather(packed, BOTH, axis=0).reshape(nr, nc, -1, lanes)]
    unnamed x84 -> x72, local copies, waits for them, and re-layouts: 17.4 us -> 15.2 us
  transfers between devices with their start and end apart: 20 -> 20, of which waited for: 8 -> 8; matrix products, arithmetic and copies ran while one was open for 5% -> 7% of each run, Pallas kernels for 20% -> 24%
where the time goes in v5:
time: 761 us; the launch traced here: 755 us
  Pallas kernels  391 us (51%)
  waiting for transfers between devices  212 us (28%)
  starting transfers between devices  59.5 us (8%)
  local copies, waits for them, and re-layouts  58.9 us (8%)
  between operations  16.3 us (2%)
  other arithmetic  11.8 us (2%)
    all_gather x1, waiting for transfers between devices, body(): g1 = lax.all_gather(packed, BOTH, axis=0).reshape(nr, nc, -1, lanes)  120 us
    pallas_call x1, Pallas kernels, mlp(): pl.pallas_call(functools.partial(mlp_kernel, tm, nm, group, per), out_sha...  105 us
    pallas_call x2, Pallas kernels, attend_back(): pl.pallas_call(functools.partial(attend_back_kernel, hh, length, qb, kb,...  88.4 us
    pallas_call x2, Pallas kernels, attend(): pl.pallas_call(functools.partial(attend_kernel, hh, length, qb, kb, len(s...  64.7 us
    ppermute x2, waiting for transfers between devices, from_heads(): got_one = lax.ppermute(far, 'cols', [(3, 1), (0, 2)])  46.5 us
    pallas_call x1, Pallas kernels, project(): pl.pallas_call(functools.partial(project_kernel, tm, width, group, per),...  30.1 us
    optimization_barrier x1, waiting for transfers between devices, body(): late, grad_tokens = lax.optimization_barrier((late, grad_tokens))  29.4 us
    pallas_call x1, Pallas kernels, project_back(): pl.pallas_call(functools.partial(project_back_kernel, tm, width), out_sha...  29.2 us
  transfers between devices with their start and end apart: 20, of which 8 were waited for; matrix products, arithmetic and copies ran while one was open for 7% of the time, Pallas kernels for 24%

profile of v5, /device:TPU:0, one launch (start us, length us, event | category | flops | bytes accessed | tf_op | source)
XLA Modules:
  0.0 755.3 jit_solution(7724746139894090759)
XLA Ops:
  18.5 120.3 %all-gather.5.cloned.1.call-done = bf16[6912,1280]{1,0:T(8,128)(2,1)} async-done(((bf16[216,1280]{1,0:T(8,128)(2,1)}), bf16[6912,1280]{1,0:T(8,128)(2,1)}) %all-gather.5.cloned.1.call-update) | async-done | bytes 17694736 | tf_op jit(solution)/shard_map/all_gather | solution.py:1146
  148.2 30.1 %project.1 = (bf16[1152,1280]{1,0:T(8,128)(2,1)}, bf16[1152,384]{1,0:T(8,128)(2,1)}, bf16[2,1152,1024]{2,1,0:T(8,128)(2,1)}, bf16[2,1152,1024]{2,1,0:T(8,128)(2,1)}) custom-call(s32[3]{0:T(128)} %broadcast_select_fusion.4.sets, f32[3]{0:T(128)} %broadcast_select_fusion.3.scales, s32[4]{0:T(128)} %and_select_fusion.4.order, bf16[1152,1280]{1,0:T(8,128)(2,1)} %x_ref.3, ...), custom_call_target="tpu_custom_call" | custom-call | flops 14722007040 | bytes 24576000 | tf_op jit(solution)/shard_map/project/pallas_call | solution.py:339
  190.3 46.1 %attend.2 = (bf16[2,1536,384]{2,1,0:T(8,128)(2,1)}, f32[2,4,1536]{2,1,0:T(4,128)}, bf16[2,1536,960]{2,1,0:T(8,128)(2,1)}) custom-call(s32[2]{0:T(128)} %pad_add_fusion.1.lens, s32[8]{0:T(128)} %pad_add_fusion.2.plan, s32[4]{0:T(128)} %constant.177.clone.index, bf16[2,1152,1024]{2,1,0:T(8,128)(2,1)} %get-tuple-element.54.refs_0_, ...), custom_call_target="tpu_custom_call" | custom-call | flops 19327352832 | bytes 17694720 | tf_op jit(solution)/shard_map/attend/pallas_call | solution.py:152
  236.4 4.0 collective-permute-start.3
  241.7 18.6 %attend.3 = (bf16[1,1536,384]{2,1,0:T(8,128)(2,1)}, f32[1,4,1536]{2,1,0:T(4,128)}, bf16[1,1536,960]{2,1,0:T(8,128)(2,1)}) custom-call(s32[1]{0:T(128)} %get-tuple-element.58.lens, s32[8]{0:T(128)} %pad_add_fusion.3.plan, s32[4]{0:T(128)} %pad_add_fusion.4.index, bf16[2,1152,1024]{2,1,0:T(8,128)(2,1)} %get-tuple-element.54.refs_0_, ...), custom_call_target="tpu_custom_call" | custom-call | flops 9663676416 | bytes 8847360 | tf_op jit(solution)/shard_map/attend/pallas_call | solution.py:152
  262.4 5.7 collective-permute-start.5
  275.5 5.5 assemble.1
  281.5 7.5 collective-permute-done.5.refs_4_
  291.5 10.9 %collect.1.refs_0_.att_ref = bf16[1152,1280]{1,0:T(8,128)(2,1)} custom-call(s32[36]{0:T(128)} %reshape.377.code, bf16[2,1536,384]{2,1,0:T(8,128)(2,1)} %get-tuple-element.56.refs_0_.refs_3_, bf16[1,1536,384]{2,1,0:T(8,128)(2,1)} %get-tuple-element.59.refs_1_.refs_5_, bf16[2,1536,384]{2,1,0:T(8,128)(2,1)} %copy-done.3, bf16[1,1536,384]{2,1,0:T(8,128)(2,1)} %copy-done.7, ...), custom_call_target="tpu_custom_call" | custom-call | flops 1474560 | bytes 14745600 | tf_op jit(solution)/shard_map/collect/pallas_call | solution.py:597
  302.4 14.3 %out_project.1 = (f32[1152,1280]{1,0:T(8,128)}, bf16[1152,1280]{1,0:T(8,128)(2,1)}, bf16[1152,128]{1,0:T(8,128)(2,1)}, bf16[1152,128]{1,0:T(8,128)(2,1)}) custom-call(s32[3]{0:T(128)} %broadcast_select_fusion.4.sets, f32[3]{0:T(128)} %broadcast_select_fusion.3.scales, bf16[1152,1280]{1,0:T(8,128)(2,1)} %collect.1.refs_0_.att_ref, bf16[1152,1280]{1,0:T(8,128)(2,1)} %x_ref.3, ...), custom_call_target="tpu_custom_call" | custom-call | flops 5662310400 | bytes 20971520 | tf_op jit(solution)/shard_map/out_project/pallas_call | solution.py:635
  316.7 5.8 all-gather.7.cloned.1.call-done
  322.5 104.8 %mlp.1 = (bf16[1152,1280]{1,0:T(8,128)(2,1)}, f32[1152,1280]{1,0:T(8,128)}, bf16[1152,1280]{1,0:T(8,128)(2,1)}, bf16[8,4,160,128]{3,2,1,0:T(8,128)(2,1)}, bf16[8...) custom-call(s32[3]{0:T(128)} %broadcast_select_fusion.4.sets, ...), custom_call_target="tpu_custom_call" | custom-call | flops 72477573120 | bytes 70451200 | tf_op jit(solution)/shard_map/mlp/pallas_call | solution.py:839
  427.3 18.0 %out_back.1 = (bf16[2,1152,384]{2,1,0:T(8,128)(2,1)}, bf16[2,1152,384]{2,1,0:T(8,128)(2,1)}, bf16[1280,128]{1,0:T(8,128)(2,1)}, bf16[8,4,48,128]{3,2,1,0:T(8,128)(2,1)}) custom-call(s32[3]{0:T(128)} %broadcast_select_fusion.4.sets, f32[3]{0:T(128)} %broadcast_select_fusion.3.scales, s32[1]{0:T(128)} %bitcast.26.side, ...), custom_call_target="tpu_custom_call" | custom-call | flops 5662310400 | bytes 12124160 | tf_op jit(solution)/shard_map/out_back/pallas_call | solution.py:716
  452.7 7.1 collective-permute-done.8.refs_2_
  461.4 20.9 %attend_back.2.refs_1_ = bf16[1,1536,1024]{2,1,0:T(8,128)(2,1)} custom-call(s32[1]{0:T(128)} %get-tuple-element.58.lens, s32[8]{0:T(128)} %pad_add_fusion.3.plan, s32[4]{0:T(128)} %pad_add_fusion.4.index, bf16[2,1152,384]{2,1,0:T(8,128)(2,1)} %get-tuple-element.75.refs_0_, bf16[2,1152,384]{2,1,0:T(8,128)(2,1)} %copy-done.26, ...), custom_call_target="tpu_custom_call" | custom-call | flops 24159191040 | bytes 8847360 | tf_op jit(solution)/shard_map/attend_back/pallas_call | solution.py:258
  482.3 67.5 %attend_back.3.refs_0_ = bf16[2,1536,1024]{2,1,0:T(8,128)(2,1)} custom-call(s32[2]{0:T(128)} %pad_add_fusion.1.lens, s32[8]{0:T(128)} %pad_add_fusion.2.plan, s32[4]{0:T(128)} %constant.177.clone.index, bf16[2,1152,384]{2,1,0:T(8,128)(2,1)} %get-tuple-element.75.refs_0_, bf16[2,1152,384]{2,1,0:T(8,128)(2,1)} %copy-done.26, ...), custom_call_target="tpu_custom_call" | custom-call | flops 48318382080 | bytes 17694720 | tf_op jit(solution)/shard_map/attend_back/pallas_call | solution.py:258
  549.8 5.9 collective-permute-start.10
  561.5 5.4 collective-permute-start.12
  572.0 39.0 %collective-permute-done.12.refs_4_ = bf16[1,768,1024]{2,1,0:T(8,128)(2,1)} collective-permute-done((bf16[1,768,1024]{2,1,0:T(8,128)(2,1)}, bf16[1,768,1024]{2,1,0:T(8,128)(2,1)}, u32[]{:S(2)}, u32[]{:S(2)}) %collective-permute-start.12) | collective-permute-done | bytes 1572896 | tf_op jit(solution)/shard_map/ppermute | solution.py:1020
  611.0 25.1 %adapt_back.1 = (bf16[4,1152,960]{2,1,0:T(8,128)(2,1)}, bf16[1152,384]{1,0:T(8,128)(2,1)}, bf16[4,27,16,128]{3,2,1,0:T(8,128)(2,1)}, bf16[2,1280,128]{2,1,0:T(8,128)(2,1)}) custom-call(s32[3]{0:T(128)} %broadcast_select_fusion.4.sets, f32[3]{0:T(128)} %broadcast_select_fusion.3.scales, s32[3]{0:T(128)} %and_select_fusion.12.slots, s32[36]{0:T(128)} %reshape.377.code, ...), custom_call_target="tpu_custom_call" | custom-call | flops 3397386240 | bytes 17694720 | tf_op jit(solution)/shard_map/adapt_back/pallas_call | solution.py:496
  639.0 29.1 %all-to-all-start = ((bf16[32,136,128]{2,1,0:T(8,128)(2,1)}), bf16[32,136,128]{2,1,0:T(8,128)(2,1)S(1)}, u32[]{:S(2)}, u32[]{:S(2)}) async-start(bf16[32,136,128]{2,1,0:T(8,128)(2,1)} %bitcast.36), calls=%async_computation | async-start | bytes 2228224 | tf_op jit(solution)/shard_map/all_to_all | solution.py:1227
  668.1 29.2 %project_back.1 = bf16[1152,1280]{1,0:T(8,128)(2,1)} custom-call(bf16[4,1152,960]{2,1,0:T(8,128)(2,1)} %get-tuple-element.86.dy_ref, bf16[8,4,216,1280]{3,2,1,0:T(8,128)(2,1)} %bitcast.136, bf16[1152,384]{1,0:T(8,128)(2,1)} %get-tuple-element.87.grank_ref, bf16[1280,768]{1,0:T(8,128)(2,1)} %bitcast.144, bf16[1152,1280]{1,0:T(8,128)(2,1)} %x_ref.3, ...), custom_call_target="tpu_custom_call" | custom-call | flops 12457082880 | bytes 30474240 | tf_op jit(solution)/shard_map/project_back/pallas_call | solution.py:562
  697.3 29.4 %reduce-scatter.5.cloned.1.call-done = bf16[488,128]{1,0:T(8,128)(2,1)} async-done(((bf16[15616,128]{1,0:T(8,128)(2,1)}), bf16[488,128]{1,0:T(8,128)(2,1)}) %reduce-scatter.5.cloned.1.call-update) | async-done | bytes 124944 | tf_op jit(solution)/shard_map/optimization_barrier | solution.py:1229
  739.5 5.7 all_gather.19
  (228 shorter events, 83.1 us)
Async XLA Ops:
  7.2 131.6 %all-gather.5.cloned.1.call-start = ((), (), s32[]{:S(2)}) async-start(), calls=%async_computation.2 | async-start | bytes 18247680 | tf_op jit(solution)/shard_map/all_gather | solution.py:1146
  16.3 122.6 %copy-start = (s32[3]{0:T(128)S(1)}, s32[3]{0:T(128)}, u32[]{:S(2)}) copy-start(s32[3]{0:T(128)} %param.36) | copy-start | bytes 40
  16.5 123.1 %copy-start.1 = (f32[3]{0:T(128)S(1)}, f32[3]{0:T(128)}, u32[]{:S(2)}) copy-start(f32[3]{0:T(128)} %param.37) | copy-start | bytes 40
  17.3 122.9 %copy-start.23 = (f32[1280]{0:T(1024)S(1)}, f32[1280]{0:T(1024)}, u32[]{:S(2)}) copy-start(f32[1280]{0:T(1024)} %param.38) | copy-start | bytes 15364
  17.3 123.5 %copy-start.24 = (f32[1280]{0:T(1024)S(1)}, f32[1280]{0:T(1024)}, u32[]{:S(2)}) copy-start(f32[1280]{0:T(1024)} %param.39) | copy-start | bytes 15364
  17.3 305.1 %all-gather.7.cloned.1.call-start = ((), (), s32[]{:S(2)}) async-start(), calls=%async_computation.3 | async-start | bytes 29736960 | tf_op jit(solution)/shard_map/all_gather | solution.py:1163
  138.8 587.9 %reduce-scatter.5.cloned.1.call-start = ((), (), s32[]{:S(2)}) async-start(), calls=%async_computation.4 | async-start | bytes 4122624
  178.3 12.0 %collective-permute-start = (bf16[2,1152,1024]{2,1,0:T(8,128)(2,1)}, bf16[2,1152,1024]{2,1,0:T(8,128)(2,1)}, u32[]{:S(2)}, u32[]{:S(2)}) collective-permute-start(bf16[2,1152,1024]{2,1,0:T(8,128)(2,1)} %get-tuple-element.55), channel_id=1, source_target_pairs={{0,1},{1,0},{2,3},{3,2},{4,5},{5,4},{6,7},{7,6},{8,9},{9,8},{10,11... | collective-permute-start | bytes 14155784 | tf_op jit(solution)/shard_map/ppermute | solution.py:1004
  184.3 57.4 %collective-permute-start.1 = (bf16[1,768,1024]{2,1,0:T(8,128)(2,1)}, bf16[1,768,1024]{2,1,0:T(8,128)(2,1)}, u32[]{:S(2)}, u32[]{:S(2)}) collective-permute-start(bf16[1,768,1024]{2,1,0:T(8,128)(2,1)} %constant_dynamic-slice_fusion.7), channel_id=1, source_target_pairs={{1,3},{2,0},{5,7},{6,4},{9,11},{10,8},{13,15},{14,12},{17,19},{18,... | collective-permute-start | bytes 4718600 | tf_op jit(solution)/shard_map/ppermute | solution.py:1007
  188.3 53.4 %collective-permute-start.2 = (bf16[1,768,1024]{2,1,0:T(8,128)(2,1)}, bf16[1,768,1024]{2,1,0:T(8,128)(2,1)}, u32[]{:S(2)}, u32[]{:S(2)}) collective-permute-start(bf16[1,768,1024]{2,1,0:T(8,128)(2,1)} %constant_dynamic-slice_fusion.6), channel_id=1, source_target_pairs={{1,2},{2,1},{5,6},{6,5},{9,10},{10,9},{13,14},{14,13},{17,18},{18,... | collective-permute-start | bytes 4718600 | tf_op jit(solution)/shard_map/ppermute | solution.py:1008
  236.4 52.7 %collective-permute-start.3 = (bf16[2,1536,384]{2,1,0:T(8,128)(2,1)}, bf16[2,1536,384]{2,1,0:T(8,128)(2,1)S(1)}, u32[]{:S(2)}, u32[]{:S(2)}) collective-permute-start(bf16[2,1536,384]{2,1,0:T(8,128)(2,1)} %get-tuple-element.56.refs_0_.refs_3_), channel_id=1, source_target_pairs={{0,1},{1,0},{2,3},{3,2},{4,5},{5,4},{6,7},{7,6},{8,9},{9,8},{10,11... | collective-permute-start | bytes 7077896 | tf_op jit(solution)/shard_map/ppermute | solution.py:1023
  260.4 28.7 %collective-permute-start.4 = (bf16[1,1536,384]{2,1,0:T(8,128)(2,1)}, bf16[1,1536,384]{2,1,0:T(8,128)(2,1)S(1)}, u32[]{:S(2)}, u32[]{:S(2)}) collective-permute-start(bf16[1,1536,384]{2,1,0:T(8,128)(2,1)} %get-tuple-element.59.refs_1_.refs_5_), channel_id=1, source_target_pairs={{0,1},{1,0},{2,3},{3,2},{4,5},{5,4},{6,7},{7,6},{8,9},{9,8},{10,11... | collective-permute-start | bytes 3538952 | tf_op jit(solution)/shard_map/ppermute | solution.py:1022
  262.4 26.7 %collective-permute-start.5 = (bf16[1,768,384]{2,1,0:T(8,128)(2,1)}, bf16[1,768,384]{2,1,0:T(8,128)(2,1)}, u32[]{:S(2)}, u32[]{:S(2)}) collective-permute-start(bf16[1,768,384]{2,1,0:T(8,128)(2,1)} %constant_dynamic-slice_fusion.5), channel_id=1, source_target_pairs={{3,1},{0,2},{7,5},{4,6},{11,9},{8,10},{15,13},{12,14},{19,17},{16,... | collective-permute-start | bytes 1769480 | tf_op jit(solution)/shard_map/ppermute | solution.py:1020
  268.0 21.0 %collective-permute-start.6 = (bf16[1,768,384]{2,1,0:T(8,128)(2,1)}, bf16[1,768,384]{2,1,0:T(8,128)(2,1)}, u32[]{:S(2)}, u32[]{:S(2)}) collective-permute-start(bf16[1,768,384]{2,1,0:T(8,128)(2,1)} %constant_dynamic-slice_fusion.5), channel_id=1, source_target_pairs={{2,1},{1,2},{6,5},{5,6},{10,9},{9,10},{14,13},{13,14},{18,17},{17,... | collective-permute-start | bytes 1769480 | tf_op jit(solution)/shard_map/ppermute | solution.py:1021
  445.3 14.5 %collective-permute-start.7 = (bf16[2,1152,384]{2,1,0:T(8,128)(2,1)}, bf16[2,1152,384]{2,1,0:T(8,128)(2,1)S(1)}, u32[]{:S(2)}, u32[]{:S(2)}) collective-permute-start(bf16[2,1152,384]{2,1,0:T(8,128)(2,1)} %get-tuple-element.76), channel_id=1, source_target_pairs={{0,1},{1,0},{2,3},{3,2},{4,5},{5,4},{6,7},{7,6},{8,9},{9,8},{10,11... | collective-permute-start | bytes 5308424 | tf_op jit(solution)/shard_map/ppermute | solution.py:1004
  448.0 11.8 %collective-permute-start.8 = (bf16[1,768,384]{2,1,0:T(8,128)(2,1)S(1)}, bf16[1,768,384]{2,1,0:T(8,128)(2,1)S(1)}, u32[]{:S(2)}, u32[]{:S(2)}) collective-permute-start(bf16[1,768,384]{2,1,0:T(8,128)(2,1)S(1)} %constant_dynamic-slice_fusion.4), channel_id=1, source_target_pairs={{1,3},{2,0},{5,7},{6,4},{9,11},{10,8},{13,15},{14,12},{17,19},{18,... | collective-permute-start | bytes 1769480 | tf_op jit(solution)/shard_map/ppermute | solution.py:1007
  449.3 10.5 %collective-permute-start.9 = (bf16[1,768,384]{2,1,0:T(8,128)(2,1)S(1)}, bf16[1,768,384]{2,1,0:T(8,128)(2,1)S(1)}, u32[]{:S(2)}, u32[]{:S(2)}) collective-permute-start(bf16[1,768,384]{2,1,0:T(8,128)(2,1)S(1)} %constant_dynamic-slice_fusion.3), channel_id=1, source_target_pairs={{1,2},{2,1},{5,6},{6,5},{9,10},{10,9},{13,14},{14,13},{17,18},{18,... | collective-permute-start | bytes 1769480 | tf_op jit(solution)/shard_map/ppermute | solution.py:1008
  549.8 61.2 %collective-permute-start.10 = (bf16[2,1536,1024]{2,1,0:T(8,128)(2,1)}, bf16[2,1536,1024]{2,1,0:T(8,128)(2,1)}, u32[]{:S(2)}, u32[]{:S(2)}) collective-permute-start(bf16[2,1536,1024]{2,1,0:T(8,128)(2,1)} %attend_back.3.refs_0_), channel_id=1, source_target_pairs={{0,1},{1,0},{2,3},{3,2},{4,5},{5,4},{6,7},{7,6},{8,9},{9,8},{10,11... | collective-permute-start | bytes 18874376 | tf_op jit(solution)/shard_map/ppermute | solution.py:1023
  560.3 50.7 %collective-permute-start.11 = (bf16[1,1536,1024]{2,1,0:T(8,128)(2,1)S(1)}, bf16[1,1536,1024]{2,1,0:T(8,128)(2,1)}, u32[]{:S(2)}, u32[]{:S(2)}) collective-permute-start(bf16[1,1536,1024]{2,1,0:T(8,128)(2,1)S(1)} %copy-done.2), channel_id=1, source_target_pairs={{0,1},{1,0},{2,3},{3,2},{4,5},{5,4},{6,7},{7,6},{8,9},{9,8},{10,11... | collective-permute-start | bytes 9437192 | tf_op jit(solution)/shard_map/ppermute | solution.py:1022
  561.5 49.4 %collective-permute-start.12 = (bf16[1,768,1024]{2,1,0:T(8,128)(2,1)}, bf16[1,768,1024]{2,1,0:T(8,128)(2,1)}, u32[]{:S(2)}, u32[]{:S(2)}) collective-permute-start(bf16[1,768,1024]{2,1,0:T(8,128)(2,1)} %constant_dynamic-slice_fusion.2), channel_id=1, source_target_pairs={{3,1},{0,2},{7,5},{4,6},{11,9},{8,10},{15,13},{12,14},{19,17},{16,... | collective-permute-start | bytes 4718600 | tf_op jit(solution)/shard_map/ppermute | solution.py:1020
  566.9 44.1 %collective-permute-start.13 = (bf16[1,768,1024]{2,1,0:T(8,128)(2,1)}, bf16[1,768,1024]{2,1,0:T(8,128)(2,1)}, u32[]{:S(2)}, u32[]{:S(2)}) collective-permute-start(bf16[1,768,1024]{2,1,0:T(8,128)(2,1)} %constant_dynamic-slice_fusion.2), channel_id=1, source_target_pairs={{2,1},{1,2},{6,5},{5,6},{10,9},{9,10},{14,13},{13,14},{18,17},{17,... | collective-permute-start | bytes 4718600 | tf_op jit(solution)/shard_map/ppermute | solution.py:1021
  639.0 98.8 %all-to-all-start = ((bf16[32,136,128]{2,1,0:T(8,128)(2,1)}), bf16[32,136,128]{2,1,0:T(8,128)(2,1)S(1)}, u32[]{:S(2)}, u32[]{:S(2)}) async-start(bf16[32,136,128]{2,1,0:T(8,128)(2,1)} %bitcast.36), calls=%async_computation | async-start | bytes 2228224 | tf_op jit(solution)/shard_map/all_to_all | solution.py:1227
  727.7 1.3 collective-permute-start.14
  729.0 5.4 collective-permute-start.15
  (26 other events, 432.7 us)
Sparse Core Ops, SparseCore 0:
  17.5 121.2 all-gather.4
  141.6 180.7 all-gather.6
  559.2 167.4 reduce-scatter.4

commit v6 on v5

--- a/solution.py
+++ b/solution.py
@@ -1041,20 +1041,6 @@
     n = whole.shape[2]
     whole = jnp.pad(whole, ((0, 0), (0, 0), (0, up_to(n, 8) - n), (0, 0)))
     return whole.reshape(-1, 128)
-
-
-def join(v, nc):
-    col = lax.axis_index("cols")
-    zeros = (0,) * v.ndim
-    held = lax.dynamic_update_slice(jnp.zeros((nc,) + v.shape, v.dtype), v[None], (col,) + zeros)
-    step = 1
-    while step < nc:
-        base = col // step * step
-        sent = lax.dynamic_slice(held, (base,) + zeros, (step,) + v.shape)
-        got = lax.ppermute(sent, "cols", [(i, i ^ step) for i in range(nc)])
-        held = lax.dynamic_update_slice(held, got, (base ^ step,) + zeros)
-        step *= 2
-    return held
 
 
 def body(
@@ -1197,11 +1183,6 @@
         t = v.shape[0] // group
         return v.reshape(t, group, 128).transpose(1, 0, 2).reshape(group, t * 128)[:, :n].reshape(SETS, per, n)
 
-    def model_tables(v):
-        k = v.shape[0] // dc
-        every = join(v, nc).reshape(nc, k, dc, wide).swapaxes(0, 1)
-        return every.reshape(k, dr, nr, SETS, per)
-
     as_down = lambda v: v.transpose(2, 0, 1, 3).reshape(SETS, dr, RANK)
     as_up = lambda v: v.transpose(2, 1, 3, 0).reshape(SETS, RANK, dr)
     flip = lambda v: jnp.swapaxes(v, 1, 2)
@@ -1233,8 +1214,8 @@
     grad_fc1_up = untile(summed[:a], hidden)
     grad_fc2_down = flip(untile(summed[a : 2 * a], hidden))
     grad_out_down = flip(untile(summed[2 * a : 2 * a + b], width))
-    model = model_tables(summed[2 * a + b : 2 * a + b + 3 * dc])
-    grad_fc1_down, grad_out_up, grad_fc2_up = as_down(model[0]), as_up(model[1]), as_up(model[2])
+    model = summed[2 * a + b : 2 * a + b + 3 * dc].reshape(3, dc, wide)
+    model = model.transpose(1, 0, 2).reshape(dc, 3 * wide)
 
     got = jnp.sum(got.reshape(nr, nc, -1, 128).astype(F32), axis=1)
     onehot = (every_set[:, :, None] == jnp.arange(SETS, dtype=jnp.int32)).astype(F32)
@@ -1248,8 +1229,10 @@
     side = side.reshape(nr, dc, clips, 3 * RANK).transpose(0, 2, 1, 3)
     side = jnp.sum(onehot[:, :, :, None, None] * side[:, :, None], axis=(0, 1))
     side = side.transpose(1, 0, 2).reshape(dc, SETS * 3 * RANK)
-    side = lax.all_gather(side, "cols", axis=0, tiled=True).reshape(dr, SETS, 3, RANK)
-    down = side.transpose(2, 1, 0, 3)
+    every = lax.all_gather(jnp.concatenate([side, model], axis=1), "cols", axis=0, tiled=True)
+    down = every[:, : SETS * 3 * RANK].reshape(dr, SETS, 3, RANK).transpose(2, 1, 0, 3)
+    model = every[:, SETS * 3 * RANK :].reshape(dr, 3, nr, SETS, per).swapaxes(0, 1)
+    grad_fc1_down, grad_out_up, grad_fc2_up = as_down(model[0]), as_up(model[1]), as_up(model[2])
     return (
         output,
         grad_tokens,

time: 761 us -> 760 us (level)
    unnamed x72 -> x78, local copies, waits for them, and re-layouts: 15.2 us -> 17.9 us
  transfers between devices with their start and end apart: 20 -> 18, of which waited for: 8 -> 6; matrix products, arithmetic and copies ran while one was open for 7% -> 6% of each run, Pallas kernels for 24% -> 24%
where the time goes in v6:
time: 760 us; the launch traced here: 754 us
  Pallas kernels  391 us (51%)
  waiting for transfers between devices  213 us (28%)
  local copies, waits for them, and re-layouts  59 us (8%)
  starting transfers between devices  57.9 us (8%)
  between operations  16.2 us (2%)
  other arithmetic  10.9 us (1%)
    all_gather x1, waiting for transfers between devices, body(): g1 = lax.all_gather(packed, BOTH, axis=0).reshape(nr, nc, -1, lanes)  120 us
    pallas_call x1, Pallas kernels, mlp(): pl.pallas_call(functools.partial(mlp_kernel, tm, nm, group, per), out_sha...  105 us
    pallas_call x2, Pallas kernels, attend_back(): pl.pallas_call(functools.partial(attend_back_kernel, hh, length, qb, kb,...  88.5 us
    pallas_call x2, Pallas kernels, attend(): pl.pallas_call(functools.partial(attend_kernel, hh, length, qb, kb, len(s...  64.7 us
    ppermute x2, waiting for transfers between devices, from_heads(): got_one = lax.ppermute(far, 'cols', [(3, 1), (0, 2)])  49.8 us
    pallas_call x1, Pallas kernels, project(): pl.pallas_call(functools.partial(project_kernel, tm, width, group, per),...  30.1 us
    all_to_all x1, starting transfers between devices, body(): got = lax.all_to_all(last, BOTH, 0, 0, tiled=True)  29.8 us
    pallas_call x1, Pallas kernels, project_back(): pl.pallas_call(functools.partial(project_back_kernel, tm, width), out_sha...  29.2 us
  transfers between devices with their start and end apart: 18, of which 6 were waited for; matrix products, arithmetic and copies ran while one was open for 6% of the time, Pallas kernels for 24%

profile of v6, /device:TPU:0, one launch (start us, length us, event | category | flops | bytes accessed | tf_op | source)
XLA Modules:
  0.0 754.0 jit_solution(16700759657096287360)
XLA Ops:
  18.5 120.3 %all-gather.5.cloned.1.call-done = bf16[6912,1280]{1,0:T(8,128)(2,1)} async-done(((bf16[216,1280]{1,0:T(8,128)(2,1)}), bf16[6912,1280]{1,0:T(8,128)(2,1)}) %all-gather.5.cloned.1.call-update) | async-done | bytes 17694736 | tf_op jit(solution)/shard_map/all_gather | solution.py:1132
  148.2 30.1 %project.1 = (bf16[1152,1280]{1,0:T(8,128)(2,1)}, bf16[1152,384]{1,0:T(8,128)(2,1)}, bf16[2,1152,1024]{2,1,0:T(8,128)(2,1)}, bf16[2,1152,1024]{2,1,0:T(8,128)(2,1)}) custom-call(s32[3]{0:T(128)} %broadcast_select_fusion.4.sets, f32[3]{0:T(128)} %broadcast_select_fusion.3.scales, s32[4]{0:T(128)} %and_select_fusion.4.order, bf16[1152,1280]{1,0:T(8,128)(2,1)} %x_ref.3, ...), custom_call_target="tpu_custom_call" | custom-call | flops 14722007040 | bytes 24576000 | tf_op jit(solution)/shard_map/project/pallas_call | solution.py:339
  190.4 46.1 %attend.2 = (bf16[2,1536,384]{2,1,0:T(8,128)(2,1)}, f32[2,4,1536]{2,1,0:T(4,128)}, bf16[2,1536,960]{2,1,0:T(8,128)(2,1)}) custom-call(s32[2]{0:T(128)} %pad_add_fusion.1.lens, s32[8]{0:T(128)} %pad_add_fusion.2.plan, s32[4]{0:T(128)} %constant.166.clone.index, bf16[2,1152,1024]{2,1,0:T(8,128)(2,1)} %get-tuple-element.54.refs_0_, ...), custom_call_target="tpu_custom_call" | custom-call | flops 19327352832 | bytes 17694720 | tf_op jit(solution)/shard_map/attend/pallas_call | solution.py:152
  236.5 4.0 collective-permute-start.3
  241.8 18.6 %attend.3 = (bf16[1,1536,384]{2,1,0:T(8,128)(2,1)}, f32[1,4,1536]{2,1,0:T(4,128)}, bf16[1,1536,960]{2,1,0:T(8,128)(2,1)}) custom-call(s32[1]{0:T(128)} %get-tuple-element.58.lens, s32[8]{0:T(128)} %pad_add_fusion.3.plan, s32[4]{0:T(128)} %pad_add_fusion.4.index, bf16[2,1152,1024]{2,1,0:T(8,128)(2,1)} %get-tuple-element.54.refs_0_, ...), custom_call_target="tpu_custom_call" | custom-call | flops 9663676416 | bytes 8847360 | tf_op jit(solution)/shard_map/attend/pallas_call | solution.py:152
  262.4 5.7 collective-permute-start.5
  275.6 5.5 assemble.1
  281.7 7.4 collective-permute-done.5.refs_4_
  291.5 10.9 %collect.1.refs_0_.att_ref = bf16[1152,1280]{1,0:T(8,128)(2,1)} custom-call(s32[36]{0:T(128)} %reshape.376.code, bf16[2,1536,384]{2,1,0:T(8,128)(2,1)} %get-tuple-element.56.refs_0_.refs_3_, bf16[1,1536,384]{2,1,0:T(8,128)(2,1)} %get-tuple-element.59.refs_1_.refs_5_, bf16[2,1536,384]{2,1,0:T(8,128)(2,1)} %copy-done.4, bf16[1,1536,384]{2,1,0:T(8,128)(2,1)} %copy-done.10, ...), custom_call_target="tpu_custom_call" | custom-call | flops 1474560 | bytes 14745600 | tf_op jit(solution)/shard_map/collect/pallas_call | solution.py:597
  302.4 14.3 %out_project.1 = (f32[1152,1280]{1,0:T(8,128)}, bf16[1152,1280]{1,0:T(8,128)(2,1)}, bf16[1152,128]{1,0:T(8,128)(2,1)}, bf16[1152,128]{1,0:T(8,128)(2,1)}) custom-call(s32[3]{0:T(128)} %broadcast_select_fusion.4.sets, f32[3]{0:T(128)} %broadcast_select_fusion.3.scales, bf16[1152,1280]{1,0:T(8,128)(2,1)} %collect.1.refs_0_.att_ref, bf16[1152,1280]{1,0:T(8,128)(2,1)} %x_ref.3, ...), custom_call_target="tpu_custom_call" | custom-call | flops 5662310400 | bytes 20971520 | tf_op jit(solution)/shard_map/out_project/pallas_call | solution.py:635
  316.7 5.6 all-gather.7.cloned.1.call-done
  322.4 104.8 %mlp.1 = (bf16[1152,1280]{1,0:T(8,128)(2,1)}, f32[1152,1280]{1,0:T(8,128)}, bf16[1152,1280]{1,0:T(8,128)(2,1)}, bf16[8,4,160,128]{3,2,1,0:T(8,128)(2,1)}, bf16[8...) custom-call(s32[3]{0:T(128)} %broadcast_select_fusion.4.sets, ...), custom_call_target="tpu_custom_call" | custom-call | flops 72477573120 | bytes 70451200 | tf_op jit(solution)/shard_map/mlp/pallas_call | solution.py:839
  427.2 18.0 %out_back.1 = (bf16[2,1152,384]{2,1,0:T(8,128)(2,1)}, bf16[2,1152,384]{2,1,0:T(8,128)(2,1)}, bf16[1280,128]{1,0:T(8,128)(2,1)}, bf16[8,4,48,128]{3,2,1,0:T(8,128)(2,1)}) custom-call(s32[3]{0:T(128)} %broadcast_select_fusion.4.sets, f32[3]{0:T(128)} %broadcast_select_fusion.3.scales, s32[1]{0:T(128)} %bitcast.26.side, ...), custom_call_target="tpu_custom_call" | custom-call | flops 5662310400 | bytes 12124160 | tf_op jit(solution)/shard_map/out_back/pallas_call | solution.py:716
  449.7 9.8 %collective-permute-done.8.refs_2_ = bf16[1,768,384]{2,1,0:T(8,128)(2,1)S(1)} collective-permute-done((bf16[1,768,384]{2,1,0:T(8,128)(2,1)S(1)}, bf16[1,768,384]{2,1,0:T(8,128)(2,1)S(1)}, u32[]{:S(2)}, u32[]{:S(2)}) %collective-permute-start.8) | collective-permute-done | bytes 589856 | tf_op jit(solution)/shard_map/ppermute | solution.py:1007
  461.2 21.0 %attend_back.2.refs_1_ = bf16[1,1536,1024]{2,1,0:T(8,128)(2,1)} custom-call(s32[1]{0:T(128)} %get-tuple-element.58.lens, s32[8]{0:T(128)} %pad_add_fusion.3.plan, s32[4]{0:T(128)} %pad_add_fusion.4.index, bf16[2,1152,384]{2,1,0:T(8,128)(2,1)} %get-tuple-element.75.refs_0_, bf16[2,1152,384]{2,1,0:T(8,128)(2,1)} %copy-done.29, ...), custom_call_target="tpu_custom_call" | custom-call | flops 24159191040 | bytes 8847360 | tf_op jit(solution)/shard_map/attend_back/pallas_call | solution.py:258
  482.2 67.5 %attend_back.3.refs_0_ = bf16[2,1536,1024]{2,1,0:T(8,128)(2,1)} custom-call(s32[2]{0:T(128)} %pad_add_fusion.1.lens, s32[8]{0:T(128)} %pad_add_fusion.2.plan, s32[4]{0:T(128)} %constant.166.clone.index, bf16[2,1152,384]{2,1,0:T(8,128)(2,1)} %get-tuple-element.75.refs_0_, bf16[2,1152,384]{2,1,0:T(8,128)(2,1)} %copy-done.29, ...), custom_call_target="tpu_custom_call" | custom-call | flops 48318382080 | bytes 17694720 | tf_op jit(solution)/shard_map/attend_back/pallas_call | solution.py:258
  549.7 5.9 collective-permute-start.10
  563.1 4.1 collective-permute-start.12
  568.5 42.4 %collective-permute-done.12.refs_4_ = bf16[1,768,1024]{2,1,0:T(8,128)(2,1)S(1)} collective-permute-done((bf16[1,768,1024]{2,1,0:T(8,128)(2,1)S(1)}, bf16[1,768,1024]{2,1,0:T(8,128)(2,1)S(1)}, u32[]{:S(2)}, u32[]{:S(2)}) %collective-permute-start.12) | collective-permute-done | bytes 1572896 | tf_op jit(solution)/shard_map/ppermute | solution.py:1020
  613.6 25.1 %adapt_back.1 = (bf16[4,1152,960]{2,1,0:T(8,128)(2,1)}, bf16[1152,384]{1,0:T(8,128)(2,1)}, bf16[4,27,16,128]{3,2,1,0:T(8,128)(2,1)}, bf16[2,1280,128]{2,1,0:T(8,128)(2,1)}) custom-call(s32[3]{0:T(128)} %broadcast_select_fusion.4.sets, f32[3]{0:T(128)} %broadcast_select_fusion.3.scales, s32[3]{0:T(128)} %and_select_fusion.12.slots, s32[36]{0:T(128)} %reshape.376.code, ...), custom_call_target="tpu_custom_call" | custom-call | flops 3397386240 | bytes 17694720 | tf_op jit(solution)/shard_map/adapt_back/pallas_call | solution.py:496
  641.6 29.8 %all-to-all-start = ((bf16[32,136,128]{2,1,0:T(8,128)(2,1)}), bf16[32,136,128]{2,1,0:T(8,128)(2,1)S(1)}, u32[]{:S(2)}, u32[]{:S(2)}) async-start(bf16[32,136,128]{2,1,0:T(8,128)(2,1)} %bitcast.36), calls=%async_computation | async-start | bytes 2228224 | tf_op jit(solution)/shard_map/all_to_all | solution.py:1208
  672.7 29.2 %project_back.1 = bf16[1152,1280]{1,0:T(8,128)(2,1)} custom-call(bf16[4,1152,960]{2,1,0:T(8,128)(2,1)} %get-tuple-element.86.dy_ref, bf16[8,4,216,1280]{3,2,1,0:T(8,128)(2,1)} %bitcast.142, bf16[1152,384]{1,0:T(8,128)(2,1)} %get-tuple-element.87.grank_ref, bf16[1280,768]{1,0:T(8,128)(2,1)} %bitcast.150, bf16[1152,1280]{1,0:T(8,128)(2,1)} %x_ref.3, ...), custom_call_target="tpu_custom_call" | custom-call | flops 12457082880 | bytes 30474240 | tf_op jit(solution)/shard_map/project_back/pallas_call | solution.py:562
  701.9 26.9 %reduce-scatter.5.cloned.1.call-done = bf16[488,128]{1,0:T(8,128)(2,1)} async-done(((bf16[15616,128]{1,0:T(8,128)(2,1)}), bf16[488,128]{1,0:T(8,128)(2,1)}) %reduce-scatter.5.cloned.1.call-update) | async-done | bytes 124944 | tf_op jit(solution)/shard_map/optimization_barrier | solution.py:1210
  734.8 6.4 all_gather.19
  (223 shorter events, 78.4 us)
Async XLA Ops:
  7.2 131.6 %all-gather.5.cloned.1.call-start = ((), (), s32[]{:S(2)}) async-start(), calls=%async_computation.2 | async-start | bytes 18247680 | tf_op jit(solution)/shard_map/all_gather | solution.py:1132
  16.3 122.6 %copy-start = (s32[3]{0:T(128)S(1)}, s32[3]{0:T(128)}, u32[]{:S(2)}) copy-start(s32[3]{0:T(128)} %param.36) | copy-start | bytes 40
  16.5 123.1 %copy-start.1 = (f32[3]{0:T(128)S(1)}, f32[3]{0:T(128)}, u32[]{:S(2)}) copy-start(f32[3]{0:T(128)} %param.37) | copy-start | bytes 40
  17.3 122.9 %copy-start.26 = (f32[1280]{0:T(1024)S(1)}, f32[1280]{0:T(1024)}, u32[]{:S(2)}) copy-start(f32[1280]{0:T(1024)} %param.38) | copy-start | bytes 15364
  17.3 123.5 %copy-start.27 = (f32[1280]{0:T(1024)S(1)}, f32[1280]{0:T(1024)}, u32[]{:S(2)}) copy-start(f32[1280]{0:T(1024)} %param.39) | copy-start | bytes 15364
  17.3 305.0 %all-gather.7.cloned.1.call-start = ((), (), s32[]{:S(2)}) async-start(), calls=%async_computation.3 | async-start | bytes 29736960 | tf_op jit(solution)/shard_map/all_gather | solution.py:1149
  138.8 589.9 %reduce-scatter.5.cloned.1.call-start = ((), (), s32[]{:S(2)}) async-start(), calls=%async_computation.4 | async-start | bytes 4122624
  148.2 30.3 %copy-start.28 = (s32[3]{0:T(128)S(1)}, s32[3]{0:T(128)}, u32[]{:S(2)}) copy-start(s32[3]{0:T(128)} %param.35) | copy-start | bytes 40
  178.3 12.1 %collective-permute-start = (bf16[2,1152,1024]{2,1,0:T(8,128)(2,1)}, bf16[2,1152,1024]{2,1,0:T(8,128)(2,1)}, u32[]{:S(2)}, u32[]{:S(2)}) collective-permute-start(bf16[2,1152,1024]{2,1,0:T(8,128)(2,1)} %get-tuple-element.55), channel_id=1, source_target_pairs={{0,1},{1,0},{2,3},{3,2},{4,5},{5,4},{6,7},{7,6},{8,9},{9,8},{10,11... | collective-permute-start | bytes 14155784 | tf_op jit(solution)/shard_map/ppermute | solution.py:1004
  184.4 57.4 %collective-permute-start.1 = (bf16[1,768,1024]{2,1,0:T(8,128)(2,1)}, bf16[1,768,1024]{2,1,0:T(8,128)(2,1)}, u32[]{:S(2)}, u32[]{:S(2)}) collective-permute-start(bf16[1,768,1024]{2,1,0:T(8,128)(2,1)} %constant_dynamic-slice_fusion.5), channel_id=1, source_target_pairs={{1,3},{2,0},{5,7},{6,4},{9,11},{10,8},{13,15},{14,12},{17,19},{18,... | collective-permute-start | bytes 4718600 | tf_op jit(solution)/shard_map/ppermute | solution.py:1007
  188.4 53.4 %collective-permute-start.2 = (bf16[1,768,1024]{2,1,0:T(8,128)(2,1)}, bf16[1,768,1024]{2,1,0:T(8,128)(2,1)}, u32[]{:S(2)}, u32[]{:S(2)}) collective-permute-start(bf16[1,768,1024]{2,1,0:T(8,128)(2,1)} %constant_dynamic-slice_fusion.4), channel_id=1, source_target_pairs={{1,2},{2,1},{5,6},{6,5},{9,10},{10,9},{13,14},{14,13},{17,18},{18,... | collective-permute-start | bytes 4718600 | tf_op jit(solution)/shard_map/ppermute | solution.py:1008
  236.5 52.6 %collective-permute-start.3 = (bf16[2,1536,384]{2,1,0:T(8,128)(2,1)}, bf16[2,1536,384]{2,1,0:T(8,128)(2,1)S(1)}, u32[]{:S(2)}, u32[]{:S(2)}) collective-permute-start(bf16[2,1536,384]{2,1,0:T(8,128)(2,1)} %get-tuple-element.56.refs_0_.refs_3_), channel_id=1, source_target_pairs={{0,1},{1,0},{2,3},{3,2},{4,5},{5,4},{6,7},{7,6},{8,9},{9,8},{10,11... | collective-permute-start | bytes 7077896 | tf_op jit(solution)/shard_map/ppermute | solution.py:1023
  260.4 28.6 %collective-permute-start.4 = (bf16[1,1536,384]{2,1,0:T(8,128)(2,1)}, bf16[1,1536,384]{2,1,0:T(8,128)(2,1)S(1)}, u32[]{:S(2)}, u32[]{:S(2)}) collective-permute-start(bf16[1,1536,384]{2,1,0:T(8,128)(2,1)} %get-tuple-element.59.refs_1_.refs_5_), channel_id=1, source_target_pairs={{0,1},{1,0},{2,3},{3,2},{4,5},{5,4},{6,7},{7,6},{8,9},{9,8},{10,11... | collective-permute-start | bytes 3538952 | tf_op jit(solution)/shard_map/ppermute | solution.py:1022
  262.4 26.6 %collective-permute-start.5 = (bf16[1,768,384]{2,1,0:T(8,128)(2,1)}, bf16[1,768,384]{2,1,0:T(8,128)(2,1)}, u32[]{:S(2)}, u32[]{:S(2)}) collective-permute-start(bf16[1,768,384]{2,1,0:T(8,128)(2,1)} %constant_dynamic-slice_fusion.3), channel_id=1, source_target_pairs={{3,1},{0,2},{7,5},{4,6},{11,9},{8,10},{15,13},{12,14},{19,17},{16,... | collective-permute-start | bytes 1769480 | tf_op jit(solution)/shard_map/ppermute | solution.py:1020
  268.1 21.0 %collective-permute-start.6 = (bf16[1,768,384]{2,1,0:T(8,128)(2,1)}, bf16[1,768,384]{2,1,0:T(8,128)(2,1)}, u32[]{:S(2)}, u32[]{:S(2)}) collective-permute-start(bf16[1,768,384]{2,1,0:T(8,128)(2,1)} %constant_dynamic-slice_fusion.3), channel_id=1, source_target_pairs={{2,1},{1,2},{6,5},{5,6},{10,9},{9,10},{14,13},{13,14},{18,17},{17,... | collective-permute-start | bytes 1769480 | tf_op jit(solution)/shard_map/ppermute | solution.py:1021
  445.1 14.3 %collective-permute-start.7 = (bf16[2,1152,384]{2,1,0:T(8,128)(2,1)}, bf16[2,1152,384]{2,1,0:T(8,128)(2,1)S(1)}, u32[]{:S(2)}, u32[]{:S(2)}) collective-permute-start(bf16[2,1152,384]{2,1,0:T(8,128)(2,1)} %get-tuple-element.76), channel_id=1, source_target_pairs={{0,1},{1,0},{2,3},{3,2},{4,5},{5,4},{6,7},{7,6},{8,9},{9,8},{10,11... | collective-permute-start | bytes 5308424 | tf_op jit(solution)/shard_map/ppermute | solution.py:1004
  447.7 11.8 %collective-permute-start.8 = (bf16[1,768,384]{2,1,0:T(8,128)(2,1)S(1)}, bf16[1,768,384]{2,1,0:T(8,128)(2,1)S(1)}, u32[]{:S(2)}, u32[]{:S(2)}) collective-permute-start(bf16[1,768,384]{2,1,0:T(8,128)(2,1)S(1)} %constant_dynamic-slice_fusion.2), channel_id=1, source_target_pairs={{1,3},{2,0},{5,7},{6,4},{9,11},{10,8},{13,15},{14,12},{17,19},{18,... | collective-permute-start | bytes 1769480 | tf_op jit(solution)/shard_map/ppermute | solution.py:1007
  449.0 10.5 %collective-permute-start.9 = (bf16[1,768,384]{2,1,0:T(8,128)(2,1)S(1)}, bf16[1,768,384]{2,1,0:T(8,128)(2,1)S(1)}, u32[]{:S(2)}, u32[]{:S(2)}) collective-permute-start(bf16[1,768,384]{2,1,0:T(8,128)(2,1)S(1)} %constant_dynamic-slice_fusion.1), channel_id=1, source_target_pairs={{1,2},{2,1},{5,6},{6,5},{9,10},{10,9},{13,14},{14,13},{17,18},{18,... | collective-permute-start | bytes 1769480 | tf_op jit(solution)/shard_map/ppermute | solution.py:1008
  482.2 73.3 %copy-start.9 = (bf16[8,4,160,128]{3,2,1,0:T(8,128)(2,1)S(1)}, bf16[8,4,160,128]{3,2,1,0:T(8,128)(2,1)}, u32[]{:S(2)}) copy-start(bf16[8,4,160,128]{3,2,1,0:T(8,128)(2,1)} %get-tuple-element.67) | copy-start | bytes 3932164
  549.7 62.9 %collective-permute-start.10 = (bf16[2,1536,1024]{2,1,0:T(8,128)(2,1)}, bf16[2,1536,1024]{2,1,0:T(8,128)(2,1)}, u32[]{:S(2)}, u32[]{:S(2)}) collective-permute-start(bf16[2,1536,1024]{2,1,0:T(8,128)(2,1)} %attend_back.3.refs_0_), channel_id=1, source_target_pairs={{0,1},{1,0},{2,3},{3,2},{4,5},{5,4},{6,7},{7,6},{8,9},{9,8},{10,11... | collective-permute-start | bytes 18874376 | tf_op jit(solution)/shard_map/ppermute | solution.py:1023
  562.7 48.2 %collective-permute-start.11 = (bf16[1,1536,1024]{2,1,0:T(8,128)(2,1)S(1)}, bf16[1,1536,1024]{2,1,0:T(8,128)(2,1)S(1)}, u32[]{:S(2)}, u32[]{:S(2)}) collective-permute-start(bf16[1,1536,1024]{2,1,0:T(8,128)(2,1)S(1)} %copy-done.2), channel_id=1, source_target_pairs={{0,1},{1,0},{2,3},{3,2},{4,5},{5,4},{6,7},{7,6},{8,9},{9,8},{10,11... | collective-permute-start | bytes 9437192 | tf_op jit(solution)/shard_map/ppermute | solution.py:1022
  563.1 47.8 %collective-permute-start.12 = (bf16[1,768,1024]{2,1,0:T(8,128)(2,1)S(1)}, bf16[1,768,1024]{2,1,0:T(8,128)(2,1)S(1)}, u32[]{:S(2)}, u32[]{:S(2)}) collective-permute-start(bf16[1,768,1024]{2,1,0:T(8,128)(2,1)S(1)} %constant_dynamic-slice_fusion), channel_id=1, source_target_pairs={{3,1},{0,2},{7,5},{4,6},{11,9},{8,10},{15,13},{12,14},{19,17},{16,... | collective-permute-start | bytes 4718600 | tf_op jit(solution)/shard_map/ppermute | solution.py:1020
  567.2 43.7 %collective-permute-start.13 = (bf16[1,768,1024]{2,1,0:T(8,128)(2,1)S(1)}, bf16[1,768,1024]{2,1,0:T(8,128)(2,1)S(1)}, u32[]{:S(2)}, u32[]{:S(2)}) collective-permute-start(bf16[1,768,1024]{2,1,0:T(8,128)(2,1)S(1)} %constant_dynamic-slice_fusion), channel_id=1, source_target_pairs={{2,1},{1,2},{6,5},{5,6},{10,9},{9,10},{14,13},{13,14},{18,17},{17,... | collective-permute-start | bytes 4718600 | tf_op jit(solution)/shard_map/ppermute | solution.py:1021
  641.6 91.5 %all-to-all-start = ((bf16[32,136,128]{2,1,0:T(8,128)(2,1)}), bf16[32,136,128]{2,1,0:T(8,128)(2,1)S(1)}, u32[]{:S(2)}, u32[]{:S(2)}) async-start(bf16[32,136,128]{2,1,0:T(8,128)(2,1)} %bitcast.36), calls=%async_computation | async-start | bytes 2228224 | tf_op jit(solution)/shard_map/all_to_all | solution.py:1208
  (27 other events, 115.1 us)
Sparse Core Ops, SparseCore 0:
  17.5 121.2 all-gather.4
  141.6 180.6 all-gather.6
  561.7 167.0 reduce-scatter.4
